TPU v7x, 256 devices: a whole 4x4x8 slice. The times are simulated.
256 devices in a mesh: batch: 64 (over z, x, y_hi), chan: 4 (over y_lo, core).
Axes of the slice: x: 4, y: 4 (y_hi: 2, y_lo: 2; y = y_hi * 2 + y_lo), z: 8, core: 2. Of those that a mesh axis runs over, the one named last changes fastest.
Arguments:
- signal: float32 [1024, 32768], P('chan', 'batch'), may hold values from -6 to 6
- cotangent: float32 [1024, 32768], P('chan', 'batch'), may hold values from -6 to 6
- first_layer: float32 [33, 64], replicated, may hold values from -5 to 5
- second_layer: float32 [64, 1024], P(None, 'chan'), may hold values from -0.75 to 0.75
- decay_rate: float32 [1024], P('chan'), may hold values from 0.3 to 600
- skip_gain: float32 [1024], P('chan'), may hold values from -4 to 4
Outputs:
- input_grad: float32 [1024, 32768], P('chan', 'batch')
- first_grad: float32 [33, 64], replicated
- second_grad: float32 [64, 1024], P(None, 'chan')
- decay_grad: float32 [1024], P('chan')
- skip_grad: float32 [1024], P('chan')
All inputs are finite; a program needn't handle non-finite values.
Results may differ from a plain program's by a relative error of at most 0.0003.
Values sent between devices are 32-bit elements; how exact they have to be, the bound alone decides.
No kernel may reach another device: no remote copies, remote signals or barrier semaphores. Data moves between devices by JAX's collectives and lax.ppermute only.
A program may use at most 128 MiB of HBM per device.

v0:
```python
import math

import jax
import jax.numpy as jnp
from jax import lax
from jax.sharding import PartitionSpec as P

ROWS = 256


precise = lax.Precision.HIGHEST
epsilon = 1e-06


def rows_first(arrays, axis, dims):
    turned = [jnp.moveaxis(a, dim, 0) for a, dim in zip(arrays, dims)]
    widths = [t[0].size for t in turned]
    both = jnp.concatenate([t.reshape(-1, w) for t, w in zip(turned, widths)], axis=1)
    result = lax.all_gather(both, axis, axis=0, tiled=True)
    parts = jnp.split(result, [sum(widths[:k]) for k in range(1, len(widths))], axis=1)
    return tuple(
        (
            jnp.moveaxis(b.reshape(-1, *t.shape[1:]), 0, dim)
            for b, t, dim in zip(parts, turned, dims)
        )
    )


def total_of_pieces(x, axis):
    return lax.all_gather(x, axis).sum(0)


def features(positions, length, band_count):
    band_index = jnp.arange(1, band_count + 1, dtype=jnp.int32)
    phase = (band_index[:, None] * positions[None, :] % length).astype(jnp.float32) * (
        2.0 * math.pi / length
    )
    linear = positions.astype(jnp.float32)[None, :] / length
    return jnp.concatenate([linear, jnp.cos(phase), jnp.sin(phase)], axis=0)


def make_filter(first_layer, columns, rates, positions, length):
    embed = features(positions, length, first_layer.shape[0] // 2)
    before = jnp.dot(first_layer.T, embed, precision=precise)
    basis = jnp.sin(before)
    fraction = positions.astype(jnp.float32) / length
    window = jnp.exp(-rates[:, None] * fraction[None, :])
    shaped = window * jnp.dot(columns.T, basis, precision=precise)
    return (embed, before, basis, fraction, window, shaped)


def dft_tables(rows):
    counter = jnp.arange(rows, dtype=jnp.int32)
    product = counter[:, None] * counter[None, :]
    angle = (product % rows).astype(jnp.float32) * (2.0 * math.pi / rows)
    twist = product.astype(jnp.float32) * (2.0 * math.pi / (rows * rows))
    return (jnp.cos(angle), jnp.sin(angle), jnp.cos(twist), jnp.sin(twist))


def right_product(values, matrix):
    return jnp.dot(values, matrix, precision=precise)


def forward(signal, tables):
    cos_rows, sin_rows, cos_twist, sin_twist = tables
    rows = cos_rows.shape[0]
    half = rows // 2
    blocks = signal.reshape(signal.shape[0], half, rows)
    first_re = jnp.einsum("cam,ak->ckm", blocks, cos_rows[:half], precision=precise)
    first_im = -jnp.einsum("cam,ak->ckm", blocks, sin_rows[:half], precision=precise)
    twist_re = first_re * cos_twist + first_im * sin_twist
    twist_im = first_im * cos_twist - first_re * sin_twist
    spec_re = right_product(twist_re, cos_rows) + right_product(twist_im, sin_rows)
    spec_im = right_product(twist_im, cos_rows) - right_product(twist_re, sin_rows)
    return (spec_re, spec_im)


def inverse(spec_re, spec_im, tables):
    cos_rows, sin_rows, cos_twist, sin_twist = tables
    rows = cos_rows.shape[0]
    half = rows // 2
    back_re = right_product(spec_re, cos_rows) - right_product(spec_im, sin_rows)
    back_im = right_product(spec_im, cos_rows) + right_product(spec_re, sin_rows)
    turn_re = back_re * cos_twist - back_im * sin_twist
    turn_im = back_im * cos_twist + back_re * sin_twist
    blocks = jnp.einsum("ak,ckm->cam", cos_rows[:half], turn_re, precision=precise) - jnp.einsum(
        "ak,ckm->cam", sin_rows[:half], turn_im, precision=precise
    )
    return blocks.reshape(blocks.shape[0], half * rows) / float(rows * rows)


def correlate(values, cotan, filt, tables):
    count = values.shape[0]
    every_re, every_im = forward(jnp.concatenate([values, cotan, filt], axis=0), tables)
    val_re, cot_re, filt_re = (every_re[:count], every_re[count : 2 * count], every_re[2 * count :])
    val_im, cot_im, filt_im = (every_im[:count], every_im[count : 2 * count], every_im[2 * count :])
    prod_re = jnp.concatenate(
        [filt_re * cot_re + filt_im * cot_im, val_re * cot_re + val_im * cot_im], axis=0
    )
    prod_im = jnp.concatenate(
        [filt_re * cot_im - filt_im * cot_re, val_re * cot_im - val_im * cot_re], axis=0
    )
    both = inverse(prod_re, prod_im, tables)
    return (both[:count], both[count:])


def local(signal, cotangent, first_layer, second_layer, decay_rate, skip_gain):
    groups = lax.axis_size("batch")
    place = lax.axis_index("batch")
    width_dev = signal.shape[0]
    local_len = signal.shape[1]
    length = local_len * groups
    factor = 1.0 / math.sqrt(length)
    tables = dft_tables(ROWS)
    narrow = width_dev // groups
    spread_val, spread_cot = (
        lax.all_to_all(signal, "batch", split_axis=0, concat_axis=1, tiled=True),
        lax.all_to_all(cotangent, "batch", split_axis=0, concat_axis=1, tiled=True),
    )
    positions = jnp.arange(length, dtype=jnp.int32)
    columns = lax.dynamic_slice_in_dim(second_layer, place * narrow, narrow, 1)
    rates = lax.dynamic_slice_in_dim(decay_rate, place * narrow, narrow, 0)
    gains = lax.dynamic_slice_in_dim(skip_gain, place * narrow, narrow, 0)
    embed, before, basis, fraction, window, shaped = make_filter(
        first_layer, columns, rates, positions, length
    )
    norms = jnp.sqrt(jnp.sum(shaped * shaped, axis=1, keepdims=True) + epsilon)
    filt = shaped / norms
    in_grad, filt_grad = correlate(spread_val, spread_cot, filt, tables)
    in_grad = in_grad + gains[:, None] * spread_cot
    dfilt = factor * filt_grad
    skip_part = factor * jnp.sum(spread_cot * spread_val, axis=1)
    project = jnp.sum(filt * dfilt, axis=1, keepdims=True)
    draw = (dfilt - filt * project) / norms
    decay_part = -jnp.sum(draw * shaped * fraction[None, :], axis=1)
    dmix = draw * window
    second_part = jnp.dot(basis, dmix.T, precision=precise)
    dbasis = jnp.dot(columns, dmix, precision=precise)
    input_grad = lax.all_to_all(in_grad, "batch", split_axis=1, concat_axis=0, tiled=True)
    second_grad, decay_grad, skip_grad = rows_first(
        (second_part, decay_part, skip_part), "batch", (1, 0, 0)
    )
    first_part = jnp.dot(embed, (jnp.cos(before) * dbasis).T, precision=precise)
    first_grad = total_of_pieces(first_part, ("batch", "chan"))
    return (input_grad, first_grad, second_grad, decay_grad, skip_grad)


def solution(mesh):
    placed = (P("chan", "batch"), P("chan", "batch"), P(), P(None, "chan"), P("chan"), P("chan"))
    return jax.shard_map(
        local,
        mesh=mesh,
        in_specs=placed,
        out_specs=(P("chan", "batch"), P(), P(None, "chan"), P("chan"), P("chan")),
        check_vma=False,
    )
```

profile of v0, /device:TPU:8, one launch (start us, length us, event | category | flops | bytes accessed | tf_op | source)
XLA Modules:
  0.0 422.9 jit_solution(8014057047468033321)
XLA Ops:
  7.2 0.0 copy-start
  7.2 2.0 all_to_all.40
  9.2 13.8 %all-to-all-start = ((f32[64,4,512]{2,1,0:T(4,128)}), f32[64,4,512]{2,1,0:T(4,128)S(1)}, u32[]{:S(2)}, u32[]{:S(2)}) async-start(f32[64,4,512]{2,1,0:T(4,128)} %all_to_all.40), calls=%async_computation | async-start | bytes 1048576 | tf_op jit(solution)/shard_map/all_to_all | solution.py:117
  23.0 0.1 convert_multiply_fusion.1
  23.2 2.0 all_to_all.43
  25.2 9.6 %fusion.51 = (f32[16,32768]{1,0:T(8,128)S(1)}, f32[16,32768]{1,0:T(8,128)}) fusion(s32[16]{0:T(128)S(1)} %iota_add_fusion), kind=kLoop, calls=%fused_computation.55 | loop fusion | flops 7340032 | bytes 4194368 | tf_op jit(solution)/shard_map/cos | solution.py:39
  34.8 0.1 dynamic-slice_negate_fusion
  34.9 38.5 %fusion.131 = (f32[32768,64]{0,1:T(8,128)S(1)}, f32[32768,64]{0,1:T(8,128)}) fusion(f32[33,64]{1,0:T(8,128)S(1)} %copy-done.8, f32[16,32768]{1,0:T(8,128)} %get-tuple-element.16, f32[16,32768]{1,0:T(8,128)S(1)} %get-tuple-element.15, f32[1,32768]{1,0:T(1,128)S(1)} %convert_multiply_fusion.1), kind=kOutput, calls=%fused_computation.152 | convolution fusion | flops 832634880 | bytes 21111040 | tf_op jit(solution)/shard_map/dot_general | solution.py:44
  73.4 4.2 multiply_reduce_fusion.3
  77.7 13.0 %all-to-all-start.1 = ((f32[64,4,512]{2,1,0:T(4,128)}), f32[64,4,512]{2,1,0:T(4,128)}, u32[]{:S(2)}, u32[]{:S(2)}) async-start(f32[64,4,512]{2,1,0:T(4,128)} %all_to_all.43), calls=%async_computation.1 | async-start | bytes 1048576 | tf_op jit(solution)/shard_map/all_to_all | solution.py:118
  90.7 0.2 all-gather.5.cloned.1.call-start
  90.9 1.0 broadcast_divide_fusion
  91.9 0.1 dynamic_slice.11
  91.9 1.6 fusion.72
  93.5 1.1 copy.61
  94.6 1.6 fusion.71
  96.2 1.1 copy.62
  97.3 1.7 fusion.77
  99.0 1.7 fusion.76
  100.7 2.0 copy.59
  102.7 1.9 concatenate.22
  104.6 4.9 %all-to-all-done.1 = f32[64,4,512]{2,1,0:T(4,128)} async-done(((f32[64,4,512]{2,1,0:T(4,128)}), f32[64,4,512]{2,1,0:T(4,128)}, u32[]{:S(2)}, u32[]{:S(2)}) %all-to-all-start.1) | async-done | bytes 524320 | tf_op jit(solution)/shard_map/all_to_all | solution.py:118
  109.5 2.0 copy.60
  111.5 1.9 concatenate.23
  113.4 1.1 constant_dynamic-update-slice_fusion.1
  114.6 1.1 constant_dynamic-update-slice_fusion
  115.7 1.2 bitcast_dynamic-update-slice_fusion
  116.8 2.6 fusion.87
  119.5 2.6 fusion.86
  122.1 4.0 fusion.2
  126.2 3.8 fusion.4
  130.0 3.8 fusion.27
  133.8 4.2 fusion.24
  138.0 0.6 multiply_add_fusion.2
  138.6 2.9 fusion.30
  141.5 2.8 fusion.31
  144.3 2.9 fusion.35
  147.2 3.0 fusion.34
  150.3 3.6 fusion.13
  153.9 3.6 fusion.42
  157.5 1.1 slice_multiply_fusion
  158.6 1.2 copy.79
  159.8 0.3 copy.112
  160.2 0.5 multiply_reduce_fusion.2
  160.6 0.5 multiply_reduce_fusion.1
  161.1 36.7 %convolution_multiply_fusion = f32[64,32768]{1,0:T(8,128)S(1)} fusion(f32[32768,64]{0,1:T(8,128)} %get-tuple-element.18, f32[4,32768]{1,0:T(4,128)S(1)} %get-tuple-element.6, f32[32768]{0:T(1024)S(1)} %convert_multiply_fusion.2, f32[4]{0:T(128)S(1)} %dynamic-slice_negate_fusion, f32[64,256]{1,0:T(8,128)S(1)} %copy-done, s32[]{:T(128)S(6)} %select_n.43), kind=kOutput, calls=%fused_computation | convolution fusion | flops 103022592 | bytes 17465860 | tf_op jit(solution)/shard_map/dot_general | solution.py:138
  197.8 7.4 %fusion.45 = f32[1,33,64]{2,1,0:T(8,128)} fusion(f32[64,32768]{1,0:T(8,128)S(1)} %convolution_multiply_fusion, f32[16,32768]{1,0:T(8,128)S(1)} %copy-done.2, f32[16,32768]{1,0:T(8,128)S(1)} %get-tuple-element.15, f32[1,32768]{1,0:T(1,128)S(1)} %convert_multiply_fusion.1), kind=kOutput, calls=%fused_computation.45 | convolution fusion | flops 832634880 | bytes 12722432 | tf_op jit(solution)/shard_map/dot_general | solution.py:143
  205.2 0.0 all-gather.5.cloned.1.call-update
  205.2 0.2 copy.77
  205.4 0.3 copy.111
  205.8 2.0 multiply_add_fusion.5
  207.8 1.4 multiply_reduce_fusion
  209.3 0.1 copy.81
  209.4 8.0 %all-to-all-start.2 = ((f32[4,64,512]{2,0,1:T(4,128)}), f32[4,64,512]{2,0,1:T(4,128)S(1)}, u32[]{:S(2)}, u32[]{:S(2)}) async-start(f32[4,64,512]{2,0,1:T(4,128)} %bitcast.18), calls=%async_computation.2 | async-start | bytes 1048576 | tf_op jit(solution)/shard_map/all_to_all | solution.py:139
  217.4 0.1 copy.80
  217.5 9.0 %fusion.53 = f32[4,64]{1,0:T(4,128)S(1)} fusion(f32[32768,64]{0,1:T(8,128)} %copy-done.1, f32[4,32768]{1,0:T(4,128)S(1)} %get-tuple-element.6, f32[32768]{0:T(1024)S(1)} %convert_multiply_fusion.2, f32[4]{0:T(128)S(1)} %dynamic-slice_negate_fusion), kind=kOutput, calls=%fused_computation.69 | convolution fusion | flops 100925440 | bytes 9045008 | tf_op jit(solution)/shard_map/dot_general | solution.py:137
  226.5 0.1 maximum_bitcast_fusion
  226.6 182.5 %all-gather.2 = f32[64,4,66]{2,1,0:T(4,128)S(1)} all-gather(f32[1,4,66]{2,1,0:T(4,128)S(1)} %maximum_bitcast_fusion), channel_id=1, replica_groups=mesh['batch'=64,'chan'=4] {'batch'}, dimensions={0}, use_global_device_ids=true | all-gather | bytes 68640 | tf_op jit(solution)/shard_map/all_gather | solution.py:19
  409.1 0.7 copy.107
  409.8 0.1 fusion.130
  409.9 0.6 copy.109
  410.6 0.6 copy.108
  411.2 1.0 all_to_all.50
  412.2 3.6 reduce_sum.47
  (29 shorter events, 0.1 us)
Async XLA Ops:
  7.2 66.2 %copy-start = (f32[64,256]{1,0:T(8,128)S(1)}, f32[64,256]{1,0:T(8,128)}, u32[]{:S(2)}) copy-start(f32[64,256]{1,0:T(8,128)} %param.9) | copy-start | bytes 196612
  9.2 25.6 %copy-start.9 = (f32[256]{0:T(256)S(1)}, f32[256]{0:T(256)}, u32[]{:S(2)}) copy-start(f32[256]{0:T(256)} %param.10) | copy-start | bytes 3076
  9.2 25.7 %copy-start.8 = (f32[33,64]{1,0:T(8,128)S(1)}, f32[33,64]{1,0:T(8,128)}, u32[]{:S(2)}) copy-start(f32[33,64]{1,0:T(8,128)} %param.8) | copy-start | bytes 25348
  9.2 68.5 %all-to-all-start = ((f32[64,4,512]{2,1,0:T(4,128)}), f32[64,4,512]{2,1,0:T(4,128)S(1)}, u32[]{:S(2)}, u32[]{:S(2)}) async-start(f32[64,4,512]{2,1,0:T(4,128)} %all_to_all.40), calls=%async_computation | async-start | bytes 1048576 | tf_op jit(solution)/shard_map/all_to_all | solution.py:117
  73.4 4.3 %copy-start.1 = (f32[32768,64]{0,1:T(8,128)}, f32[32768,64]{0,1:T(8,128)S(1)}, u32[]{:S(2)}) copy-start(f32[32768,64]{0,1:T(8,128)S(1)} %get-tuple-element.17) | copy-start | bytes 25165828
  73.4 18.5 %copy-start.10 = (f32[256]{0:T(256)S(1)}, f32[256]{0:T(256)}, u32[]{:S(2)}) copy-start(f32[256]{0:T(256)} %param.11) | copy-start | bytes 3076
  77.7 14.3 %copy-start.3 = (f32[64,4,512]{2,1,0:T(4,128)}, f32[64,4,512]{2,1,0:T(4,128)S(1)}, u32[]{:S(2)}) copy-start(f32[64,4,512]{2,1,0:T(4,128)S(1)} %all-to-all-done) | copy-start | bytes 1572868
  77.7 31.8 %all-to-all-start.1 = ((f32[64,4,512]{2,1,0:T(4,128)}), f32[64,4,512]{2,1,0:T(4,128)}, u32[]{:S(2)}, u32[]{:S(2)}) async-start(f32[64,4,512]{2,1,0:T(4,128)} %all_to_all.43), calls=%async_computation.1 | async-start | bytes 1048576 | tf_op jit(solution)/shard_map/all_to_all | solution.py:118
  90.7 321.5 %all-gather.5.cloned.1.call-start = ((), (), s32[]{:S(2)}) async-start(), calls=%async_computation.3 | async-start | bytes 5263360 | tf_op jit(solution)/shard_map/all_gather | solution.py:30
  113.4 3.4 copy-start.7
  115.6 3.8 copy-start.6
  161.1 36.7 %copy-start.2 = (f32[16,32768]{1,0:T(8,128)S(1)}, f32[16,32768]{1,0:T(8,128)}, u32[]{:S(2)}) copy-start(f32[16,32768]{1,0:T(8,128)} %get-tuple-element.16) | copy-start | bytes 6291460
  197.8 7.4 %copy-start.5 = (f32[4,128,256]{1,2,0:T(8,128)S(1)}, f32[4,128,256]{1,2,0:T(8,128)}, u32[]{:S(2)}) copy-start(f32[4,128,256]{1,2,0:T(8,128)} %get-tuple-element.12) | copy-start | bytes 1572868
  205.2 2.6 copy-start.4
  209.4 201.8 %all-to-all-start.2 = ((f32[4,64,512]{2,0,1:T(4,128)}), f32[4,64,512]{2,0,1:T(4,128)S(1)}, u32[]{:S(2)}, u32[]{:S(2)}) async-start(f32[4,64,512]{2,0,1:T(4,128)} %bitcast.18), calls=%async_computation.2 | async-start | bytes 1048576 | tf_op jit(solution)/shard_map/all_to_all | solution.py:139
Sparse Core Ops, SparseCore 0:
  205.3 113.1 all-gather.4
where the time goes:
time: 431 us; the launch traced here: 423 us
  blocking collectives  183 us (42%)
  matrix products  136 us (32%)
  starting transfers between devices  35 us (8%)
  other arithmetic  27.1 us (6%)
  local copies, waits for them, and re-layouts  22.9 us (5%)
  between operations  14.6 us (3%)
  waiting for transfers between devices  4.92 us (1%)
    all_gather x1, blocking collectives, rows_first(): result = lax.all_gather(both, axis, axis=0, tiled=True)  183 us
    dot_general x1, matrix products, make_filter(): before = jnp.dot(first_layer.T, embed, precision=precise)  38.5 us
    dot_general x1, matrix products, local(): dbasis = jnp.dot(columns, dmix, precision=precise)  36.7 us
    dot_general x8, matrix products, right_product(): return jnp.dot(values, matrix, precision=precise)  27.5 us
    all_to_all x1, starting transfers between devices, local(): lax.all_to_all(signal, 'batch', split_axis=0, concat_axis=1, tiled=True)  13.8 us
    all_to_all x1, starting transfers between devices, local(): lax.all_to_all(cotangent, 'batch', split_axis=0, concat_axis=1, tiled=True)  13 us
    cos x1, other arithmetic, features(): return jnp.concatenate([linear, jnp.cos(phase), jnp.sin(phase)], axis=0)  9.62 us
    dot_general x1, matrix products, local(): second_part = jnp.dot(basis, dmix.T, precision=precise)  9.01 us
  transfers between devices with their start and end apart: 4, of which 1 were waited for; matrix products, arithmetic and copies ran while one was open for 19% of the time, Pallas kernels for 0%

commit v1 on v0

v1 whole, which is shorter than its diff:
```python
import math

import jax
import jax.numpy as jnp
import numpy as np
from jax import lax
from jax.experimental import pallas as pl
from jax.experimental.pallas import tpu as pltpu
from jax.sharding import PartitionSpec as P

ROWS = 256
COLS = 128
LENGTH = ROWS * COLS
NARROW = 4
TINY = 1e-06
f32 = jnp.float32
bf16 = jnp.bfloat16
highest = lax.Precision.HIGHEST


def halves(x):
    high = x.astype(bf16)
    low = (x - high.astype(np.float64)).astype(bf16)
    return high, low


def make_tables(embed):
    a = np.arange(ROWS)
    k = np.arange(ROWS)
    m = np.arange(COLS)
    bands = embed // 2
    turn = np.pi * ((a[None, :] * (4 * k + 1)[:, None]) % (4 * ROWS)) / (2 * ROWS)
    first = np.concatenate([np.cos(turn), -np.sin(turn)], axis=0)
    twist = np.pi * (4 * k + 1)[:, None] * m[None, :] / (2 * LENGTH)
    angle = 2.0 * np.pi * ((m[:, None] * m[None, :]) % COLS) / COLS
    c, s = np.cos(angle), np.sin(angle)
    second = np.concatenate(
        [np.concatenate([c, -s], axis=1), np.concatenate([s, c], axis=1)], axis=0
    )
    high, low = halves(first)
    forward_left = np.concatenate([high, low, high], axis=1)
    inverse_left = np.concatenate([high.T, low.T, high.T], axis=1)
    high, low = halves(second)
    forward_right = np.concatenate([high, high, low], axis=0)
    inverse_right = np.concatenate([high.T, high.T, low.T], axis=0)
    rows = np.zeros((ROWS, COLS))
    lanes = np.zeros((COLS, COLS))
    half = COLS // 2
    rows[:, 0] = a * COLS / LENGTH
    lanes[0] = 1.0
    rows[:, half] = 1.0
    lanes[half] = m / LENGTH
    for b in range(1, bands + 1):
        big = 2.0 * np.pi * ((b * COLS * a) % LENGTH) / LENGTH
        small = 2.0 * np.pi * b * m / LENGTH
        rows[:, b] = np.cos(big)
        rows[:, half + b] = -np.sin(big)
        rows[:, bands + b] = np.sin(big)
        rows[:, half + bands + b] = np.cos(big)
        lanes[b] = np.cos(small)
        lanes[half + b] = np.sin(small)
        lanes[bands + b] = np.cos(small)
        lanes[half + bands + b] = np.sin(small)
    high, low = halves(lanes.T)
    gather = np.concatenate([high, high, low], axis=0)
    return dict(
        forward_left=forward_left,
        inverse_left=inverse_left,
        forward_right=forward_right,
        inverse_right=inverse_right,
        twist_cos=np.cos(twist).astype(np.float32),
        twist_sin=np.sin(twist).astype(np.float32),
        rows=rows.astype(np.float32),
        lanes=lanes.astype(np.float32),
        gather=gather,
    )


def split(x):
    high = x.astype(bf16)
    low = (x - high.astype(f32)).astype(bf16)
    return high, low


def mm(left, right):
    return lax.dot_general(left, right, (((1,), (0,)), ((), ())), preferred_element_type=f32)


def dot_rows(table, x):
    high, low = split(x)
    return mm(table, jnp.concatenate([high, high, low], axis=0))


def dot_cols(x, table):
    high, low = split(x)
    return mm(jnp.concatenate([high, low, high], axis=1), table)


def forward_pair(x, y, left, right, twist_cos, twist_sin):
    u = dot_rows(left, jnp.concatenate([x, y], axis=1))
    spectra = []
    for n in range(2):
        re = u[:ROWS, n * COLS : (n + 1) * COLS]
        im = u[ROWS:, n * COLS : (n + 1) * COLS]
        v = jnp.concatenate(
            [re * twist_cos + im * twist_sin, im * twist_cos - re * twist_sin], axis=1
        )
        spectra.append(dot_cols(v, right))
    return spectra


def times_conj(f, c):
    fr, fi, cr, ci = f[:, :COLS], f[:, COLS:], c[:, :COLS], c[:, COLS:]
    return jnp.concatenate([fr * cr + fi * ci, fr * ci - fi * cr], axis=1)


def inverse_pair(g, h, left, right, twist_cos, twist_sin):
    parts = []
    for x in (g, h):
        w = dot_cols(x, right)
        re, im = w[:, :COLS], w[:, COLS:]
        parts.append(
            jnp.concatenate(
                [re * twist_cos - im * twist_sin, im * twist_cos + re * twist_sin], axis=0
            )
        )
    y = dot_rows(left, jnp.concatenate(parts, axis=1))
    return y[:, :COLS], y[:, COLS:]


def sin_and_cos(x):
    q = jnp.round(x * (2.0 / math.pi))
    r = x - q * 1.5703125
    r = r - q * 4.837512969970703e-4
    r = r - q * 7.549789954891882e-8
    z = r * r
    s = ((-1.9515295891e-4 * z + 8.3321608736e-3) * z - 1.6666654611e-1) * z * r + r
    c = ((2.443315711809948e-5 * z - 1.388731625493765e-3) * z + 4.166664568298827e-2) * (z * z)
    c = c - 0.5 * z + 1.0
    turns = q.astype(jnp.int32)
    odd = (turns & 1) == 1
    sin_x = jnp.where(odd, c, s)
    cos_x = jnp.where(odd, s, c)
    sin_x = jnp.where((turns & 2) == 2, -sin_x, sin_x)
    cos_x = jnp.where(((turns + 1) & 2) == 2, -cos_x, cos_x)
    return sin_x, cos_x


def fraction_rows(count, offset):
    a = lax.broadcasted_iota(jnp.int32, (count, COLS), 0) + offset
    m = lax.broadcasted_iota(jnp.int32, (count, COLS), 1)
    return (a * COLS + m).astype(f32) * (1.0 / LENGTH)


def filter_kernel(
    weights, columns, rates, rows, lanes, left, right, tcos, tsin,
    basis, slope, filt, window, norms, spectra,
):
    order = basis.shape[0]

    def fill(k, carry):
        scaled = rows[...] * weights[pl.ds(k, 1), :]
        basis[k] = jnp.dot(scaled, lanes[...], precision=highest, preferred_element_type=f32)
        return carry

    lax.fori_loop(0, order, fill, 0)
    chunk = 64

    def bend(k, carry):
        for n in range(ROWS // chunk):
            here = pl.ds(n * chunk, chunk)
            s, c = sin_and_cos(basis[k, here, :])
            basis[k, here, :] = s
            slope[k, here, :] = c
        return carry

    lax.fori_loop(0, order, bend, 0)
    part = 32

    def mix(n, totals):
        start = pl.multiple_of(n * part, part)
        here = pl.ds(start, part)

        def add(k, acc):
            b = basis[k, here, :]
            return tuple(acc[c] + columns[k, c] * b for c in range(NARROW))

        acc = lax.fori_loop(
            0, order, add, tuple(jnp.zeros((part, COLS), f32) for _ in range(NARROW)), unroll=2
        )
        fraction = fraction_rows(part, start)
        out = []
        for c in range(NARROW):
            win = jnp.exp(-rates[c] * fraction)
            raw = win * acc[c]
            window[c, here, :] = win
            filt[c, here, :] = raw
            out.append(totals[c] + (raw * raw).reshape(part // 8, 8, COLS).sum(0))
        return tuple(out)

    totals = lax.fori_loop(
        0, ROWS // part, mix, tuple(jnp.zeros((8, COLS), f32) for _ in range(NARROW))
    )
    for c in range(NARROW):
        norm = jnp.sqrt(jnp.sum(totals[c], keepdims=True) + TINY)
        norms[pl.ds(c, 1), :] = jnp.broadcast_to(norm, (1, COLS))
        filt[c] = filt[c] / norm
    for c in range(0, NARROW, 2):
        x, y = forward_pair(filt[c], filt[c + 1], left[...], right[...], tcos[...], tsin[...])
        spectra[c] = x
        spectra[c + 1] = y


def main_kernel(
    both, columns, gains, basis, slope, filt, window, norms, spectra, rows, gather,
    fleft, fright, ileft, iright, tcos, tsin,
    grad, small, first,
    dmix, second_rows, first_rows, staged,
):
    order = basis.shape[0]
    factor = 1.0 / math.sqrt(LENGTH)
    lane = lax.broadcasted_iota(jnp.int32, (1, COLS), 1)
    scalars = jnp.zeros((1, COLS), f32)
    fraction = fraction_rows(ROWS, 0)
    for c in range(NARROW):
        x = both[pl.ds(c, ROWS, stride=2 * NARROW), :]
        y = both[pl.ds(NARROW + c, ROWS, stride=2 * NARROW), :]
        skip = factor * jnp.sum(x * y, keepdims=True)
        val, cot = forward_pair(x, y, fleft[...], fright[...], tcos[...], tsin[...])
        back, into = inverse_pair(
            times_conj(val, cot), times_conj(spectra[c], cot),
            ileft[...], iright[...], tcos[...], tsin[...],
        )
        y = both[pl.ds(NARROW + c, ROWS, stride=2 * NARROW), :]
        staged[pl.ds(c, ROWS, stride=NARROW), :] = into * (1.0 / LENGTH) + gains[c] * y
        dfilt = back * (factor / LENGTH)
        project = jnp.sum(filt[c] * dfilt, keepdims=True)
        norm = norms[pl.ds(c, 1), :][:, :1]
        draw = (dfilt - filt[c] * project) / norm
        decay = -jnp.sum(draw * filt[c] * fraction, keepdims=True) * norm
        dmix[c] = draw * window[c]
        scalars = jnp.where(lane == c, decay, scalars)
        scalars = jnp.where(lane == NARROW + c, skip, scalars)
    grad[...] = staged[...].reshape(grad.shape)
    chunk = 64

    def tail(k, carry):
        acc = [jnp.zeros((8, COLS), f32) for _ in range(NARROW)]
        pieces = []
        for n in range(ROWS // chunk):
            here = pl.ds(n * chunk, chunk)
            b = basis[k, here, :]
            mixed = jnp.zeros((chunk, COLS), f32)
            for c in range(NARROW):
                d = dmix[c, here, :]
                acc[c] = acc[c] + (b * d).reshape(chunk // 8, 8, COLS).sum(0)
                mixed = mixed + columns[k, c] * d
            pieces.append(mixed * slope[k, here, :])
        r = dot_cols(jnp.concatenate(pieces, axis=0), gather[...])
        first_rows[pl.ds(k, 1), :] = jnp.sum(r * rows[...], axis=0, keepdims=True)
        for c in range(NARROW):
            second_rows[pl.ds(c * order + k, 1), :] = jnp.sum(acc[c], axis=0, keepdims=True)
        return carry

    lax.fori_loop(0, order, tail, 0, unroll=2)
    ones = jnp.ones((8, COLS), f32)
    for n in range(NARROW * order // COLS):
        block = second_rows[pl.ds(n * COLS, COLS), :]
        sums = lax.dot_general(
            ones, block, (((1,), (1,)), ((), ())), precision=highest, preferred_element_type=f32
        )
        small[pl.ds(n, 1), :] = sums[:1, :]
    small[pl.ds(2, 1), :] = scalars
    turned = jnp.transpose(first_rows[...], (1, 0))
    half = COLS // 2
    folded = turned[:half] + turned[half:]
    first[...] = jnp.concatenate([folded[:20], folded[20:40]], axis=1)


def pack(signal, cotangent, groups):
    def turn(x):
        return x.reshape(groups, NARROW, -1, COLS).transpose(0, 2, 1, 3)

    both = jnp.concatenate([turn(signal), turn(cotangent)], axis=2)
    return both.reshape(groups, -1, COLS)


def local(signal, cotangent, first_layer, second_layer, decay_rate, skip_gain):
    groups = lax.axis_size("batch")
    place = lax.axis_index("batch")
    side = lax.axis_index("chan")
    sides = lax.axis_size("chan")
    embed, order = first_layer.shape
    t = make_tables(embed)
    vmem = pl.BlockSpec(memory_space=pltpu.VMEM)
    smem = pl.BlockSpec(memory_space=pltpu.SMEM)

    sent = pack(signal, cotangent, groups)
    spread = lax.all_to_all(sent, "batch", split_axis=0, concat_axis=0, tiled=True)

    columns = lax.dynamic_slice_in_dim(second_layer, place * NARROW, NARROW, 1)
    rates = lax.dynamic_slice_in_dim(decay_rate, place * NARROW, NARROW, 0)
    gains = lax.dynamic_slice_in_dim(skip_gain, place * NARROW, NARROW, 0)
    weights = jnp.pad(first_layer.T, ((0, 0), (0, COLS // 2 - embed)))
    weights = jnp.concatenate([weights, weights], axis=1)

    cube = jax.ShapeDtypeStruct((order, ROWS, COLS), f32)
    four = jax.ShapeDtypeStruct((NARROW, ROWS, COLS), f32)
    basis, slope, filt, window, norms, spectra = pl.pallas_call(
        filter_kernel,
        out_shape=(
            cube, cube, four, four,
            jax.ShapeDtypeStruct((NARROW, COLS), f32),
            jax.ShapeDtypeStruct((NARROW, ROWS, 2 * COLS), f32),
        ),
        in_specs=[vmem, smem, smem] + [vmem] * 6,
        out_specs=(vmem,) * 6,
        cost_estimate=pl.CostEstimate(flops=20_000_000_000, bytes_accessed=20_000_000, transcendentals=0),
        name="make_filter",
    )(
        weights, columns, rates, t["rows"], t["lanes"],
        t["forward_left"], t["forward_right"], t["twist_cos"], t["twist_sin"],
    )

    grad, small, first = pl.pallas_call(
        main_kernel,
        out_shape=(
            jax.ShapeDtypeStruct((groups, 4 * NARROW, COLS), f32),
            jax.ShapeDtypeStruct((3, COLS), f32),
            jax.ShapeDtypeStruct((20, COLS), f32),
        ),
        in_specs=[vmem, smem, smem] + [vmem] * 14,
        out_specs=(vmem,) * 3,
        scratch_shapes=[
            pltpu.VMEM((NARROW, ROWS, COLS), f32),
            pltpu.VMEM((NARROW * order, COLS), f32),
            pltpu.VMEM((order, COLS), f32),
            pltpu.VMEM((NARROW * ROWS, COLS), f32),
        ],
        name="correlate",
    )(
        spread.reshape(-1, COLS), columns, gains, basis, slope, filt, window, norms, spectra,
        t["rows"], t["gather"], t["forward_left"], t["forward_right"],
        t["inverse_left"], t["inverse_right"], t["twist_cos"], t["twist_sin"],
    )

    quarter = first.shape[0] // sides
    own = lax.dynamic_slice_in_dim(first, side * quarter, quarter, 0)
    for step in range(1, sides):
        ring = [(i, (i + step) % sides) for i in range(sides)]
        piece = lax.dynamic_slice_in_dim(first, (side + step) % sides * quarter, quarter, 0)
        own = own + lax.ppermute(piece, "chan", ring)
    shared = jnp.concatenate([small, own], axis=0)
    back = jnp.concatenate([grad, jnp.broadcast_to(shared, (groups,) + shared.shape)], axis=1)
    home = lax.all_to_all(back, "batch", split_axis=0, concat_axis=0, tiled=True)

    rows = 4 * NARROW
    input_grad = (
        home[:, :rows].reshape(groups, 4, NARROW, COLS).transpose(0, 2, 1, 3)
        .reshape(groups * NARROW, 4 * COLS)
    )
    second_grad = home[:, rows : rows + 2].reshape(groups * NARROW, order).T
    decay_grad = home[:, rows + 2, :NARROW].reshape(groups * NARROW)
    skip_grad = home[:, rows + 2, NARROW : 2 * NARROW].reshape(groups * NARROW)
    mine = home[:, rows + 3 :].sum(0)
    gathered = [mine]
    for step in range(1, sides):
        ring = [((i + step) % sides, i) for i in range(sides)]
        gathered.append(lax.ppermute(mine, "chan", ring))
    twice = jnp.concatenate(gathered + gathered, axis=0)
    ordered = lax.dynamic_slice_in_dim(
        twice, (sides - side) % sides * quarter, sides * quarter, 0
    )
    first_grad = jnp.concatenate([ordered[:, :order], ordered[:, order:]], axis=0)[:embed]
    return (input_grad, first_grad, second_grad, decay_grad, skip_grad)


def solution(mesh):
    placed = (P("chan", "batch"), P("chan", "batch"), P(), P(None, "chan"), P("chan"), P("chan"))
    return jax.shard_map(
        local,
        mesh=mesh,
        in_specs=placed,
        out_specs=(P("chan", "batch"), P(), P(None, "chan"), P("chan"), P("chan")),
        check_vma=False,
    )
```

time: 431 us -> 141 us (0.33)
  the two profiles are of different devices: /device:TPU:8 before, /device:TPU:1 now
where the time goes in v1:
time: 141 us; the launch traced here: 140 us
  Pallas kernels  64.3 us (46%)
  starting transfers between devices  36.8 us (26%)
  waiting for transfers between devices  21.9 us (16%)
  local copies, waits for them, and re-layouts  11.3 us (8%)
  other arithmetic  5.04 us (4%)
    pallas_call x1, Pallas kernels, local(): pl.pallas_call(filter_kernel, out_shape=(cube, cube, four, four, jax.Shap...  40.6 us
    pallas_call x1, Pallas kernels, local(): pl.pallas_call(main_kernel, out_shape=(jax.ShapeDtypeStruct((groups, 4 *...  23.7 us
    all_to_all x1, waiting for transfers between devices, local(): lax.all_to_all(back, 'batch', split_axis=0, concat_axis=0, tiled=True)  21.2 us
    all_to_all x1, starting transfers between devices, local(): lax.all_to_all(sent, 'batch', split_axis=0, concat_axis=0, tiled=True)  15.1 us
    all_to_all x1, starting transfers between devices, local(): lax.all_to_all(back, 'batch', split_axis=0, concat_axis=0, tiled=True)  12.5 us
    ppermute x3, starting transfers between devices, local(): gathered.append(lax.ppermute(mine, 'chan', ring))  6.51 us
  transfers between devices with their start and end apart: 8, of which 3 were waited for; matrix products, arithmetic and copies ran while one was open for 4% of the time, Pallas kernels for 29%

profile of v1, /device:TPU:1, one launch (start us, length us, event | category | flops | bytes accessed | tf_op | source)
XLA Modules:
  0.0 140.2 jit_solution(16170669487367378507)
XLA Ops:
  0.6 0.0 copy-start
  0.6 0.0 copy-start.2
  0.7 0.0 copy-start.3
  0.7 0.0 copy-start.4
  0.7 1.3 reshape.32
  1.9 1.2 reshape.31
  3.2 0.3 pad_maximum_fusion
  3.4 1.1 copy.31
  4.5 15.1 %all-to-all-start = ((f32[64,32,128]{2,1,0:T(8,128)}), f32[64,32,128]{2,1,0:T(8,128)S(1)}, u32[]{:S(2)}, u32[]{:S(2)}) async-start(f32[64,32,128]{2,1,0:T(8,128)} %bitcast.14), calls=%async_computation | async-start | bytes 2097152 | tf_op jit(solution)/shard_map/all_to_all | solution.py:299
  19.7 0.0 copy-done.2
  19.7 0.1 copy.25
  19.8 0.0 copy-done.3
  19.8 0.6 dynamic_slice.25.gains
  20.4 0.0 copy-done.4
  20.4 0.6 dynamic_slice.26.rates
  21.0 0.0 copy-done
  21.0 0.7 constant_dynamic-slice_fusion.4.columns
  21.7 0.7 pad_maximum_fusion.2.weights
  22.4 40.6 %make_filter.1 = (f32[64,256,128]{2,1,0:T(8,128)}, f32[64,256,128]{2,1,0:T(8,128)}, f32[4,256,128]{2,1,0:T(8,128)}, f32[4,256,128]{2,1,0:T(8,128)}, f32[4,128]{1,0:T(4,128)}, /*index=5*/f32[4,256,256]{2,1,0:T(8,128)}) custom-call(f32[64,128]{1,0:T(8,128)} %pad_maximum_fusion.2.weights, f32[64,4]{1,0:T(8,128)} %constant_dynamic-slice_fusion.4.columns, ...), custom_call_target="tpu_custom_call" | custom-call | flops 20000000000 | bytes 20000000 | tf_op jit(solution)/shard_map/make_filter/pallas_call | solution.py:309
  63.0 0.0 all-to-all-done
  63.0 0.0 copy-start.1
  63.0 1.0 copy-done.1
  64.0 23.7 %correlate.1 = (f32[64,16,128]{2,1,0:T(8,128)}, f32[3,128]{1,0:T(4,128)}, f32[20,128]{1,0:T(8,128)}) custom-call(f32[2048,128]{1,0:T(8,128)} %bitcast.16, f32[64,4]{1,0:T(8,128)} %constant_dynamic-slice_fusion.4.columns, f32[4]{0:T(128)} %dynamic_slice.25.gains, f32[64,256,128]{2,1,0:T(8,128)} %get-tuple-element.14.basis, ...), custom_call_target="tpu_custom_call" | custom-call | tf_op jit(solution)/shard_map/correlate/pallas_call | solution.py:325
  87.7 0.8 constant_dynamic-slice_fusion.3
  88.5 1.0 collective-permute-start.2
  89.4 0.3 collective-permute-start.1
  89.8 1.4 collective-permute-start
  91.1 0.4 collective-permute-done.2
  91.5 0.4 collective-permute-done.1
  91.9 0.0 collective-permute-done
  91.9 0.7 add_add_fusion
  92.6 0.7 pad_maximum_fusion.4
  93.3 2.0 %pad_maximum_fusion.1 = f32[64,24,128]{2,1,0:T(8,128)} fusion(f32[64,8,128]{2,1,0:T(8,128)S(1)} %broadcast_in_dim.3, f32[64,16,128]{2,1,0:T(8,128)} %get-tuple-element.20), kind=kLoop, calls=%fused_computation.2 | loop fusion | flops 196608 | bytes 1572864 | tf_op jit(solution)/shard_map/concatenate | solution.py:354
  95.3 12.5 %all-to-all-start.1 = ((f32[64,24,128]{2,1,0:T(8,128)}), f32[64,24,128]{2,1,0:T(8,128)S(1)}, u32[]{:S(2)}, u32[]{:S(2)}) async-start(f32[64,24,128]{2,1,0:T(8,128)} %pad_maximum_fusion.1), calls=%async_computation.1 | async-start | bytes 1572864 | tf_op jit(solution)/shard_map/all_to_all | solution.py:355
  107.8 21.2 %all-to-all-done.1 = f32[64,24,128]{2,1,0:T(8,128)S(1)} async-done(((f32[64,24,128]{2,1,0:T(8,128)}), f32[64,24,128]{2,1,0:T(8,128)S(1)}, u32[]{:S(2)}, u32[]{:S(2)}) %all-to-all-start.1) | async-done | bytes 786464 | tf_op jit(solution)/shard_map/all_to_all | solution.py:355
  129.0 0.1 slice_reduce_fusion
  129.1 4.8 %collective-permute-start.3 = (f32[5,128]{1,0:T(8,128)S(1)}, f32[5,128]{1,0:T(8,128)S(1)}, u32[]{:S(2)}, u32[]{:S(2)}) collective-permute-start(f32[5,128]{1,0:T(8,128)S(1)} %slice_reduce_fusion), channel_id=1, source_target_pairs={{1,0},{2,1},{3,2},{0,3},{5,4},{6,5},{7,6},{4,7},{9,8},{10,9},{11,1... | collective-permute-start | bytes 7688 | tf_op jit(solution)/shard_map/ppermute | solution.py:369
  133.8 0.3 collective-permute-start.4
  134.1 1.4 %collective-permute-start.5 = (f32[5,128]{1,0:T(8,128)S(1)}, f32[5,128]{1,0:T(8,128)S(1)}, u32[]{:S(2)}, u32[]{:S(2)}) collective-permute-start(f32[5,128]{1,0:T(8,128)S(1)} %slice_reduce_fusion), channel_id=1, source_target_pairs={{3,0},{0,1},{1,2},{2,3},{7,4},{4,5},{5,6},{6,7},{11,8},{8,9},{9,10... | collective-permute-start | bytes 7688 | tf_op jit(solution)/shard_map/ppermute | solution.py:369
  135.6 0.2 slice_reduce_fusion.1
  135.9 0.1 copy.26
  136.0 0.8 copy.32
  136.9 0.1 reshape.37
  137.0 0.7 copy.27
  137.7 0.7 reshape_squeeze.6
  138.4 0.7 reshape_squeeze.7
  139.1 0.0 collective-permute-done.3
  139.1 0.0 collective-permute-done.4
  139.1 0.0 collective-permute-done.5
  139.1 0.4 concatenate.22
  139.5 0.1 constant_dynamic-slice_fusion
  139.5 0.6 pad_maximum_fusion.3
  (4 shorter events, 0.1 us)
Async XLA Ops:
  0.6 20.3 %copy-start = (f32[64,256]{1,0:T(8,128)S(1)}, f32[64,256]{1,0:T(8,128)}, u32[]{:S(2)}) copy-start(f32[64,256]{1,0:T(8,128)} %param.18) | copy-start | bytes 196612
  0.6 19.0 %copy-start.2 = (f32[33,64]{1,0:T(8,128)S(1)}, f32[33,64]{1,0:T(8,128)}, u32[]{:S(2)}) copy-start(f32[33,64]{1,0:T(8,128)} %param.17) | copy-start | bytes 25348
  0.7 19.1 %copy-start.3 = (f32[256]{0:T(256)S(1)}, f32[256]{0:T(256)}, u32[]{:S(2)}) copy-start(f32[256]{0:T(256)} %param.20) | copy-start | bytes 3076
  0.7 19.7 %copy-start.4 = (f32[256]{0:T(256)S(1)}, f32[256]{0:T(256)}, u32[]{:S(2)}) copy-start(f32[256]{0:T(256)} %param.19) | copy-start | bytes 3076
  4.5 58.5 %all-to-all-start = ((f32[64,32,128]{2,1,0:T(8,128)}), f32[64,32,128]{2,1,0:T(8,128)S(1)}, u32[]{:S(2)}, u32[]{:S(2)}) async-start(f32[64,32,128]{2,1,0:T(8,128)} %bitcast.14), calls=%async_computation | async-start | bytes 2097152 | tf_op jit(solution)/shard_map/all_to_all | solution.py:299
  63.0 1.0 copy-start.1
  88.5 3.0 %collective-permute-start.2 = (f32[5,128]{1,0:T(8,128)S(1)}, f32[5,128]{1,0:T(8,128)S(1)}, u32[]{:S(2)}, u32[]{:S(2)}) collective-permute-start(f32[5,128]{1,0:T(8,128)S(1)} %get-tuple-element.33), channel_id=1, source_target_pairs={{0,3},{1,0},{2,1},{3,2},{4,7},{5,4},{6,5},{7,6},{8,11},{9,8},{10,9... | collective-permute-start | bytes 7688 | tf_op jit(solution)/shard_map/ppermute | solution.py:352
  89.4 2.5 %collective-permute-start.1 = (f32[5,128]{1,0:T(8,128)S(1)}, f32[5,128]{1,0:T(8,128)S(1)}, u32[]{:S(2)}, u32[]{:S(2)}) collective-permute-start(f32[5,128]{1,0:T(8,128)S(1)} %get-tuple-element.34), channel_id=1, source_target_pairs={{0,2},{1,3},{2,0},{3,1},{4,6},{5,7},{6,4},{7,5},{8,10},{9,11},{10,... | collective-permute-start | bytes 7688 | tf_op jit(solution)/shard_map/ppermute | solution.py:352
  89.8 2.1 %collective-permute-start = (f32[5,128]{1,0:T(8,128)S(1)}, f32[5,128]{1,0:T(8,128)S(1)}, u32[]{:S(2)}, u32[]{:S(2)}) collective-permute-start(f32[5,128]{1,0:T(8,128)S(1)} %get-tuple-element.32), channel_id=1, source_target_pairs={{0,1},{1,2},{2,3},{3,0},{4,5},{5,6},{6,7},{7,4},{8,9},{9,10},{10,1... | collective-permute-start | bytes 7688 | tf_op jit(solution)/shard_map/ppermute | solution.py:352
  95.3 33.7 %all-to-all-start.1 = ((f32[64,24,128]{2,1,0:T(8,128)}), f32[64,24,128]{2,1,0:T(8,128)S(1)}, u32[]{:S(2)}, u32[]{:S(2)}) async-start(f32[64,24,128]{2,1,0:T(8,128)} %pad_maximum_fusion.1), calls=%async_computation.1 | async-start | bytes 1572864 | tf_op jit(solution)/shard_map/all_to_all | solution.py:355
  129.1 10.0 %collective-permute-start.3 = (f32[5,128]{1,0:T(8,128)S(1)}, f32[5,128]{1,0:T(8,128)S(1)}, u32[]{:S(2)}, u32[]{:S(2)}) collective-permute-start(f32[5,128]{1,0:T(8,128)S(1)} %slice_reduce_fusion), channel_id=1, source_target_pairs={{1,0},{2,1},{3,2},{0,3},{5,4},{6,5},{7,6},{4,7},{9,8},{10,9},{11,1... | collective-permute-start | bytes 7688 | tf_op jit(solution)/shard_map/ppermute | solution.py:369
  133.8 5.2 %collective-permute-start.4 = (f32[5,128]{1,0:T(8,128)S(1)}, f32[5,128]{1,0:T(8,128)S(1)}, u32[]{:S(2)}, u32[]{:S(2)}) collective-permute-start(f32[5,128]{1,0:T(8,128)S(1)} %slice_reduce_fusion), channel_id=1, source_target_pairs={{2,0},{3,1},{0,2},{1,3},{6,4},{7,5},{4,6},{5,7},{10,8},{11,9},{8,1... | collective-permute-start | bytes 7688 | tf_op jit(solution)/shard_map/ppermute | solution.py:369
  134.1 4.9 %collective-permute-start.5 = (f32[5,128]{1,0:T(8,128)S(1)}, f32[5,128]{1,0:T(8,128)S(1)}, u32[]{:S(2)}, u32[]{:S(2)}) collective-permute-start(f32[5,128]{1,0:T(8,128)S(1)} %slice_reduce_fusion), channel_id=1, source_target_pairs={{3,0},{0,1},{1,2},{2,3},{7,4},{4,5},{5,6},{6,7},{11,8},{8,9},{9,10... | collective-permute-start | bytes 7688 | tf_op jit(solution)/shard_map/ppermute | solution.py:369

commit v2 on v1

v2 whole, which is shorter than its diff:
```python
import math

import jax
import jax.numpy as jnp
import numpy as np
from jax import lax
from jax.experimental import pallas as pl
from jax.experimental.pallas import tpu as pltpu
from jax.sharding import PartitionSpec as P

ROWS = 256
COLS = 128
LENGTH = ROWS * COLS
NARROW = 4
FILTER_MIB = 24
MAIN_MIB = 28
TINY = 1e-06
f32 = jnp.float32
bf16 = jnp.bfloat16
highest = lax.Precision.HIGHEST


def halves(x):
    high = x.astype(bf16)
    low = (x - high.astype(np.float64)).astype(bf16)
    return high, low


SIN = (6.28318528, -10.33542017, 5.100155046, -1.196582571, 0.1553153206)
COS = (0.9999999532, -4.934792831, 4.058411353, -1.331876568, 0.2196896111)


def make_tables(embed):
    a = np.arange(ROWS)
    k = np.arange(ROWS)
    m = np.arange(COLS)
    bands = embed // 2
    turn = np.pi * ((a[None, :] * (4 * k + 1)[:, None]) % (4 * ROWS)) / (2 * ROWS)
    first = np.concatenate([np.cos(turn), -np.sin(turn)], axis=0)
    twist = np.pi * (4 * k + 1)[:, None] * m[None, :] / (2 * LENGTH)
    angle = 2.0 * np.pi * ((m[:, None] * m[None, :]) % COLS) / COLS
    c, s = np.cos(angle), np.sin(angle)
    second = np.concatenate(
        [np.concatenate([c, -s], axis=1), np.concatenate([s, c], axis=1)], axis=0
    )
    high, low = halves(first)
    forward_left = np.concatenate([high, low], axis=1)
    inverse_left = np.concatenate([high.T, low.T], axis=1)
    high, low = halves(second)
    forward_right = np.concatenate([high, low], axis=0)
    inverse_right = np.concatenate([high.T, low.T], axis=0)
    rows = np.zeros((ROWS, COLS))
    lanes = np.zeros((COLS, COLS))
    half = COLS // 2
    rows[:, 0] = a * COLS / LENGTH
    lanes[0] = 1.0
    rows[:, half] = 1.0
    lanes[half] = m / LENGTH
    for b in range(1, bands + 1):
        big = 2.0 * np.pi * ((b * COLS * a) % LENGTH) / LENGTH
        small = 2.0 * np.pi * b * m / LENGTH
        rows[:, b] = np.cos(big)
        rows[:, half + b] = -np.sin(big)
        rows[:, bands + b] = np.sin(big)
        rows[:, half + bands + b] = np.cos(big)
        lanes[b] = np.cos(small)
        lanes[half + b] = np.sin(small)
        lanes[bands + b] = np.cos(small)
        lanes[half + bands + b] = np.sin(small)
    high, low = halves(lanes.T)
    gather = np.concatenate([high, low], axis=0)
    high, low = halves(lanes)
    lowest = (lanes - high.astype(np.float64) - low.astype(np.float64)).astype(bf16)
    spread = np.concatenate([high, low, lowest, high, low, high], axis=0)
    return dict(
        forward_left=forward_left,
        inverse_left=inverse_left,
        forward_right=forward_right,
        inverse_right=inverse_right,
        twist_cos=np.cos(twist).astype(np.float32),
        twist_sin=np.sin(twist).astype(np.float32),
        rows=rows.astype(np.float32),
        spread=spread,
        gather=gather,
    )


def split(x):
    high = x.astype(bf16)
    low = (x - high.astype(f32)).astype(bf16)
    return high, low


def mm(left, right):
    return lax.dot_general(left, right, (((1,), (0,)), ((), ())), preferred_element_type=f32)


def dot_rows(table, x):
    high, low = split(x)
    left = jnp.concatenate([table, table[:, : x.shape[0]]], axis=1)
    return mm(left, jnp.concatenate([high, high, low], axis=0))


def dot_cols(x, table):
    high, low = split(x)
    count = x.shape[1]
    right = jnp.concatenate([table[:count], table], axis=0)
    return mm(jnp.concatenate([high, low, high], axis=1), right)


def forward_pair(x, y, left, right, twist_cos, twist_sin):
    u = dot_rows(left, jnp.concatenate([x, y], axis=1))
    spectra = []
    for n in range(2):
        re = u[:ROWS, n * COLS : (n + 1) * COLS]
        im = u[ROWS:, n * COLS : (n + 1) * COLS]
        v = jnp.concatenate(
            [re * twist_cos + im * twist_sin, im * twist_cos - re * twist_sin], axis=1
        )
        spectra.append(dot_cols(v, right))
    return spectra


def times_conj(f, c):
    fr, fi, cr, ci = f[:, :COLS], f[:, COLS:], c[:, :COLS], c[:, COLS:]
    return jnp.concatenate([fr * cr + fi * ci, fr * ci - fi * cr], axis=1)


def inverse_pair(g, h, left, right, twist_cos, twist_sin):
    parts = []
    for x in (g, h):
        w = dot_cols(x, right)
        re, im = w[:, :COLS], w[:, COLS:]
        parts.append(
            jnp.concatenate(
                [re * twist_cos - im * twist_sin, im * twist_cos + re * twist_sin], axis=0
            )
        )
    y = dot_rows(left, jnp.concatenate(parts, axis=1))
    return y[:, :COLS], y[:, COLS:]


def sin_and_cos(x):
    r = x - ((x + 12582912.0) - 12582912.0)
    z = r * r
    s = SIN[4]
    for n in (3, 2, 1, 0):
        s = s * z + SIN[n]
    s = s * r
    c = COS[4]
    for n in (3, 2, 1, 0):
        c = c * z + COS[n]
    return s * c, 1.0 - 0.5 * (s * s)


def fraction_rows(count, offset):
    a = lax.broadcasted_iota(jnp.int32, (count, COLS), 0) + offset
    m = lax.broadcasted_iota(jnp.int32, (count, COLS), 1)
    return (a * COLS + m).astype(f32) * (1.0 / LENGTH)


def zip_rows(x, y):
    low = lax.broadcasted_iota(jnp.int32, x.shape, 0) % 8 < 4
    count = x.shape[0]
    return (
        jnp.where(low, x, pltpu.roll(y, 4, 0)),
        jnp.where(low, pltpu.roll(x, count - 4, 0), y),
    )


def pack_kernel(signal, cotangent, out):
    for q in range(signal.shape[1] // COLS):
        here = pl.ds(q * COLS, COLS)
        for n, part in enumerate(zip_rows(signal[:, here], cotangent[:, here])):
            out[:, n, 8 * q : 8 * q + 8, :] = part.reshape(-1, 8, COLS)


def filter_kernel(
    weights, columns, rates, rows, spread, left, right, tcos, tsin,
    basis, slope, filt, window, norms, spectra,
):
    order = basis.shape[0]
    batch = 4

    def fill(n, carry):
        scaled = jnp.concatenate(
            [rows[...] * weights[pl.ds(n * batch + i, 1), :] for i in range(batch)], axis=0
        )
        high = scaled.astype(bf16)
        rest = scaled - high.astype(f32)
        low = rest.astype(bf16)
        lowest = (rest - low.astype(f32)).astype(bf16)
        turns = mm(jnp.concatenate([high, high, high, low, low, lowest], axis=1), spread[...])
        for i in range(batch):
            basis[n * batch + i] = turns[i * ROWS : (i + 1) * ROWS]
        return carry

    lax.fori_loop(0, order // batch, fill, 0)
    chunk = 64

    def bend(k, carry):
        for n in range(ROWS // chunk):
            here = pl.ds(n * chunk, chunk)
            s, c = sin_and_cos(basis[k, here, :])
            basis[k, here, :] = s
            slope[k, here, :] = c
        return carry

    lax.fori_loop(0, order, bend, 0)
    part = 32

    def mix(n, totals):
        start = pl.multiple_of(n * part, part)
        here = pl.ds(start, part)

        def add(k, acc):
            b = basis[k, here, :]
            return tuple(acc[c] + columns[k, c] * b for c in range(NARROW))

        acc = lax.fori_loop(
            0, order, add, tuple(jnp.zeros((part, COLS), f32) for _ in range(NARROW)), unroll=4
        )
        fraction = fraction_rows(part, start)
        out = []
        for c in range(NARROW):
            win = jnp.exp(-rates[c] * fraction)
            raw = win * acc[c]
            window[c, here, :] = win
            filt[c, here, :] = raw
            out.append(totals[c] + (raw * raw).reshape(part // 8, 8, COLS).sum(0))
        return tuple(out)

    totals = lax.fori_loop(
        0, ROWS // part, mix, tuple(jnp.zeros((8, COLS), f32) for _ in range(NARROW))
    )
    for c in range(NARROW):
        norm = jnp.sqrt(jnp.sum(totals[c], keepdims=True) + TINY)
        norms[pl.ds(c, 1), :] = jnp.broadcast_to(norm, (1, COLS))
        filt[c] = filt[c] / norm
    for c in range(0, NARROW, 2):
        x, y = forward_pair(filt[c], filt[c + 1], left[...], right[...], tcos[...], tsin[...])
        spectra[c] = x
        spectra[c + 1] = y


def main_kernel(
    both, columns, basis, slope, filt, window, norms, rows, gather,
    fleft, fright, ileft, iright, tcos, tsin,
    small, first, cotan,
    dmix, product, second_rows, first_rows,
):
    order = basis.shape[0]
    factor = 1.0 / math.sqrt(LENGTH)
    lane = lax.broadcasted_iota(jnp.int32, (1, COLS), 1)
    scalars = jnp.zeros((1, COLS), f32)
    fraction = fraction_rows(ROWS, 0)
    for c in range(NARROW):
        x = both[pl.ds(c, ROWS, stride=2 * NARROW), :]
        y = both[pl.ds(NARROW + c, ROWS, stride=2 * NARROW), :]
        skip = factor * jnp.sum(x * y, keepdims=True)
        scalars = jnp.where(lane == NARROW + c, skip, scalars)
        val, cot = forward_pair(x, y, fleft[...], fright[...], tcos[...], tsin[...])
        cotan[c] = cot
        product[c] = times_conj(val, cot)
    for c in range(0, NARROW, 2):
        pair = inverse_pair(
            product[c], product[c + 1], ileft[...], iright[...], tcos[...], tsin[...]
        )
        for n in range(2):
            i = c + n
            dfilt = pair[n] * (factor / LENGTH)
            project = jnp.sum(filt[i] * dfilt, keepdims=True)
            norm = norms[pl.ds(i, 1), :][:, :1]
            draw = (dfilt - filt[i] * project) / norm
            decay = -jnp.sum(draw * filt[i] * fraction, keepdims=True) * norm
            dmix[i] = draw * window[i]
            scalars = jnp.where(lane == i, decay, scalars)
    chunk = 64

    def tail(k, carry):
        acc = [jnp.zeros((8, COLS), f32) for _ in range(NARROW)]
        pieces = []
        for n in range(ROWS // chunk):
            here = pl.ds(n * chunk, chunk)
            b = basis[k, here, :]
            mixed = None
            for c in range(NARROW):
                d = dmix[c, here, :]
                acc[c] = acc[c] + (b * d).reshape(chunk // 8, 8, COLS).sum(0)
                mixed = columns[k, c] * d if c == 0 else mixed + columns[k, c] * d
            pieces.append(mixed * slope[k, here, :])
        r = dot_cols(jnp.concatenate(pieces, axis=0), gather[...])
        first_rows[pl.ds(k, 1), :] = jnp.sum(r * rows[...], axis=0, keepdims=True)
        for c in range(NARROW):
            second_rows[pl.ds(c * order + k, 1), :] = jnp.sum(acc[c], axis=0, keepdims=True)
        return carry

    lax.fori_loop(0, order, tail, 0, unroll=2)
    ones = jnp.ones((8, COLS), f32)
    for n in range(NARROW * order // COLS):
        block = second_rows[pl.ds(n * COLS, COLS), :]
        sums = lax.dot_general(
            ones, block, (((1,), (1,)), ((), ())), precision=highest, preferred_element_type=f32
        )
        small[pl.ds(n, 1), :] = sums[:1, :]
    small[pl.ds(2, 1), :] = scalars
    turned = jnp.transpose(first_rows[...], (1, 0))
    half = COLS // 2
    folded = turned[:half] + turned[half:]
    first[...] = jnp.concatenate([folded[:20], folded[20:40]], axis=1)


def input_kernel(both, gains, spectra, cotan, ileft, iright, tcos, tsin, grad):
    for c in range(0, NARROW, 2):
        pair = inverse_pair(
            times_conj(spectra[c], cotan[c]), times_conj(spectra[c + 1], cotan[c + 1]),
            ileft[...], iright[...], tcos[...], tsin[...],
        )
        for n in range(2):
            i = c + n
            y = both[pl.ds(NARROW + i, ROWS, stride=2 * NARROW), :]
            grad[pl.ds(i, ROWS, stride=NARROW), :] = pair[n] * (1.0 / LENGTH) + gains[i] * y


def join_kernel(grad, small, own, one, two, three, out, tile):
    rows = grad.shape[0] // out.shape[0]
    tile[:3] = small[...]
    tile[3:] = own[...] + one[...] + two[...] + three[...]
    out[:, :rows, :] = grad[...].reshape(out.shape[0], rows, COLS)
    out[:, rows:, :] = jnp.broadcast_to(tile[...][None], (out.shape[0],) + tile.shape)


def unpack_kernel(pairs, home, grad, second, decay, skip):
    groups = grad.shape[0] // NARROW
    order = second.shape[0]
    rows = grad.shape[1] // COLS * NARROW
    block = rows + 8
    for p in range(rows // 8):
        even = pairs[:, 0, 8 * p : 8 * p + 8, :].reshape(-1, COLS)
        odd = pairs[:, 1, 8 * p : 8 * p + 8, :].reshape(-1, COLS)
        for n, part in enumerate(zip_rows(even, odd)):
            grad[:, pl.ds((2 * p + n) * COLS, COLS)] = part
    i = lax.broadcasted_iota(jnp.int32, (groups, groups * NARROW), 0)
    j = lax.broadcasted_iota(jnp.int32, (groups, groups * NARROW), 1)
    flat = [jnp.transpose(home[pl.ds(rows + n, groups, stride=block), :], (1, 0)) for n in range(3)]
    total = jnp.zeros(second.shape, f32)
    scalars = jnp.zeros((8, groups * NARROW), f32)
    line = lax.broadcasted_iota(jnp.int32, scalars.shape, 0)
    for c in range(NARROW):
        place = (j == NARROW * i + c).astype(f32)
        mine = flat[c // 2][(c % 2) * order : (c % 2 + 1) * order]
        total = total + jnp.dot(mine, place, precision=highest, preferred_element_type=f32)
        moved = jnp.dot(flat[2][:8], place, precision=highest, preferred_element_type=f32)
        scalars = scalars + jnp.where(line % NARROW == c, moved, 0.0)
    second[...] = total
    decay[...] = jnp.sum(scalars[:NARROW], axis=0, keepdims=True)
    skip[...] = jnp.sum(scalars[NARROW:], axis=0, keepdims=True)


def local(signal, cotangent, first_layer, second_layer, decay_rate, skip_gain):
    groups = lax.axis_size("batch")
    place = lax.axis_index("batch")
    side = lax.axis_index("chan")
    sides = lax.axis_size("chan")
    embed, order = first_layer.shape
    t = make_tables(embed)
    vmem = pl.BlockSpec(memory_space=pltpu.VMEM)
    smem = pl.BlockSpec(memory_space=pltpu.SMEM)
    shape = jax.ShapeDtypeStruct
    rows = signal.shape[1] // COLS * NARROW

    def call(body, name, outs, specs, args, mib, flops=0, scratch=()):
        return pl.pallas_call(
            body,
            out_shape=outs,
            in_specs=specs,
            out_specs=(vmem,) * len(outs),
            scratch_shapes=[pltpu.VMEM(s, f32) for s in scratch],
            compiler_params=pltpu.CompilerParams(vmem_limit_bytes=mib << 20),
            cost_estimate=pl.CostEstimate(flops=flops, bytes_accessed=0, transcendentals=0),
            name=name,
        )(*args)

    (sent,) = call(
        pack_kernel, "pack", (shape((groups // 2, 2, 2 * rows, COLS), f32),), [vmem] * 2,
        (signal, cotangent), 8,
    )
    spread = lax.all_to_all(
        sent.reshape(groups, 2 * rows, COLS), "batch", split_axis=0, concat_axis=0, tiled=True
    ).reshape(-1, COLS)

    columns = lax.dynamic_slice_in_dim(second_layer, place * NARROW, NARROW, 1)
    rates = lax.dynamic_slice_in_dim(decay_rate, place * NARROW, NARROW, 0)
    gains = lax.dynamic_slice_in_dim(skip_gain, place * NARROW, NARROW, 0)
    weights = jnp.pad(first_layer.T * (0.5 / math.pi), ((0, 0), (0, COLS // 2 - embed)))
    weights = jnp.concatenate([weights, weights], axis=1)

    cube = shape((order, ROWS, COLS), f32)
    four = shape((NARROW, ROWS, COLS), f32)
    wide = shape((NARROW, ROWS, 2 * COLS), f32)
    basis, slope, filt, window, norms, spectra = call(
        filter_kernel, "make_filter",
        (cube, cube, four, four, shape((NARROW, COLS), f32), wide),
        [vmem, smem, smem] + [vmem] * 6,
        (
            weights, columns, rates, t["rows"], t["spread"],
            t["forward_left"], t["forward_right"], t["twist_cos"], t["twist_sin"],
        ),
        FILTER_MIB, flops=20_000_000_000,
    )
    small, first, cotan = call(
        main_kernel, "correlate",
        (shape((3, COLS), f32), shape((20, COLS), f32), wide),
        [vmem, smem] + [vmem] * 13,
        (
            spread, columns, basis, slope, filt, window, norms, t["rows"], t["gather"],
            t["forward_left"], t["forward_right"], t["inverse_left"], t["inverse_right"],
            t["twist_cos"], t["twist_sin"],
        ),
        MAIN_MIB, flops=10_000_000_000,
        scratch=(
            (NARROW, ROWS, COLS), (NARROW, ROWS, 2 * COLS), (NARROW * order, COLS), (order, COLS)
        ),
    )

    quarter = first.shape[0] // sides
    pieces = [lax.dynamic_slice_in_dim(first, side * quarter, quarter, 0)]
    for step in range(1, sides):
        ring = [(i, (i + step) % sides) for i in range(sides)]
        piece = lax.dynamic_slice_in_dim(first, (side + step) % sides * quarter, quarter, 0)
        pieces.append(lax.ppermute(piece, "chan", ring))
    (grad,) = call(
        input_kernel, "input_grad", (shape((groups * rows, COLS), f32),),
        [vmem, smem] + [vmem] * 6,
        (
            spread, gains, spectra, cotan, t["inverse_left"], t["inverse_right"],
            t["twist_cos"], t["twist_sin"],
        ),
        16, flops=4_000_000_000,
    )
    (back,) = call(
        join_kernel, "join", (shape((groups, rows + 8, COLS), f32),), [vmem] * 6,
        (grad, small, *pieces), 8, scratch=((8, COLS),),
    )
    home = lax.all_to_all(back, "batch", split_axis=0, concat_axis=0, tiled=True)

    mine = home[:, rows + 3 :].sum(0)
    gathered = [mine]
    for step in range(1, sides):
        ring = [((i + step) % sides, i) for i in range(sides)]
        gathered.append(lax.ppermute(mine, "chan", ring))
    input_grad, second_grad, decay_grad, skip_grad = call(
        unpack_kernel, "unpack",
        (
            shape(signal.shape, f32), shape(second_layer.shape, f32),
            shape((1,) + decay_rate.shape, f32), shape((1,) + skip_gain.shape, f32),
        ),
        [vmem] * 2, (home.reshape(groups // 2, 2, -1, COLS), home.reshape(-1, COLS)), 8,
        flops=1_000_000_000,
    )
    twice = jnp.concatenate(gathered + gathered, axis=0)
    ordered = lax.dynamic_slice_in_dim(
        twice, (sides - side) % sides * quarter, sides * quarter, 0
    )
    first_grad = jnp.concatenate([ordered[:, :order], ordered[:, order:]], axis=0)[:embed]
    return (input_grad, first_grad, second_grad, decay_grad[0], skip_grad[0])


def solution(mesh):
    placed = (P("chan", "batch"), P("chan", "batch"), P(), P(None, "chan"), P("chan"), P("chan"))
    return jax.shard_map(
        local,
        mesh=mesh,
        in_specs=placed,
        out_specs=(P("chan", "batch"), P(), P(None, "chan"), P("chan"), P("chan")),
        check_vma=False,
    )
```

time: 141 us -> 133 us (0.943)
  Pallas kernels: 64.3 us -> 43.9 us
  local copies, waits for them, and re-layouts: 11.3 us -> 28.6 us
  other arithmetic: 5.04 us -> 0.77 us
  starting transfers between devices: 36.8 us -> 34.6 us
  waiting for transfers between devices: 21.9 us -> 23.5 us
    unnamed x13 -> x55, local copies, waits for them, and re-layouts: 2.65 us -> 26.5 us
    pallas_call x2 -> x6, Pallas kernels: 64.3 us -> 43.9 us  [call(): pl.pallas_call(body, out_shape=outs, in_specs=specs, out_specs=(vmem,) *...]
    concatenate x3 -> x0, other arithmetic: 2.95 us -> none  [the longest x1 1.99 us: local(): jnp.concatenate([grad, jnp.broadcast_to(shared, (groups,) + shared.shape)...]
    reshape x3 -> x0, local copies, waits for them, and re-layouts: 2.6 us -> none  [the longest x2 2.47 us: turn(): return x.reshape(groups, NARROW, -1, COLS).transpose(0, 2, 1, 3)]
    ppermute x3, starting transfers between devices: 6.51 us -> 4.64 us  [local(): gathered.append(lax.ppermute(mine, 'chan', ring))]
  transfers between devices with their start and end apart: 8 -> 8, of which waited for: 3 -> 2; matrix products, arithmetic and copies ran while one was open for 4% -> 2% of each run, Pallas kernels for 29% -> 20%
where the time goes in v2:
time: 133 us; the launch traced here: 132 us
  Pallas kernels  43.9 us (33%)
  starting transfers between devices  34.6 us (26%)
  local copies, waits for them, and re-layouts  28.6 us (22%)
  waiting for transfers between devices  23.5 us (18%)
    pallas_call x6, Pallas kernels, call(): pl.pallas_call(body, out_shape=outs, in_specs=specs, out_specs=(vmem,) *...  43.9 us
    unnamed x55, local copies, waits for them, and re-layouts  26.5 us
    all_to_all x1, waiting for transfers between devices, local(): lax.all_to_all(back, 'batch', split_axis=0, concat_axis=0, tiled=True)  22.5 us
    all_to_all x1, starting transfers between devices, local(): lax.all_to_all(sent.reshape(groups, 2 * rows, COLS), 'batch', split_axis=...  15.1 us
    all_to_all x1, starting transfers between devices, local(): lax.all_to_all(back, 'batch', split_axis=0, concat_axis=0, tiled=True)  12.4 us
    ppermute x3, starting transfers between devices, local(): gathered.append(lax.ppermute(mine, 'chan', ring))  4.64 us
  transfers between devices with their start and end apart: 8, of which 2 were waited for; matrix products, arithmetic and copies ran while one was open for 2% of the time, Pallas kernels for 20%

profile of v2, /device:TPU:1, one launch (start us, length us, event | category | flops | bytes accessed | tf_op | source)
XLA Modules:
  0.0 132.3 jit_solution(14209881303438495620)
XLA Ops:
  0.6 0.0 copy-start
  0.6 0.0 copy-start.1
  0.7 1.1 copy-done.1
  1.7 1.0 copy-done.2
  2.8 1.2 pack.1
  3.9 15.1 %all-to-all-start = ((f32[64,32,128]{2,1,0:T(8,128)}), f32[64,32,128]{2,1,0:T(8,128)S(1)}, u32[]{:S(2)}, u32[]{:S(2)}) async-start(f32[64,32,128]{2,1,0:T(8,128)} %bitcast), calls=%async_computation | async-start | bytes 2097152 | tf_op jit(solution)/shard_map/all_to_all | solution.py:388
  19.1 0.8 copy.21
  19.9 0.8 dynamic_slice.24.gains
  20.7 0.8 dynamic_slice.26.rates
  21.4 0.1 pad_maximum_fusion.weights
  21.5 0.0 copy-done
  21.5 0.1 constant_dynamic-slice_fusion.5.columns
  21.6 1.0 copy-done.4
  22.6 0.9 copy-done.7
  23.6 0.9 copy-done.9
  24.5 0.9 copy-done.10
  25.4 0.9 copy-done.12
  26.3 0.9 copy-done.14
  27.2 0.0 copy-start.11
  27.3 0.0 copy-start.13
  27.3 0.0 copy-start.15
  27.3 0.0 copy-start.16
  27.3 23.3 %make_filter.1 = (f32[64,256,128]{2,1,0:T(8,128)S(1)}, f32[64,256,128]{2,1,0:T(8,128)S(1)}, f32[4,256,128]{2,1,0:T(8,128)S(1)}, f32[4,256,128]{2,1,0:T(8,128)S(1...) custom-call(f32[64,128]{1,0:T(8,128)S(1)} %pad_maximum_fusion.weights, ...), custom_call_target="tpu_custom_call" | custom-call | flops 20000000000 | tf_op jit(solution)/shard_map/make_filter/pallas_call | solution.py:373
  50.6 0.0 copy-start.17
  50.6 3.3 %copy-done.17 = f32[64,256,128]{2,1,0:T(8,128)} copy-done((f32[64,256,128]{2,1,0:T(8,128)}, f32[64,256,128]{2,1,0:T(8,128)S(1)}, u32[]{:S(2)}) %copy-start.17) | copy-done | bytes 8388632
  53.9 3.2 %copy-done.19 = f32[64,256,128]{2,1,0:T(8,128)} copy-done((f32[64,256,128]{2,1,0:T(8,128)}, f32[64,256,128]{2,1,0:T(8,128)S(1)}, u32[]{:S(2)}) %copy-start.19) | copy-done | bytes 8388632
  57.1 1.0 copy-done.21
  58.1 0.8 copy-done.23
  58.9 0.8 copy-done.25
  59.7 0.0 all-to-all-done
  59.7 0.0 copy-done.3
  59.7 0.0 copy-done.6
  59.7 0.0 copy-done.8
  59.7 0.0 copy-done.11
  59.8 0.0 copy-done.13
  59.8 0.0 copy-done.15
  59.8 0.0 copy-done.16
  59.8 0.0 copy-start.18
  59.8 3.4 %copy-done.18 = f32[64,256,128]{2,1,0:T(8,128)S(1)} copy-done((f32[64,256,128]{2,1,0:T(8,128)S(1)}, f32[64,256,128]{2,1,0:T(8,128)}, u32[]{:S(2)}) %copy-start.18) | copy-done | bytes 8388632
  63.2 3.4 %copy-done.20 = f32[64,256,128]{2,1,0:T(8,128)S(1)} copy-done((f32[64,256,128]{2,1,0:T(8,128)S(1)}, f32[64,256,128]{2,1,0:T(8,128)}, u32[]{:S(2)}) %copy-start.20) | copy-done | bytes 8388632
  66.5 1.0 copy-done.24
  67.6 1.0 copy-done.26
  68.6 15.3 %correlate.1 = (f32[3,128]{1,0:T(4,128)S(1)}, f32[20,128]{1,0:T(8,128)S(1)}, f32[4,256,256]{2,1,0:T(8,128)S(1)}) custom-call(f32[2048,128]{1,0:T(8,128)S(1)} %bitcast.10, f32[64,4]{1,0:T(8,128)S(1)} %constant_dynamic-slice_fusion.5.columns, f32[64,256,128]{2,1,0:T(8,128)S(1)} %copy-done.18, f32[64,256,128]{2,1,0:T(8,128)S(1)} %copy-done.20, ...), custom_call_target="tpu_custom_call" | custom-call | flops 10000000000 | tf_op jit(solution)/shard_map/correlate/pallas_call | solution.py:373
  84.0 1.3 collective-permute-start
  85.3 1.1 collective-permute-start.1
  86.3 0.0 collective-permute-start.2
  86.3 2.1 %input_grad.1.grad = f32[1024,128]{1,0:T(8,128)S(1)} custom-call(f32[2048,128]{1,0:T(8,128)S(1)} %bitcast.11, f32[4]{0:T(128)S(1)} %dynamic_slice.24.gains, f32[4,256,256]{2,1,0:T(8,128)S(1)} %copy-done.22, f32[4,256,256]{2,1,0:T(8,128)S(1)} %get-tuple-element.24.cotan, bf16[256,1024]{1,0:T(8,128)(2,1)S(1)} %copy-done.3, bf16[512,256]{1,0:T(8,128)(2,1)S(1)} %copy-done.6, ...), custom_call_target="tpu_custom_call" | custom-call | flops 4000000000 | tf_op jit(solution)/shard_map/input_grad/pallas_call | solution.py:373
  88.4 0.0 collective-permute-done.one
  88.4 0.0 collective-permute-done.1.two
  88.4 0.9 collective-permute-done.2.three
  89.4 0.9 join.1
  90.3 12.4 %all-to-all-start.1 = ((f32[64,24,128]{2,1,0:T(8,128)}), f32[64,24,128]{2,1,0:T(8,128)S(1)}, u32[]{:S(2)}, u32[]{:S(2)}) async-start(f32[64,24,128]{2,1,0:T(8,128)} %join.1), calls=%async_computation.1 | async-start | bytes 1572864 | tf_op jit(solution)/shard_map/all_to_all | solution.py:445
  102.8 22.5 %all-to-all-done.1 = f32[64,24,128]{2,1,0:T(8,128)S(1)} async-done(((f32[64,24,128]{2,1,0:T(8,128)}), f32[64,24,128]{2,1,0:T(8,128)S(1)}, u32[]{:S(2)}, u32[]{:S(2)}) %all-to-all-start.1) | async-done | bytes 786464 | tf_op jit(solution)/shard_map/all_to_all | solution.py:445
  125.3 0.1 slice_reduce_fusion
  125.4 2.9 %collective-permute-start.3 = (f32[5,128]{1,0:T(8,128)S(1)}, f32[5,128]{1,0:T(8,128)S(1)}, u32[]{:S(2)}, u32[]{:S(2)}) collective-permute-start(f32[5,128]{1,0:T(8,128)S(1)} %slice_reduce_fusion), channel_id=1, source_target_pairs={{1,0},{2,1},{3,2},{0,3},{5,4},{6,5},{7,6},{4,7},{9,8},{10,9},{11,1... | collective-permute-start | bytes 7688 | tf_op jit(solution)/shard_map/ppermute | solution.py:451
  128.3 0.5 collective-permute-start.4
  128.8 1.2 collective-permute-start.5
  130.0 1.2 unpack.1
  131.2 0.0 collective-permute-done.3
  131.2 0.0 collective-permute-done.4
  131.2 0.0 collective-permute-done.5
  131.2 0.4 concatenate.10
  131.6 0.1 constant_dynamic-slice_fusion
  131.7 0.6 pad_maximum_fusion.1
  (24 shorter events, 0.1 us)
Async XLA Ops:
  0.6 20.9 %copy-start = (f32[64,256]{1,0:T(8,128)S(1)}, f32[64,256]{1,0:T(8,128)}, u32[]{:S(2)}) copy-start(f32[64,256]{1,0:T(8,128)} %param.18) | copy-start | bytes 196612
  0.6 1.1 copy-start.1
  1.7 1.0 copy-start.2
  3.9 55.8 %all-to-all-start = ((f32[64,32,128]{2,1,0:T(8,128)}), f32[64,32,128]{2,1,0:T(8,128)S(1)}, u32[]{:S(2)}, u32[]{:S(2)}) async-start(f32[64,32,128]{2,1,0:T(8,128)} %bitcast), calls=%async_computation | async-start | bytes 2097152 | tf_op jit(solution)/shard_map/all_to_all | solution.py:388
  21.6 1.0 copy-start.4
  22.6 0.9 copy-start.7
  23.6 0.9 copy-start.9
  24.5 0.9 copy-start.10
  25.4 0.9 copy-start.12
  26.3 0.9 copy-start.14
  27.2 32.5 %copy-start.3 = (bf16[256,1024]{1,0:T(8,128)(2,1)S(1)}, bf16[256,1024]{1,0:T(8,128)(2,1)}, u32[]{:S(2)}) copy-start(bf16[256,1024]{1,0:T(8,128)(2,1)} %constant.78.clone.ileft) | copy-start | bytes 1572868
  27.2 32.5 %copy-start.5 = (bf16[512,512]{1,0:T(8,128)(2,1)S(1)}, bf16[512,512]{1,0:T(8,128)(2,1)}, u32[]{:S(2)}) copy-start(bf16[512,512]{1,0:T(8,128)(2,1)} %constant.73.clone.left.fleft) | copy-start | bytes 1572868
  27.2 32.5 %copy-start.6 = (bf16[512,256]{1,0:T(8,128)(2,1)S(1)}, bf16[512,256]{1,0:T(8,128)(2,1)}, u32[]{:S(2)}) copy-start(bf16[512,256]{1,0:T(8,128)(2,1)} %constant.79.clone.iright) | copy-start | bytes 786436
  27.2 32.5 %copy-start.8 = (bf16[512,256]{1,0:T(8,128)(2,1)S(1)}, bf16[512,256]{1,0:T(8,128)(2,1)}, u32[]{:S(2)}) copy-start(bf16[512,256]{1,0:T(8,128)(2,1)} %constant.74.clone.right.fright) | copy-start | bytes 786436
  27.2 32.5 %copy-start.11 = (f32[256,128]{1,0:T(8,128)S(1)}, f32[256,128]{1,0:T(8,128)}, u32[]{:S(2)}) copy-start(f32[256,128]{1,0:T(8,128)} %constant.75.clone.tcos) | copy-start | bytes 393220
  27.3 32.5 %copy-start.13 = (f32[256,128]{1,0:T(8,128)S(1)}, f32[256,128]{1,0:T(8,128)}, u32[]{:S(2)}) copy-start(f32[256,128]{1,0:T(8,128)} %constant.76.clone.tsin) | copy-start | bytes 393220
  27.3 32.5 %copy-start.15 = (f32[256,128]{1,0:T(8,128)S(1)}, f32[256,128]{1,0:T(8,128)}, u32[]{:S(2)}) copy-start(f32[256,128]{1,0:T(8,128)} %constant.71.clone.rows) | copy-start | bytes 393220
  27.3 32.5 %copy-start.16 = (bf16[256,128]{1,0:T(8,128)(2,1)S(1)}, bf16[256,128]{1,0:T(8,128)(2,1)}, u32[]{:S(2)}) copy-start(bf16[256,128]{1,0:T(8,128)(2,1)} %constant.77.clone.gather) | copy-start | bytes 196612
  50.6 3.3 %copy-start.17 = (f32[64,256,128]{2,1,0:T(8,128)}, f32[64,256,128]{2,1,0:T(8,128)S(1)}, u32[]{:S(2)}) copy-start(f32[64,256,128]{2,1,0:T(8,128)S(1)} %get-tuple-element.19.basis) | copy-start | bytes 25165828
  53.9 3.2 %copy-start.19 = (f32[64,256,128]{2,1,0:T(8,128)}, f32[64,256,128]{2,1,0:T(8,128)S(1)}, u32[]{:S(2)}) copy-start(f32[64,256,128]{2,1,0:T(8,128)S(1)} %get-tuple-element.20.slope) | copy-start | bytes 25165828
  57.1 1.0 copy-start.21
  58.1 0.8 copy-start.23
  58.9 0.8 copy-start.25
  59.8 3.4 %copy-start.18 = (f32[64,256,128]{2,1,0:T(8,128)S(1)}, f32[64,256,128]{2,1,0:T(8,128)}, u32[]{:S(2)}) copy-start(f32[64,256,128]{2,1,0:T(8,128)} %copy-done.17) | copy-start | bytes 25165828
  63.2 3.4 %copy-start.20 = (f32[64,256,128]{2,1,0:T(8,128)S(1)}, f32[64,256,128]{2,1,0:T(8,128)}, u32[]{:S(2)}) copy-start(f32[64,256,128]{2,1,0:T(8,128)} %copy-done.19) | copy-start | bytes 25165828
  66.5 1.0 copy-start.24
  67.6 1.0 copy-start.26
  68.6 17.7 %copy-start.22 = (f32[4,256,256]{2,1,0:T(8,128)S(1)}, f32[4,256,256]{2,1,0:T(8,128)}, u32[]{:S(2)}) copy-start(f32[4,256,256]{2,1,0:T(8,128)} %copy-done.21) | copy-start | bytes 3145732
  84.0 4.4 %collective-permute-start = (f32[5,128]{1,0:T(8,128)S(1)}, f32[5,128]{1,0:T(8,128)S(1)}, u32[]{:S(2)}, u32[]{:S(2)}) collective-permute-start(f32[5,128]{1,0:T(8,128)S(1)} %get-tuple-element.35), channel_id=1, source_target_pairs={{0,1},{1,2},{2,3},{3,0},{4,5},{5,6},{6,7},{7,4},{8,9},{9,10},{10,1... | collective-permute-start | bytes 7688 | tf_op jit(solution)/shard_map/ppermute | solution.py:431
  85.3 3.2 %collective-permute-start.1 = (f32[5,128]{1,0:T(8,128)S(1)}, f32[5,128]{1,0:T(8,128)S(1)}, u32[]{:S(2)}, u32[]{:S(2)}) collective-permute-start(f32[5,128]{1,0:T(8,128)S(1)} %get-tuple-element.34), channel_id=1, source_target_pairs={{0,2},{1,3},{2,0},{3,1},{4,6},{5,7},{6,4},{7,5},{8,10},{9,11},{10,... | collective-permute-start | bytes 7688 | tf_op jit(solution)/shard_map/ppermute | solution.py:431
  86.3 3.0 %collective-permute-start.2 = (f32[5,128]{1,0:T(8,128)S(1)}, f32[5,128]{1,0:T(8,128)S(1)}, u32[]{:S(2)}, u32[]{:S(2)}) collective-permute-start(f32[5,128]{1,0:T(8,128)S(1)} %get-tuple-element.33), channel_id=1, source_target_pairs={{0,3},{1,0},{2,1},{3,2},{4,7},{5,4},{6,5},{7,6},{8,11},{9,8},{10,9... | collective-permute-start | bytes 7688 | tf_op jit(solution)/shard_map/ppermute | solution.py:431
  90.3 35.0 %all-to-all-start.1 = ((f32[64,24,128]{2,1,0:T(8,128)}), f32[64,24,128]{2,1,0:T(8,128)S(1)}, u32[]{:S(2)}, u32[]{:S(2)}) async-start(f32[64,24,128]{2,1,0:T(8,128)} %join.1), calls=%async_computation.1 | async-start | bytes 1572864 | tf_op jit(solution)/shard_map/all_to_all | solution.py:445
  125.4 5.8 %collective-permute-start.3 = (f32[5,128]{1,0:T(8,128)S(1)}, f32[5,128]{1,0:T(8,128)S(1)}, u32[]{:S(2)}, u32[]{:S(2)}) collective-permute-start(f32[5,128]{1,0:T(8,128)S(1)} %slice_reduce_fusion), channel_id=1, source_target_pairs={{1,0},{2,1},{3,2},{0,3},{5,4},{6,5},{7,6},{4,7},{9,8},{10,9},{11,1... | collective-permute-start | bytes 7688 | tf_op jit(solution)/shard_map/ppermute | solution.py:451
  128.3 2.9 %collective-permute-start.4 = (f32[5,128]{1,0:T(8,128)S(1)}, f32[5,128]{1,0:T(8,128)S(1)}, u32[]{:S(2)}, u32[]{:S(2)}) collective-permute-start(f32[5,128]{1,0:T(8,128)S(1)} %slice_reduce_fusion), channel_id=1, source_target_pairs={{2,0},{3,1},{0,2},{1,3},{6,4},{7,5},{4,6},{5,7},{10,8},{11,9},{8,1... | collective-permute-start | bytes 7688 | tf_op jit(solution)/shard_map/ppermute | solution.py:451
  128.8 2.4 %collective-permute-start.5 = (f32[5,128]{1,0:T(8,128)S(1)}, f32[5,128]{1,0:T(8,128)S(1)}, u32[]{:S(2)}, u32[]{:S(2)}) collective-permute-start(f32[5,128]{1,0:T(8,128)S(1)} %slice_reduce_fusion), channel_id=1, source_target_pairs={{3,0},{0,1},{1,2},{2,3},{7,4},{4,5},{5,6},{6,7},{11,8},{8,9},{9,10... | collective-permute-start | bytes 7688 | tf_op jit(solution)/shard_map/ppermute | solution.py:451

commit v3 on v2

--- a/solution.py
+++ b/solution.py
@@ -12,8 +12,8 @@
 COLS = 128
 LENGTH = ROWS * COLS
 NARROW = 4
-FILTER_MIB = 24
-MAIN_MIB = 28
+FILTER_BATCH = 16
+TAIL_BATCH = 32
 TINY = 1e-06
 f32 = jnp.float32
 bf16 = jnp.bfloat16
@@ -177,83 +177,96 @@
 
 def filter_kernel(
     weights, columns, rates, rows, spread, left, right, tcos, tsin,
-    basis, slope, filt, window, norms, spectra,
+    high_out, low_out, slope_out, filt_out, window_out, norms, spectra_out,
+    high, low, slope, filt, window, spectra, raws, wins, sems,
 ):
-    order = basis.shape[0]
-    batch = 4
-
-    def fill(n, carry):
+    order = weights.shape[0]
+    batch = FILTER_BATCH
+    wide = batch * COLS
+
+    def copy(source, target, n, here=None):
+        if here is not None:
+            source, target = source.at[:, here], target.at[:, here]
+        return pltpu.make_async_copy(source, target, sems.at[n])
+
+    mixer = jnp.concatenate(split(columns[...]), axis=0)
+    lane = lax.broadcasted_iota(jnp.int32, (8, COLS), 1)
+
+    def block(n, total):
         scaled = jnp.concatenate(
-            [rows[...] * weights[pl.ds(n * batch + i, 1), :] for i in range(batch)], axis=0
+            [weights[...] * rows[pl.ds(n * batch + i, 1), :] for i in range(batch)], axis=0
         )
-        high = scaled.astype(bf16)
-        rest = scaled - high.astype(f32)
-        low = rest.astype(bf16)
-        lowest = (rest - low.astype(f32)).astype(bf16)
-        turns = mm(jnp.concatenate([high, high, high, low, low, lowest], axis=1), spread[...])
+        one = scaled.astype(bf16)
+        rest = scaled - one.astype(f32)
+        two = rest.astype(bf16)
+        three = (rest - two.astype(f32)).astype(bf16)
+        turns = mm(jnp.concatenate([one, one, one, two, two, three], axis=1), spread[...])
         for i in range(batch):
-            basis[n * batch + i] = turns[i * ROWS : (i + 1) * ROWS]
-        return carry
-
-    lax.fori_loop(0, order // batch, fill, 0)
-    chunk = 64
-
-    def bend(k, carry):
-        for n in range(ROWS // chunk):
-            here = pl.ds(n * chunk, chunk)
-            s, c = sin_and_cos(basis[k, here, :])
-            basis[k, here, :] = s
-            slope[k, here, :] = c
-        return carry
-
-    lax.fori_loop(0, order, bend, 0)
-    part = 32
-
-    def mix(n, totals):
-        start = pl.multiple_of(n * part, part)
-        here = pl.ds(start, part)
-
-        def add(k, acc):
-            b = basis[k, here, :]
-            return tuple(acc[c] + columns[k, c] * b for c in range(NARROW))
-
-        acc = lax.fori_loop(
-            0, order, add, tuple(jnp.zeros((part, COLS), f32) for _ in range(NARROW)), unroll=4
-        )
-        fraction = fraction_rows(part, start)
-        out = []
-        for c in range(NARROW):
-            win = jnp.exp(-rates[c] * fraction)
-            raw = win * acc[c]
-            window[c, here, :] = win
-            filt[c, here, :] = raw
-            out.append(totals[c] + (raw * raw).reshape(part // 8, 8, COLS).sum(0))
-        return tuple(out)
-
-    totals = lax.fori_loop(
-        0, ROWS // part, mix, tuple(jnp.zeros((8, COLS), f32) for _ in range(NARROW))
-    )
+            here = pl.ds(pl.multiple_of(n * wide + i * COLS, COLS), COLS)
+            s, c = sin_and_cos(turns[i * order : (i + 1) * order])
+            slope[:, here] = c
+            s_high, s_low = split(s)
+            high[:, here] = s_high
+            low[:, here] = s_low
+        here = pl.ds(pl.multiple_of(n * wide, wide), wide)
+        copy(high, high_out, 0, here).start()
+        copy(low, low_out, 1, here).start()
+        copy(slope, slope_out, 2, here).start()
+        p = mm(mixer, high[:, here])
+        r = mm(mixer, low[:, here])
+        mixed = p[:8] + p[8:] + (r[:8] + r[8:])
+        for i in range(batch):
+            a = n * batch + i
+            fraction = (a * COLS + lane).astype(f32) * (1.0 / LENGTH)
+            win = jnp.exp(-rates[...] * fraction)
+            raw = win * mixed[:, i * COLS : (i + 1) * COLS]
+            raws[pl.ds(pl.multiple_of(a * 8, 8), 8), :] = raw
+            wins[pl.ds(pl.multiple_of(a * 8, 8), 8), :] = win
+            total = total + raw * raw
+        return total
+
+    total = lax.fori_loop(0, ROWS // batch, block, jnp.zeros((8, COLS), f32))
+    norm = jnp.sqrt(jnp.sum(total, axis=1, keepdims=True) + TINY)
+    norms[...] = jnp.broadcast_to(norm, norms.shape)
     for c in range(NARROW):
-        norm = jnp.sqrt(jnp.sum(totals[c], keepdims=True) + TINY)
-        norms[pl.ds(c, 1), :] = jnp.broadcast_to(norm, (1, COLS))
-        filt[c] = filt[c] / norm
+        filt[c] = raws[pl.ds(c, ROWS, stride=8), :] / norms[pl.ds(c, 1), :]
+        window[c] = wins[pl.ds(c, ROWS, stride=8), :]
+    copy(filt, filt_out, 3).start()
+    copy(window, window_out, 4).start()
     for c in range(0, NARROW, 2):
         x, y = forward_pair(filt[c], filt[c + 1], left[...], right[...], tcos[...], tsin[...])
         spectra[c] = x
         spectra[c + 1] = y
+    copy(spectra, spectra_out, 5).start()
+    copy(high, high_out, 0).wait()
+    copy(low, low_out, 1).wait()
+    copy(slope, slope_out, 2).wait()
+    copy(filt, filt_out, 3).wait()
+    copy(window, window_out, 4).wait()
+    copy(spectra, spectra_out, 5).wait()
 
 
 def main_kernel(
-    both, columns, basis, slope, filt, window, norms, rows, gather,
-    fleft, fright, ileft, iright, tcos, tsin,
+    both, columns, norms, rows, gather, fleft, fright, ileft, iright, tcos, tsin,
+    high_in, low_in, slope_in, filt_in, window_in,
     small, first, cotan,
-    dmix, product, second_rows, first_rows,
+    high, low, slope, filt, window, dmix, product, sems,
 ):
-    order = basis.shape[0]
+    order = slope.shape[0]
     factor = 1.0 / math.sqrt(LENGTH)
+    copies = [
+        pltpu.make_async_copy(source, target, sems.at[n])
+        for n, (source, target) in enumerate((
+            (filt_in, filt), (window_in, window),
+            (high_in, high), (low_in, low), (slope_in, slope),
+        ))
+    ]
+    for one in copies:
+        one.start()
     lane = lax.broadcasted_iota(jnp.int32, (1, COLS), 1)
     scalars = jnp.zeros((1, COLS), f32)
     fraction = fraction_rows(ROWS, 0)
+    dmix[...] = jnp.zeros(dmix.shape, f32)
     for c in range(NARROW):
         x = both[pl.ds(c, ROWS, stride=2 * NARROW), :]
         y = both[pl.ds(NARROW + c, ROWS, stride=2 * NARROW), :]
@@ -262,6 +275,8 @@
         val, cot = forward_pair(x, y, fleft[...], fright[...], tcos[...], tsin[...])
         cotan[c] = cot
         product[c] = times_conj(val, cot)
+    copies[0].wait()
+    copies[1].wait()
     for c in range(0, NARROW, 2):
         pair = inverse_pair(
             product[c], product[c + 1], ileft[...], iright[...], tcos[...], tsin[...]
@@ -273,38 +288,48 @@
             norm = norms[pl.ds(i, 1), :][:, :1]
             draw = (dfilt - filt[i] * project) / norm
             decay = -jnp.sum(draw * filt[i] * fraction, keepdims=True) * norm
-            dmix[i] = draw * window[i]
+            dmix[pl.ds(i, ROWS, stride=8), :] = draw * window[i]
             scalars = jnp.where(lane == i, decay, scalars)
-    chunk = 64
-
-    def tail(k, carry):
-        acc = [jnp.zeros((8, COLS), f32) for _ in range(NARROW)]
-        pieces = []
-        for n in range(ROWS // chunk):
-            here = pl.ds(n * chunk, chunk)
-            b = basis[k, here, :]
-            mixed = None
-            for c in range(NARROW):
-                d = dmix[c, here, :]
-                acc[c] = acc[c] + (b * d).reshape(chunk // 8, 8, COLS).sum(0)
-                mixed = columns[k, c] * d if c == 0 else mixed + columns[k, c] * d
-            pieces.append(mixed * slope[k, here, :])
-        r = dot_cols(jnp.concatenate(pieces, axis=0), gather[...])
-        first_rows[pl.ds(k, 1), :] = jnp.sum(r * rows[...], axis=0, keepdims=True)
-        for c in range(NARROW):
-            second_rows[pl.ds(c * order + k, 1), :] = jnp.sum(acc[c], axis=0, keepdims=True)
-        return carry
-
-    lax.fori_loop(0, order, tail, 0, unroll=2)
-    ones = jnp.ones((8, COLS), f32)
-    for n in range(NARROW * order // COLS):
-        block = second_rows[pl.ds(n * COLS, COLS), :]
-        sums = lax.dot_general(
-            ones, block, (((1,), (1,)), ((), ())), precision=highest, preferred_element_type=f32
-        )
-        small[pl.ds(n, 1), :] = sums[:1, :]
-    small[pl.ds(2, 1), :] = scalars
-    turned = jnp.transpose(first_rows[...], (1, 0))
+    lanes = lax.broadcasted_iota(jnp.int32, columns.shape, 1)
+    col_high = columns[...].astype(bf16).astype(f32)
+    mixer = jnp.where(lanes // 8 == 2, columns[...] - col_high, col_high).astype(bf16)[:, :32]
+    copies[2].wait()
+    copies[3].wait()
+    copies[4].wait()
+    batch = TAIL_BATCH
+    wide = batch * COLS
+    contract = (((1,), (1,)), ((), ()))
+
+    def tail(n, carry):
+        firsts, seconds = carry
+        stack = []
+        for i in range(batch):
+            d = dmix[pl.ds(pl.multiple_of((n * batch + i) * 8, 8), 8), :]
+            d_high = d.astype(bf16).astype(f32)
+            stack.append(
+                jnp.concatenate([d_high, d - d_high, d_high, jnp.zeros_like(d)], axis=0).astype(bf16)
+            )
+        stack = jnp.concatenate(stack, axis=1)
+        here = pl.ds(pl.multiple_of(n * wide, wide), wide)
+        for part in (high, low):
+            seconds = seconds + lax.dot_general(
+                stack[:16], part[:, here], contract, preferred_element_type=f32
+            )
+        q = mm(mixer, stack) * slope[:, here]
+        q = jnp.concatenate([q[:, i * COLS : (i + 1) * COLS] for i in range(batch)], axis=0)
+        r = dot_cols(q, gather[...])
+        for i in range(batch):
+            firsts = firsts + r[i * order : (i + 1) * order] * rows[pl.ds(n * batch + i, 1), :]
+        return firsts, seconds
+
+    firsts, seconds = lax.fori_loop(
+        0, ROWS // batch, tail, (jnp.zeros((order, COLS), f32), jnp.zeros((16, order), f32))
+    )
+    seconds = seconds[:8] + seconds[8:]
+    small[:1] = jnp.concatenate([seconds[0:1], seconds[1:2]], axis=1)
+    small[1:2] = jnp.concatenate([seconds[2:3], seconds[3:4]], axis=1)
+    small[2:3] = scalars
+    turned = jnp.transpose(firsts, (1, 0))
     half = COLS // 2
     folded = turned[:half] + turned[half:]
     first[...] = jnp.concatenate([folded[:20], folded[20:40]], axis=1)
@@ -366,16 +391,17 @@
     t = make_tables(embed)
     vmem = pl.BlockSpec(memory_space=pltpu.VMEM)
     smem = pl.BlockSpec(memory_space=pltpu.SMEM)
+    hbm = pl.BlockSpec(memory_space=pltpu.HBM)
     shape = jax.ShapeDtypeStruct
     rows = signal.shape[1] // COLS * NARROW
 
-    def call(body, name, outs, specs, args, mib, flops=0, scratch=()):
+    def call(body, name, outs, specs, args, mib, flops=0, scratch=(), out_specs=None):
         return pl.pallas_call(
             body,
             out_shape=outs,
             in_specs=specs,
-            out_specs=(vmem,) * len(outs),
-            scratch_shapes=[pltpu.VMEM(s, f32) for s in scratch],
+            out_specs=out_specs or (vmem,) * len(outs),
+            scratch_shapes=list(scratch),
             compiler_params=pltpu.CompilerParams(vmem_limit_bytes=mib << 20),
             cost_estimate=pl.CostEstimate(flops=flops, bytes_accessed=0, transcendentals=0),
             name=name,
@@ -394,33 +420,43 @@
     gains = lax.dynamic_slice_in_dim(skip_gain, place * NARROW, NARROW, 0)
     weights = jnp.pad(first_layer.T * (0.5 / math.pi), ((0, 0), (0, COLS // 2 - embed)))
     weights = jnp.concatenate([weights, weights], axis=1)
-
-    cube = shape((order, ROWS, COLS), f32)
-    four = shape((NARROW, ROWS, COLS), f32)
-    wide = shape((NARROW, ROWS, 2 * COLS), f32)
-    basis, slope, filt, window, norms, spectra = call(
+    eight = jnp.pad(columns, ((0, 0), (0, 8 - NARROW)))
+    tiled = jnp.pad(jnp.concatenate([eight] * 3, axis=1), ((0, 0), (0, COLS - 24)))
+    rates = jnp.broadcast_to(jnp.pad(rates, (0, 8 - NARROW))[:, None], (8, COLS))
+
+    full = (order, LENGTH)
+    four = (NARROW, ROWS, COLS)
+    wide = (NARROW, ROWS, 2 * COLS)
+    kept = ((full, bf16), (full, bf16), (full, f32), (four, f32), (four, f32))
+    tall = (ROWS * 8, COLS)
+    *state, norms, spectra = call(
         filter_kernel, "make_filter",
-        (cube, cube, four, four, shape((NARROW, COLS), f32), wide),
-        [vmem, smem, smem] + [vmem] * 6,
+        tuple(shape(*k) for k in kept) + (shape((8, COLS), f32), shape(wide, f32)),
+        [vmem] * 9,
         (
-            weights, columns, rates, t["rows"], t["spread"],
+            weights, eight.T, rates, t["rows"], t["spread"],
             t["forward_left"], t["forward_right"], t["twist_cos"], t["twist_sin"],
         ),
-        FILTER_MIB, flops=20_000_000_000,
+        40, flops=20_000_000_000,
+        scratch=[pltpu.VMEM(*k) for k in kept] + [
+            pltpu.VMEM(wide, f32), pltpu.VMEM(tall, f32), pltpu.VMEM(tall, f32),
+            pltpu.SemaphoreType.DMA((6,)),
+        ],
+        out_specs=(hbm,) * 5 + (vmem, hbm),
     )
     small, first, cotan = call(
         main_kernel, "correlate",
-        (shape((3, COLS), f32), shape((20, COLS), f32), wide),
-        [vmem, smem] + [vmem] * 13,
+        (shape((3, COLS), f32), shape((20, COLS), f32), shape(wide, f32)),
+        [vmem] * 11 + [hbm] * 5,
         (
-            spread, columns, basis, slope, filt, window, norms, t["rows"], t["gather"],
+            spread, tiled, norms, t["rows"], t["gather"],
             t["forward_left"], t["forward_right"], t["inverse_left"], t["inverse_right"],
-            t["twist_cos"], t["twist_sin"],
+            t["twist_cos"], t["twist_sin"], *state,
         ),
-        MAIN_MIB, flops=10_000_000_000,
-        scratch=(
-            (NARROW, ROWS, COLS), (NARROW, ROWS, 2 * COLS), (NARROW * order, COLS), (order, COLS)
-        ),
+        40, flops=10_000_000_000,
+        scratch=[pltpu.VMEM(*k) for k in kept] + [
+            pltpu.VMEM(tall, f32), pltpu.VMEM(wide, f32), pltpu.SemaphoreType.DMA((5,)),
+        ],
     )
 
     quarter = first.shape[0] // sides
@@ -440,7 +476,7 @@
     )
     (back,) = call(
         join_kernel, "join", (shape((groups, rows + 8, COLS), f32),), [vmem] * 6,
-        (grad, small, *pieces), 8, scratch=((8, COLS),),
+        (grad, small, *pieces), 8, scratch=[pltpu.VMEM((8, COLS), f32)],
     )
     home = lax.all_to_all(back, "batch", split_axis=0, concat_axis=0, tiled=True)
 

time: 133 us -> 118 us (0.89)
  local copies, waits for them, and re-layouts: 28.6 us -> 16.2 us
  Pallas kernels: 43.9 us -> 41.3 us
    unnamed x55 -> x52, local copies, waits for them, and re-layouts: 26.5 us -> 15.3 us
    pallas_call x6, Pallas kernels: 43.9 us -> 41.3 us  [call(): pl.pallas_call(body, out_shape=outs, in_specs=specs, out_specs=out_specs...]
  transfers between devices with their start and end apart: 8 -> 8, of which waited for: 2 -> 2; matrix products, arithmetic and copies ran while one was open for 2% -> 1% of each run, Pallas kernels for 20% -> 21%
where the time goes in v3:
time: 118 us; the launch traced here: 117 us
  Pallas kernels  41.3 us (35%)
  starting transfers between devices  34.7 us (29%)
  waiting for transfers between devices  23.5 us (20%)
  local copies, waits for them, and re-layouts  16.2 us (14%)
    pallas_call x6, Pallas kernels, call(): pl.pallas_call(body, out_shape=outs, in_specs=specs, out_specs=out_specs...  41.3 us
    all_to_all x1, waiting for transfers between devices, local(): lax.all_to_all(back, 'batch', split_axis=0, concat_axis=0, tiled=True)  22.6 us
    unnamed x52, local copies, waits for them, and re-layouts  15.3 us
    all_to_all x1, starting transfers between devices, local(): lax.all_to_all(sent.reshape(groups, 2 * rows, COLS), 'batch', split_axis=...  15.1 us
    all_to_all x1, starting transfers between devices, local(): lax.all_to_all(back, 'batch', split_axis=0, concat_axis=0, tiled=True)  11.4 us
    ppermute x3, starting transfers between devices, local(): gathered.append(lax.ppermute(mine, 'chan', ring))  4.61 us
    ppermute x3, starting transfers between devices, local(): pieces.append(lax.ppermute(piece, 'chan', ring))  3.62 us
  transfers between devices with their start and end apart: 8, of which 2 were waited for; matrix products, arithmetic and copies ran while one was open for 1% of the time, Pallas kernels for 21%

profile of v3, /device:TPU:1, one launch (start us, length us, event | category | flops | bytes accessed | tf_op | source)
XLA Modules:
  0.0 117.4 jit_solution(1522310131864911233)
XLA Ops:
  0.6 0.0 copy-start
  0.6 0.0 copy-start.1
  0.7 1.1 copy-done.1
  1.7 1.0 copy-done.2
  2.8 0.0 copy-start.6
  2.8 0.0 copy-start.7
  2.8 0.0 copy-start.8
  2.8 0.0 copy-start.9
  2.8 0.0 copy-start.10
  2.8 1.2 %pack.1 = f32[32,2,32,128]{3,2,1,0:T(8,128)} custom-call(f32[256,512]{1,0:T(8,128)S(1)} %copy-done.1, f32[256,512]{1,0:T(8,128)S(1)} %copy-done.2), custom_call_target="tpu_custom_call" | custom-call | tf_op jit(solution)/shard_map/pack/pallas_call | solution.py:399
  4.0 15.1 %all-to-all-start = ((f32[64,32,128]{2,1,0:T(8,128)}), f32[64,32,128]{2,1,0:T(8,128)S(1)}, u32[]{:S(2)}, u32[]{:S(2)}) async-start(f32[64,32,128]{2,1,0:T(8,128)} %bitcast), calls=%async_computation | async-start | bytes 2097152 | tf_op jit(solution)/shard_map/all_to_all | solution.py:414
  19.2 0.0 copy-done.22
  19.2 0.1 copy.25
  19.3 0.0 copy-done.23
  19.3 0.1 dynamic_slice.24.gains
  19.4 0.0 copy-done
  19.4 0.1 constant_dynamic-slice_fusion.5
  19.5 0.1 copy.29
  19.5 0.0 copy-done.24
  19.5 0.1 dynamic_slice.26
  19.7 0.1 copy.28
  19.8 0.1 pad_maximum_fusion.weights
  19.8 0.1 broadcast_in_dim.2.rates
  19.9 0.0 copy-done.4
  19.9 0.0 copy-done.6
  19.9 0.0 copy-done.7
  19.9 0.0 copy-done.8
  19.9 0.0 copy-done.9
  19.9 0.0 copy-start.3
  20.0 0.0 copy-start.5
  20.0 0.0 copy-start.11
  20.0 21.8 %make_filter.1 = (bf16[64,32768]{1,0:T(8,128)(2,1)S(1)}, bf16[64,32768]{1,0:T(8,128)(2,1)S(1)}, f32[64,32768]{1,0:T(8,128)}, f32[4,256,128]{2,1,0:T(8,128)S(1)},...) custom-call(f32[64,128]{1,0:T(8,128)S(1)} %pad_maximum_fusion.weights, ...), custom_call_target="tpu_custom_call" | custom-call | flops 20000000000 | tf_op jit(solution)/shard_map/make_filter/pallas_call | solution.py:399
  41.8 2.0 %copy-done.12 = bf16[64,32768]{1,0:T(8,128)(2,1)} copy-done((bf16[64,32768]{1,0:T(8,128)(2,1)}, bf16[64,32768]{1,0:T(8,128)(2,1)S(1)}, u32[]{:S(2)}) %copy-start.12) | copy-done | bytes 4194328
  43.8 1.9 %copy-done.14 = bf16[64,32768]{1,0:T(8,128)(2,1)} copy-done((bf16[64,32768]{1,0:T(8,128)(2,1)}, bf16[64,32768]{1,0:T(8,128)(2,1)S(1)}, u32[]{:S(2)}) %copy-start.14) | copy-done | bytes 4194328
  45.7 1.0 copy-done.16
  46.6 0.8 copy-done.18
  47.4 0.8 copy-done.20
  48.2 0.0 all-to-all-done
  48.3 2.2 %copy-done.13 = bf16[64,32768]{1,0:T(8,128)(2,1)S(1)} copy-done((bf16[64,32768]{1,0:T(8,128)(2,1)S(1)}, bf16[64,32768]{1,0:T(8,128)(2,1)}, u32[]{:S(2)}) %copy-start.13) | copy-done | bytes 4194328
  50.5 2.2 %copy-done.15 = bf16[64,32768]{1,0:T(8,128)(2,1)S(1)} copy-done((bf16[64,32768]{1,0:T(8,128)(2,1)S(1)}, bf16[64,32768]{1,0:T(8,128)(2,1)}, u32[]{:S(2)}) %copy-start.15) | copy-done | bytes 4194328
  52.6 1.0 copy-done.19
  53.7 1.0 copy-done.21
  54.7 14.1 %correlate.1 = (f32[3,128]{1,0:T(4,128)S(1)}, f32[20,128]{1,0:T(8,128)S(1)}, f32[4,256,256]{2,1,0:T(8,128)S(1)}) custom-call(f32[2048,128]{1,0:T(8,128)S(1)} %bitcast.12, f32[64,128]{1,0:T(8,128)S(1)} %pad.19.columns, f32[8,128]{1,0:T(8,128)S(1)} %get-tuple-element.20.norms, f32[256,128]{1,0:T(8,128)S(1)} %copy-done.10, bf16[256,128]{1,0:T(8,128)(2,1)S(1)} %copy-done.11, ...), custom_call_target="tpu_custom_call" | custom-call | flops 10000000000 | tf_op jit(solution)/shard_map/correlate/pallas_call | solution.py:399
  68.9 2.6 %collective-permute-start = (f32[5,128]{1,0:T(8,128)S(1)}, f32[5,128]{1,0:T(8,128)S(1)}, u32[]{:S(2)}, u32[]{:S(2)}) collective-permute-start(f32[5,128]{1,0:T(8,128)S(1)} %get-tuple-element.37), channel_id=1, source_target_pairs={{0,1},{1,2},{2,3},{3,0},{4,5},{5,6},{6,7},{7,4},{8,9},{9,10},{10,1... | collective-permute-start | bytes 7688 | tf_op jit(solution)/shard_map/ppermute | solution.py:467
  71.4 1.1 collective-permute-start.1
  72.5 0.0 collective-permute-start.2
  72.5 2.1 %input_grad.1.grad = f32[1024,128]{1,0:T(8,128)S(1)} custom-call(f32[2048,128]{1,0:T(8,128)S(1)} %bitcast.13, f32[4]{0:T(128)S(1)} %dynamic_slice.24.gains, f32[4,256,256]{2,1,0:T(8,128)S(1)} %copy-done.17, f32[4,256,256]{2,1,0:T(8,128)S(1)} %get-tuple-element.26.cotan, bf16[256,1024]{1,0:T(8,128)(2,1)S(1)} %copy-done.3, bf16[512,256]{1,0:T(8,128)(2,1)S(1)} %copy-done.5, ...), custom_call_target="tpu_custom_call" | custom-call | flops 4000000000 | tf_op jit(solution)/shard_map/input_grad/pallas_call | solution.py:399
  74.6 0.0 collective-permute-done.one
  74.6 0.0 collective-permute-done.1.two
  74.6 0.9 collective-permute-done.2.three
  75.5 0.9 join.1
  76.5 11.4 %all-to-all-start.1 = ((f32[64,24,128]{2,1,0:T(8,128)}), f32[64,24,128]{2,1,0:T(8,128)S(1)}, u32[]{:S(2)}, u32[]{:S(2)}) async-start(f32[64,24,128]{2,1,0:T(8,128)} %join.1), calls=%async_computation.1 | async-start | bytes 1572864 | tf_op jit(solution)/shard_map/all_to_all | solution.py:481
  87.9 22.6 %all-to-all-done.1 = f32[64,24,128]{2,1,0:T(8,128)S(1)} async-done(((f32[64,24,128]{2,1,0:T(8,128)}), f32[64,24,128]{2,1,0:T(8,128)S(1)}, u32[]{:S(2)}, u32[]{:S(2)}) %all-to-all-start.1) | async-done | bytes 786464 | tf_op jit(solution)/shard_map/all_to_all | solution.py:481
  110.4 0.1 slice_reduce_fusion
  110.5 2.9 %collective-permute-start.3 = (f32[5,128]{1,0:T(8,128)S(1)}, f32[5,128]{1,0:T(8,128)S(1)}, u32[]{:S(2)}, u32[]{:S(2)}) collective-permute-start(f32[5,128]{1,0:T(8,128)S(1)} %slice_reduce_fusion), channel_id=1, source_target_pairs={{1,0},{2,1},{3,2},{0,3},{5,4},{6,5},{7,6},{4,7},{9,8},{10,9},{11,1... | collective-permute-start | bytes 7688 | tf_op jit(solution)/shard_map/ppermute | solution.py:487
  113.4 0.6 collective-permute-start.4
  113.9 1.2 collective-permute-start.5
  115.1 1.2 %unpack.1 = (f32[256,512]{1,0:T(8,128)}, f32[64,256]{1,0:T(8,128)}, f32[1,256]{1,0:T(1,128)}, f32[1,256]{1,0:T(1,128)}) custom-call(f32[32,2,24,128]{3,2,1,0:T(8,128)S(1)} %bitcast.10, f32[1536,128]{1,0:T(8,128)S(1)} %bitcast.11), custom_call_target="tpu_custom_call" | custom-call | flops 1000000000 | tf_op jit(solution)/shard_map/unpack/pallas_call | solution.py:399
  116.3 0.0 collective-permute-done.3
  116.3 0.0 collective-permute-done.4
  116.3 0.0 collective-permute-done.5
  116.3 0.4 concatenate.14
  116.7 0.1 constant_dynamic-slice_fusion
  116.8 0.6 pad_maximum_fusion.1
  (27 shorter events, 0.1 us)
Async XLA Ops:
  0.6 18.7 %copy-start = (f32[64,256]{1,0:T(8,128)S(1)}, f32[64,256]{1,0:T(8,128)}, u32[]{:S(2)}) copy-start(f32[64,256]{1,0:T(8,128)} %param.18) | copy-start | bytes 196612
  0.6 1.1 copy-start.1
  1.7 1.0 copy-start.2
  2.8 16.4 %copy-start.22 = (f32[33,64]{1,0:T(8,128)S(1)}, f32[33,64]{1,0:T(8,128)}, u32[]{:S(2)}) copy-start(f32[33,64]{1,0:T(8,128)} %param.17) | copy-start | bytes 25348
  2.8 16.5 %copy-start.23 = (f32[256]{0:T(256)S(1)}, f32[256]{0:T(256)}, u32[]{:S(2)}) copy-start(f32[256]{0:T(256)} %param.20) | copy-start | bytes 3076
  2.8 16.8 %copy-start.24 = (f32[256]{0:T(256)S(1)}, f32[256]{0:T(256)}, u32[]{:S(2)}) copy-start(f32[256]{0:T(256)} %param.19) | copy-start | bytes 3076
  2.8 17.1 %copy-start.4 = (bf16[512,512]{1,0:T(8,128)(2,1)S(1)}, bf16[512,512]{1,0:T(8,128)(2,1)}, u32[]{:S(2)}) copy-start(bf16[512,512]{1,0:T(8,128)(2,1)} %constant.73.clone.left.fleft) | copy-start | bytes 1572868
  2.8 17.1 %copy-start.6 = (bf16[512,256]{1,0:T(8,128)(2,1)S(1)}, bf16[512,256]{1,0:T(8,128)(2,1)}, u32[]{:S(2)}) copy-start(bf16[512,256]{1,0:T(8,128)(2,1)} %constant.74.clone.right.fright) | copy-start | bytes 786436
  2.8 17.1 %copy-start.7 = (bf16[768,128]{1,0:T(8,128)(2,1)S(1)}, bf16[768,128]{1,0:T(8,128)(2,1)}, u32[]{:S(2)}) copy-start(bf16[768,128]{1,0:T(8,128)(2,1)} %constant.72.clone.spread) | copy-start | bytes 589828
  2.8 17.1 %copy-start.8 = (f32[256,128]{1,0:T(8,128)S(1)}, f32[256,128]{1,0:T(8,128)}, u32[]{:S(2)}) copy-start(f32[256,128]{1,0:T(8,128)} %constant.75.clone.tcos) | copy-start | bytes 393220
  2.8 17.1 %copy-start.9 = (f32[256,128]{1,0:T(8,128)S(1)}, f32[256,128]{1,0:T(8,128)}, u32[]{:S(2)}) copy-start(f32[256,128]{1,0:T(8,128)} %constant.76.clone.tsin) | copy-start | bytes 393220
  2.8 17.1 %copy-start.10 = (f32[256,128]{1,0:T(8,128)S(1)}, f32[256,128]{1,0:T(8,128)}, u32[]{:S(2)}) copy-start(f32[256,128]{1,0:T(8,128)} %constant.71.clone.rows) | copy-start | bytes 393220
  4.0 44.2 %all-to-all-start = ((f32[64,32,128]{2,1,0:T(8,128)}), f32[64,32,128]{2,1,0:T(8,128)S(1)}, u32[]{:S(2)}, u32[]{:S(2)}) async-start(f32[64,32,128]{2,1,0:T(8,128)} %bitcast), calls=%async_computation | async-start | bytes 2097152 | tf_op jit(solution)/shard_map/all_to_all | solution.py:414
  19.9 28.3 %copy-start.3 = (bf16[256,1024]{1,0:T(8,128)(2,1)S(1)}, bf16[256,1024]{1,0:T(8,128)(2,1)}, u32[]{:S(2)}) copy-start(bf16[256,1024]{1,0:T(8,128)(2,1)} %constant.78.clone.ileft) | copy-start | bytes 1572868
  20.0 28.3 %copy-start.5 = (bf16[512,256]{1,0:T(8,128)(2,1)S(1)}, bf16[512,256]{1,0:T(8,128)(2,1)}, u32[]{:S(2)}) copy-start(bf16[512,256]{1,0:T(8,128)(2,1)} %constant.79.clone.iright) | copy-start | bytes 786436
  20.0 28.3 %copy-start.11 = (bf16[256,128]{1,0:T(8,128)(2,1)S(1)}, bf16[256,128]{1,0:T(8,128)(2,1)}, u32[]{:S(2)}) copy-start(bf16[256,128]{1,0:T(8,128)(2,1)} %constant.77.clone.gather) | copy-start | bytes 196612
  41.8 2.0 %copy-start.12 = (bf16[64,32768]{1,0:T(8,128)(2,1)}, bf16[64,32768]{1,0:T(8,128)(2,1)S(1)}, u32[]{:S(2)}) copy-start(bf16[64,32768]{1,0:T(8,128)(2,1)S(1)} %get-tuple-element.21.high_in) | copy-start | bytes 12582916
  43.7 1.9 %copy-start.14 = (bf16[64,32768]{1,0:T(8,128)(2,1)}, bf16[64,32768]{1,0:T(8,128)(2,1)S(1)}, u32[]{:S(2)}) copy-start(bf16[64,32768]{1,0:T(8,128)(2,1)S(1)} %get-tuple-element.22.low_in) | copy-start | bytes 12582916
  45.7 1.0 copy-start.16
  46.6 0.8 copy-start.18
  47.4 0.8 copy-start.20
  48.3 2.2 %copy-start.13 = (bf16[64,32768]{1,0:T(8,128)(2,1)S(1)}, bf16[64,32768]{1,0:T(8,128)(2,1)}, u32[]{:S(2)}) copy-start(bf16[64,32768]{1,0:T(8,128)(2,1)} %copy-done.12) | copy-start | bytes 12582916
  50.5 2.2 %copy-start.15 = (bf16[64,32768]{1,0:T(8,128)(2,1)S(1)}, bf16[64,32768]{1,0:T(8,128)(2,1)}, u32[]{:S(2)}) copy-start(bf16[64,32768]{1,0:T(8,128)(2,1)} %copy-done.14) | copy-start | bytes 12582916
  52.6 1.0 copy-start.19
  53.7 1.0 copy-start.21
  54.7 17.8 %copy-start.17 = (f32[4,256,256]{2,1,0:T(8,128)S(1)}, f32[4,256,256]{2,1,0:T(8,128)}, u32[]{:S(2)}) copy-start(f32[4,256,256]{2,1,0:T(8,128)} %copy-done.16) | copy-start | bytes 3145732
  68.9 5.7 %collective-permute-start = (f32[5,128]{1,0:T(8,128)S(1)}, f32[5,128]{1,0:T(8,128)S(1)}, u32[]{:S(2)}, u32[]{:S(2)}) collective-permute-start(f32[5,128]{1,0:T(8,128)S(1)} %get-tuple-element.37), channel_id=1, source_target_pairs={{0,1},{1,2},{2,3},{3,0},{4,5},{5,6},{6,7},{7,4},{8,9},{9,10},{10,1... | collective-permute-start | bytes 7688 | tf_op jit(solution)/shard_map/ppermute | solution.py:467
  71.4 3.2 %collective-permute-start.1 = (f32[5,128]{1,0:T(8,128)S(1)}, f32[5,128]{1,0:T(8,128)S(1)}, u32[]{:S(2)}, u32[]{:S(2)}) collective-permute-start(f32[5,128]{1,0:T(8,128)S(1)} %get-tuple-element.36), channel_id=1, source_target_pairs={{0,2},{1,3},{2,0},{3,1},{4,6},{5,7},{6,4},{7,5},{8,10},{9,11},{10,... | collective-permute-start | bytes 7688 | tf_op jit(solution)/shard_map/ppermute | solution.py:467
  72.5 3.0 %collective-permute-start.2 = (f32[5,128]{1,0:T(8,128)S(1)}, f32[5,128]{1,0:T(8,128)S(1)}, u32[]{:S(2)}, u32[]{:S(2)}) collective-permute-start(f32[5,128]{1,0:T(8,128)S(1)} %get-tuple-element.35), channel_id=1, source_target_pairs={{0,3},{1,0},{2,1},{3,2},{4,7},{5,4},{6,5},{7,6},{8,11},{9,8},{10,9... | collective-permute-start | bytes 7688 | tf_op jit(solution)/shard_map/ppermute | solution.py:467
  76.5 33.9 %all-to-all-start.1 = ((f32[64,24,128]{2,1,0:T(8,128)}), f32[64,24,128]{2,1,0:T(8,128)S(1)}, u32[]{:S(2)}, u32[]{:S(2)}) async-start(f32[64,24,128]{2,1,0:T(8,128)} %join.1), calls=%async_computation.1 | async-start | bytes 1572864 | tf_op jit(solution)/shard_map/all_to_all | solution.py:481
  110.5 5.8 %collective-permute-start.3 = (f32[5,128]{1,0:T(8,128)S(1)}, f32[5,128]{1,0:T(8,128)S(1)}, u32[]{:S(2)}, u32[]{:S(2)}) collective-permute-start(f32[5,128]{1,0:T(8,128)S(1)} %slice_reduce_fusion), channel_id=1, source_target_pairs={{1,0},{2,1},{3,2},{0,3},{5,4},{6,5},{7,6},{4,7},{9,8},{10,9},{11,1... | collective-permute-start | bytes 7688 | tf_op jit(solution)/shard_map/ppermute | solution.py:487
  113.4 2.9 %collective-permute-start.4 = (f32[5,128]{1,0:T(8,128)S(1)}, f32[5,128]{1,0:T(8,128)S(1)}, u32[]{:S(2)}, u32[]{:S(2)}) collective-permute-start(f32[5,128]{1,0:T(8,128)S(1)} %slice_reduce_fusion), channel_id=1, source_target_pairs={{2,0},{3,1},{0,2},{1,3},{6,4},{7,5},{4,6},{5,7},{10,8},{11,9},{8,1... | collective-permute-start | bytes 7688 | tf_op jit(solution)/shard_map/ppermute | solution.py:487
  113.9 2.4 %collective-permute-start.5 = (f32[5,128]{1,0:T(8,128)S(1)}, f32[5,128]{1,0:T(8,128)S(1)}, u32[]{:S(2)}, u32[]{:S(2)}) collective-permute-start(f32[5,128]{1,0:T(8,128)S(1)} %slice_reduce_fusion), channel_id=1, source_target_pairs={{3,0},{0,1},{1,2},{2,3},{7,4},{4,5},{5,6},{6,7},{11,8},{8,9},{9,10... | collective-permute-start | bytes 7688 | tf_op jit(solution)/shard_map/ppermute | solution.py:487

commit v4 on v3

--- a/solution.py
+++ b/solution.py
@@ -168,11 +168,27 @@
     )
 
 
-def pack_kernel(signal, cotangent, out):
-    for q in range(signal.shape[1] // COLS):
+def pack_kernel(signal, cotangent, out, values, turned, into, outof):
+    quarters = signal.shape[1] // COLS
+    reads, writes = [], []
+    for q in range(quarters):
         here = pl.ds(q * COLS, COLS)
-        for n, part in enumerate(zip_rows(signal[:, here], cotangent[:, here])):
-            out[:, n, 8 * q : 8 * q + 8, :] = part.reshape(-1, 8, COLS)
+        for n, source in enumerate((signal, cotangent)):
+            copy = pltpu.make_async_copy(source.at[:, here], values.at[q, n], into.at[q, n])
+            copy.start()
+            reads.append(copy)
+    for q in range(quarters):
+        for copy in reads[2 * q : 2 * q + 2]:
+            copy.wait()
+        for n, part in enumerate(zip_rows(values[q, 0], values[q, 1])):
+            turned[q, :, n] = part.reshape(-1, 8, COLS)
+        copy = pltpu.make_async_copy(
+            turned.at[q], out.at[:, :, pl.ds(8 * q, 8), :], outof.at[q]
+        )
+        copy.start()
+        writes.append(copy)
+    for copy in writes:
+        copy.wait()
 
 
 def filter_kernel(
@@ -395,6 +411,9 @@
     shape = jax.ShapeDtypeStruct
     rows = signal.shape[1] // COLS * NARROW
 
+    def keep(x):
+        return pltpu.with_memory_space_constraint(x, pltpu.HBM)
+
     def call(body, name, outs, specs, args, mib, flops=0, scratch=(), out_specs=None):
         return pl.pallas_call(
             body,
@@ -407,9 +426,16 @@
             name=name,
         )(*args)
 
+    quarters = signal.shape[1] // COLS
     (sent,) = call(
-        pack_kernel, "pack", (shape((groups // 2, 2, 2 * rows, COLS), f32),), [vmem] * 2,
-        (signal, cotangent), 8,
+        pack_kernel, "pack", (pltpu.HBM((groups // 2, 2, 2 * rows, COLS), f32),), [hbm] * 2,
+        (keep(signal), keep(cotangent)), 8, out_specs=(hbm,),
+        scratch=[
+            pltpu.VMEM((quarters, 2, signal.shape[0], COLS), f32),
+            pltpu.VMEM((quarters, groups // 2, 2, 8, COLS), f32),
+            pltpu.SemaphoreType.DMA((quarters, 2)),
+            pltpu.SemaphoreType.DMA((quarters,)),
+        ],
     )
     spread = lax.all_to_all(
         sent.reshape(groups, 2 * rows, COLS), "batch", split_axis=0, concat_axis=0, tiled=True
@@ -431,7 +457,7 @@
     tall = (ROWS * 8, COLS)
     *state, norms, spectra = call(
         filter_kernel, "make_filter",
-        tuple(shape(*k) for k in kept) + (shape((8, COLS), f32), shape(wide, f32)),
+        tuple(pltpu.HBM(*k) for k in kept) + (shape((8, COLS), f32), pltpu.HBM(wide, f32)),
         [vmem] * 9,
         (
             weights, eight.T, rates, t["rows"], t["spread"],
@@ -451,7 +477,7 @@
         (
             spread, tiled, norms, t["rows"], t["gather"],
             t["forward_left"], t["forward_right"], t["inverse_left"], t["inverse_right"],
-            t["twist_cos"], t["twist_sin"], *state,
+            t["twist_cos"], t["twist_sin"], *map(keep, state),
         ),
         40, flops=10_000_000_000,
         scratch=[pltpu.VMEM(*k) for k in kept] + [

time: 118 us -> 107 us (0.907)
  local copies, waits for them, and re-layouts: 16.2 us -> 1.16 us
  waiting for transfers between devices: 23.5 us -> 28 us
  starting transfers between devices: 34.7 us -> 30.6 us
  Pallas kernels: 41.3 us -> 44.9 us
    unnamed x52 -> x30, local copies, waits for them, and re-layouts: 15.3 us -> 0.25 us
    all_to_all x1, starting transfers between devices: 11.4 us -> 5.6 us  [local(): lax.all_to_all(back, 'batch', split_axis=0, concat_axis=0, tiled=True)]
    all_to_all x1, waiting for transfers between devices: 0.01 us -> 4.36 us  [local(): lax.all_to_all(sent.reshape(groups, 2 * rows, COLS), 'batch', split_axis=...]
    pallas_call x6, Pallas kernels: 41.3 us -> 44.9 us  [call(): pl.pallas_call(body, out_shape=outs, in_specs=specs, out_specs=out_specs...]
    ppermute x3, starting transfers between devices: 3.62 us -> 5.3 us  [local(): pieces.append(lax.ppermute(piece, 'chan', ring))]
  transfers between devices with their start and end apart: 8 -> 8, of which waited for: 2 -> 3; matrix products, arithmetic and copies ran while one was open for 1% -> 1% of each run, Pallas kernels for 21% -> 24%
where the time goes in v4:
time: 107 us; the launch traced here: 106 us
  Pallas kernels  44.9 us (42%)
  starting transfers between devices  30.6 us (29%)
  waiting for transfers between devices  28 us (26%)
  local copies, waits for them, and re-layouts  1.16 us (1%)
    pallas_call x6, Pallas kernels, call(): pl.pallas_call(body, out_shape=outs, in_specs=specs, out_specs=out_specs...  44.9 us
    all_to_all x1, waiting for transfers between devices, local(): lax.all_to_all(back, 'batch', split_axis=0, concat_axis=0, tiled=True)  22.7 us
    all_to_all x1, starting transfers between devices, local(): lax.all_to_all(sent.reshape(groups, 2 * rows, COLS), 'batch', split_axis=...  15.1 us
    all_to_all x1, starting transfers between devices, local(): lax.all_to_all(back, 'batch', split_axis=0, concat_axis=0, tiled=True)  5.6 us
    ppermute x3, starting transfers between devices, local(): pieces.append(lax.ppermute(piece, 'chan', ring))  5.3 us
    ppermute x3, starting transfers between devices, local(): gathered.append(lax.ppermute(mine, 'chan', ring))  4.56 us
    all_to_all x1, waiting for transfers between devices, local(): lax.all_to_all(sent.reshape(groups, 2 * rows, COLS), 'batch', split_axis=...  4.36 us
  transfers between devices with their start and end apart: 8, of which 3 were waited for; matrix products, arithmetic and copies ran while one was open for 1% of the time, Pallas kernels for 24%

profile of v4, /device:TPU:1, one launch (start us, length us, event | category | flops | bytes accessed | tf_op | source)
XLA Modules:
  0.0 106.4 jit_solution(4765269716303710178)
XLA Ops:
  0.6 0.0 copy-start
  0.6 0.0 copy-start.8
  0.7 0.0 copy-start.5
  0.7 0.0 copy-start.2
  0.7 0.0 copy-start.4
  0.7 0.0 copy-start.6
  0.7 0.0 copy-start.7
  0.7 0.0 copy-start.11
  0.7 0.0 copy-start.12
  0.7 0.0 copy-start.13
  0.8 2.4 %pack.1 = f32[32,2,32,128]{3,2,1,0:T(8,128)} custom-call(f32[256,512]{1,0:T(8,128)} %signal.1, f32[256,512]{1,0:T(8,128)} %cotangent.1), custom_call_target="tpu_custom_call" | custom-call | tf_op jit(solution)/shard_map/pack/pallas_call | solution.py:418
  3.2 15.1 %all-to-all-start = ((f32[64,32,128]{2,1,0:T(8,128)}), f32[64,32,128]{2,1,0:T(8,128)S(1)}, u32[]{:S(2)}, u32[]{:S(2)}) async-start(f32[64,32,128]{2,1,0:T(8,128)} %bitcast.14), calls=%async_computation | async-start | bytes 2097152 | tf_op jit(solution)/shard_map/all_to_all | solution.py:440
  18.3 0.0 copy-done.11
  18.3 0.1 copy.25
  18.4 0.0 copy-done.12
  18.4 0.1 dynamic_slice.24.gains
  18.5 0.0 copy-done
  18.5 0.1 constant_dynamic-slice_fusion.5
  18.6 0.1 copy.29
  18.7 0.0 copy-done.13
  18.7 0.1 dynamic_slice.26
  18.8 0.1 copy.28
  18.9 0.1 pad_maximum_fusion.weights
  19.0 0.1 broadcast_in_dim.2.rates
  19.1 0.0 copy-done.8
  19.1 0.0 copy-done.5
  19.1 0.0 copy-done.2
  19.1 0.0 copy-done.4
  19.1 0.0 copy-done.6
  19.1 0.0 copy-done.7
  19.1 0.0 copy-start.1
  19.1 0.0 copy-start.3
  19.1 0.0 copy-start.9
  19.1 22.2 %make_filter.1 = (bf16[64,32768]{1,0:T(8,128)(2,1)}, bf16[64,32768]{1,0:T(8,128)(2,1)}, f32[64,32768]{1,0:T(8,128)}, f32[4,256,128]{2,1,0:T(8,128)}, f32[4,256,1...) custom-call(f32[64,128]{1,0:T(8,128)S(1)} %pad_maximum_fusion.weights, ...), custom_call_target="tpu_custom_call" | custom-call | flops 20000000000 | tf_op jit(solution)/shard_map/make_filter/pallas_call | solution.py:418
  41.4 4.4 %all-to-all-done = f32[64,32,128]{2,1,0:T(8,128)S(1)} async-done(((f32[64,32,128]{2,1,0:T(8,128)}), f32[64,32,128]{2,1,0:T(8,128)S(1)}, u32[]{:S(2)}, u32[]{:S(2)}) %all-to-all-start) | async-done | bytes 1048608 | tf_op jit(solution)/shard_map/all_to_all | solution.py:440
  45.7 0.0 copy-done.1
  45.7 0.0 copy-done.3
  45.7 0.0 copy-done.9
  45.7 0.0 copy-start.10
  45.8 16.1 %correlate.1 = (f32[3,128]{1,0:T(4,128)S(1)}, f32[20,128]{1,0:T(8,128)S(1)}, f32[4,256,256]{2,1,0:T(8,128)S(1)}) custom-call(f32[2048,128]{1,0:T(8,128)S(1)} %bitcast.12, f32[64,128]{1,0:T(8,128)S(1)} %pad.19.columns, f32[8,128]{1,0:T(8,128)S(1)} %get-tuple-element.20.norms, f32[256,128]{1,0:T(8,128)S(1)} %copy-done.8, bf16[256,128]{1,0:T(8,128)(2,1)S(1)} %copy-done.9, ...), custom_call_target="tpu_custom_call" | custom-call | flops 10000000000 | tf_op jit(solution)/shard_map/correlate/pallas_call | solution.py:418
  61.9 4.2 %collective-permute-start = (f32[5,128]{1,0:T(8,128)S(1)}, f32[5,128]{1,0:T(8,128)S(1)}, u32[]{:S(2)}, u32[]{:S(2)}) collective-permute-start(f32[5,128]{1,0:T(8,128)S(1)} %get-tuple-element.37), channel_id=1, source_target_pairs={{0,1},{1,2},{2,3},{3,0},{4,5},{5,6},{6,7},{7,4},{8,9},{9,10},{10,1... | collective-permute-start | bytes 7688 | tf_op jit(solution)/shard_map/ppermute | solution.py:493
  66.1 1.1 %collective-permute-start.1 = (f32[5,128]{1,0:T(8,128)S(1)}, f32[5,128]{1,0:T(8,128)S(1)}, u32[]{:S(2)}, u32[]{:S(2)}) collective-permute-start(f32[5,128]{1,0:T(8,128)S(1)} %get-tuple-element.36), channel_id=1, source_target_pairs={{0,2},{1,3},{2,0},{3,1},{4,6},{5,7},{6,4},{7,5},{8,10},{9,11},{10,... | collective-permute-start | bytes 7688 | tf_op jit(solution)/shard_map/ppermute | solution.py:493
  67.2 0.0 collective-permute-start.2
  67.2 0.0 copy-done.10
  67.2 2.1 %input_grad.1.grad = f32[1024,128]{1,0:T(8,128)S(1)} custom-call(f32[2048,128]{1,0:T(8,128)S(1)} %bitcast.13, f32[4]{0:T(128)S(1)} %dynamic_slice.24.gains, f32[4,256,256]{2,1,0:T(8,128)S(1)} %copy-done.10, f32[4,256,256]{2,1,0:T(8,128)S(1)} %get-tuple-element.26.cotan, bf16[256,1024]{1,0:T(8,128)(2,1)S(1)} %copy-done.1, bf16[512,256]{1,0:T(8,128)(2,1)S(1)} %copy-done.3, ...), custom_call_target="tpu_custom_call" | custom-call | flops 4000000000 | tf_op jit(solution)/shard_map/input_grad/pallas_call | solution.py:418
  69.3 0.0 collective-permute-done.one
  69.3 0.0 collective-permute-done.1.two
  69.3 0.9 collective-permute-done.2.three
  70.2 0.9 join.1
  71.2 5.6 %all-to-all-start.1 = ((f32[64,24,128]{2,1,0:T(8,128)}), f32[64,24,128]{2,1,0:T(8,128)S(1)}, u32[]{:S(2)}, u32[]{:S(2)}) async-start(f32[64,24,128]{2,1,0:T(8,128)} %join.1), calls=%async_computation.1 | async-start | bytes 1572864 | tf_op jit(solution)/shard_map/all_to_all | solution.py:507
  76.8 22.7 %all-to-all-done.1 = f32[64,24,128]{2,1,0:T(8,128)S(1)} async-done(((f32[64,24,128]{2,1,0:T(8,128)}), f32[64,24,128]{2,1,0:T(8,128)S(1)}, u32[]{:S(2)}, u32[]{:S(2)}) %all-to-all-start.1) | async-done | bytes 786464 | tf_op jit(solution)/shard_map/all_to_all | solution.py:507
  99.5 0.1 slice_reduce_fusion
  99.6 2.8 %collective-permute-start.3 = (f32[5,128]{1,0:T(8,128)S(1)}, f32[5,128]{1,0:T(8,128)S(1)}, u32[]{:S(2)}, u32[]{:S(2)}) collective-permute-start(f32[5,128]{1,0:T(8,128)S(1)} %slice_reduce_fusion), channel_id=1, source_target_pairs={{1,0},{2,1},{3,2},{0,3},{5,4},{6,5},{7,6},{4,7},{9,8},{10,9},{11,1... | collective-permute-start | bytes 7688 | tf_op jit(solution)/shard_map/ppermute | solution.py:513
  102.4 0.3 collective-permute-start.4
  102.7 1.4 %collective-permute-start.5 = (f32[5,128]{1,0:T(8,128)S(1)}, f32[5,128]{1,0:T(8,128)S(1)}, u32[]{:S(2)}, u32[]{:S(2)}) collective-permute-start(f32[5,128]{1,0:T(8,128)S(1)} %slice_reduce_fusion), channel_id=1, source_target_pairs={{3,0},{0,1},{1,2},{2,3},{7,4},{4,5},{5,6},{6,7},{11,8},{8,9},{9,10... | collective-permute-start | bytes 7688 | tf_op jit(solution)/shard_map/ppermute | solution.py:513
  104.1 1.2 %unpack.1 = (f32[256,512]{1,0:T(8,128)}, f32[64,256]{1,0:T(8,128)}, f32[1,256]{1,0:T(1,128)}, f32[1,256]{1,0:T(1,128)}) custom-call(f32[32,2,24,128]{3,2,1,0:T(8,128)S(1)} %bitcast.10, f32[1536,128]{1,0:T(8,128)S(1)} %bitcast.11), custom_call_target="tpu_custom_call" | custom-call | flops 1000000000 | tf_op jit(solution)/shard_map/unpack/pallas_call | solution.py:418
  105.3 0.0 collective-permute-done.3
  105.3 0.0 collective-permute-done.4
  105.3 0.0 collective-permute-done.5
  105.3 0.4 concatenate.14
  105.7 0.1 constant_dynamic-slice_fusion
  105.8 0.6 pad_maximum_fusion.1
  (7 shorter events, 0.1 us)
Async XLA Ops:
  0.6 17.9 %copy-start = (f32[64,256]{1,0:T(8,128)S(1)}, f32[64,256]{1,0:T(8,128)}, u32[]{:S(2)}) copy-start(f32[64,256]{1,0:T(8,128)} %param.18) | copy-start | bytes 196612
  0.6 18.4 %copy-start.8 = (f32[256,128]{1,0:T(8,128)S(1)}, f32[256,128]{1,0:T(8,128)}, u32[]{:S(2)}) copy-start(f32[256,128]{1,0:T(8,128)} %constant.71.clone.rows) | copy-start | bytes 393220
  0.7 18.4 %copy-start.5 = (bf16[768,128]{1,0:T(8,128)(2,1)S(1)}, bf16[768,128]{1,0:T(8,128)(2,1)}, u32[]{:S(2)}) copy-start(bf16[768,128]{1,0:T(8,128)(2,1)} %constant.72.clone.spread) | copy-start | bytes 589828
  0.7 18.4 %copy-start.2 = (bf16[512,512]{1,0:T(8,128)(2,1)S(1)}, bf16[512,512]{1,0:T(8,128)(2,1)}, u32[]{:S(2)}) copy-start(bf16[512,512]{1,0:T(8,128)(2,1)} %constant.73.clone.left.fleft) | copy-start | bytes 1572868
  0.7 18.4 %copy-start.4 = (bf16[512,256]{1,0:T(8,128)(2,1)S(1)}, bf16[512,256]{1,0:T(8,128)(2,1)}, u32[]{:S(2)}) copy-start(bf16[512,256]{1,0:T(8,128)(2,1)} %constant.74.clone.right.fright) | copy-start | bytes 786436
  0.7 18.4 %copy-start.6 = (f32[256,128]{1,0:T(8,128)S(1)}, f32[256,128]{1,0:T(8,128)}, u32[]{:S(2)}) copy-start(f32[256,128]{1,0:T(8,128)} %constant.75.clone.tcos) | copy-start | bytes 393220
  0.7 18.4 %copy-start.7 = (f32[256,128]{1,0:T(8,128)S(1)}, f32[256,128]{1,0:T(8,128)}, u32[]{:S(2)}) copy-start(f32[256,128]{1,0:T(8,128)} %constant.76.clone.tsin) | copy-start | bytes 393220
  0.7 17.6 %copy-start.11 = (f32[33,64]{1,0:T(8,128)S(1)}, f32[33,64]{1,0:T(8,128)}, u32[]{:S(2)}) copy-start(f32[33,64]{1,0:T(8,128)} %param.17) | copy-start | bytes 25348
  0.7 17.7 %copy-start.12 = (f32[256]{0:T(256)S(1)}, f32[256]{0:T(256)}, u32[]{:S(2)}) copy-start(f32[256]{0:T(256)} %param.20) | copy-start | bytes 3076
  0.7 17.9 %copy-start.13 = (f32[256]{0:T(256)S(1)}, f32[256]{0:T(256)}, u32[]{:S(2)}) copy-start(f32[256]{0:T(256)} %param.19) | copy-start | bytes 3076
  3.2 42.6 %all-to-all-start = ((f32[64,32,128]{2,1,0:T(8,128)}), f32[64,32,128]{2,1,0:T(8,128)S(1)}, u32[]{:S(2)}, u32[]{:S(2)}) async-start(f32[64,32,128]{2,1,0:T(8,128)} %bitcast.14), calls=%async_computation | async-start | bytes 2097152 | tf_op jit(solution)/shard_map/all_to_all | solution.py:440
  19.1 26.6 %copy-start.1 = (bf16[256,1024]{1,0:T(8,128)(2,1)S(1)}, bf16[256,1024]{1,0:T(8,128)(2,1)}, u32[]{:S(2)}) copy-start(bf16[256,1024]{1,0:T(8,128)(2,1)} %constant.78.clone.ileft) | copy-start | bytes 1572868
  19.1 26.6 %copy-start.3 = (bf16[512,256]{1,0:T(8,128)(2,1)S(1)}, bf16[512,256]{1,0:T(8,128)(2,1)}, u32[]{:S(2)}) copy-start(bf16[512,256]{1,0:T(8,128)(2,1)} %constant.79.clone.iright) | copy-start | bytes 786436
  19.1 26.6 %copy-start.9 = (bf16[256,128]{1,0:T(8,128)(2,1)S(1)}, bf16[256,128]{1,0:T(8,128)(2,1)}, u32[]{:S(2)}) copy-start(bf16[256,128]{1,0:T(8,128)(2,1)} %constant.77.clone.gather) | copy-start | bytes 196612
  45.7 21.5 %copy-start.10 = (f32[4,256,256]{2,1,0:T(8,128)S(1)}, f32[4,256,256]{2,1,0:T(8,128)}, u32[]{:S(2)}) copy-start(f32[4,256,256]{2,1,0:T(8,128)} %get-tuple-element.19.spectra) | copy-start | bytes 3145732
  61.9 7.4 %collective-permute-start = (f32[5,128]{1,0:T(8,128)S(1)}, f32[5,128]{1,0:T(8,128)S(1)}, u32[]{:S(2)}, u32[]{:S(2)}) collective-permute-start(f32[5,128]{1,0:T(8,128)S(1)} %get-tuple-element.37), channel_id=1, source_target_pairs={{0,1},{1,2},{2,3},{3,0},{4,5},{5,6},{6,7},{7,4},{8,9},{9,10},{10,1... | collective-permute-start | bytes 7688 | tf_op jit(solution)/shard_map/ppermute | solution.py:493
  66.1 3.2 %collective-permute-start.1 = (f32[5,128]{1,0:T(8,128)S(1)}, f32[5,128]{1,0:T(8,128)S(1)}, u32[]{:S(2)}, u32[]{:S(2)}) collective-permute-start(f32[5,128]{1,0:T(8,128)S(1)} %get-tuple-element.36), channel_id=1, source_target_pairs={{0,2},{1,3},{2,0},{3,1},{4,6},{5,7},{6,4},{7,5},{8,10},{9,11},{10,... | collective-permute-start | bytes 7688 | tf_op jit(solution)/shard_map/ppermute | solution.py:493
  67.2 3.0 %collective-permute-start.2 = (f32[5,128]{1,0:T(8,128)S(1)}, f32[5,128]{1,0:T(8,128)S(1)}, u32[]{:S(2)}, u32[]{:S(2)}) collective-permute-start(f32[5,128]{1,0:T(8,128)S(1)} %get-tuple-element.35), channel_id=1, source_target_pairs={{0,3},{1,0},{2,1},{3,2},{4,7},{5,4},{6,5},{7,6},{8,11},{9,8},{10,9... | collective-permute-start | bytes 7688 | tf_op jit(solution)/shard_map/ppermute | solution.py:493
  71.2 28.3 %all-to-all-start.1 = ((f32[64,24,128]{2,1,0:T(8,128)}), f32[64,24,128]{2,1,0:T(8,128)S(1)}, u32[]{:S(2)}, u32[]{:S(2)}) async-start(f32[64,24,128]{2,1,0:T(8,128)} %join.1), calls=%async_computation.1 | async-start | bytes 1572864 | tf_op jit(solution)/shard_map/all_to_all | solution.py:507
  99.6 5.7 %collective-permute-start.3 = (f32[5,128]{1,0:T(8,128)S(1)}, f32[5,128]{1,0:T(8,128)S(1)}, u32[]{:S(2)}, u32[]{:S(2)}) collective-permute-start(f32[5,128]{1,0:T(8,128)S(1)} %slice_reduce_fusion), channel_id=1, source_target_pairs={{1,0},{2,1},{3,2},{0,3},{5,4},{6,5},{7,6},{4,7},{9,8},{10,9},{11,1... | collective-permute-start | bytes 7688 | tf_op jit(solution)/shard_map/ppermute | solution.py:513
  102.4 2.9 %collective-permute-start.4 = (f32[5,128]{1,0:T(8,128)S(1)}, f32[5,128]{1,0:T(8,128)S(1)}, u32[]{:S(2)}, u32[]{:S(2)}) collective-permute-start(f32[5,128]{1,0:T(8,128)S(1)} %slice_reduce_fusion), channel_id=1, source_target_pairs={{2,0},{3,1},{0,2},{1,3},{6,4},{7,5},{4,6},{5,7},{10,8},{11,9},{8,1... | collective-permute-start | bytes 7688 | tf_op jit(solution)/shard_map/ppermute | solution.py:513
  102.7 2.6 %collective-permute-start.5 = (f32[5,128]{1,0:T(8,128)S(1)}, f32[5,128]{1,0:T(8,128)S(1)}, u32[]{:S(2)}, u32[]{:S(2)}) collective-permute-start(f32[5,128]{1,0:T(8,128)S(1)} %slice_reduce_fusion), channel_id=1, source_target_pairs={{3,0},{0,1},{1,2},{2,3},{7,4},{4,5},{5,6},{6,7},{11,8},{8,9},{9,10... | collective-permute-start | bytes 7688 | tf_op jit(solution)/shard_map/ppermute | solution.py:513

commit v5 on v4

--- a/solution.py
+++ b/solution.py
@@ -68,7 +68,7 @@
         lanes[bands + b] = np.cos(small)
         lanes[half + bands + b] = np.sin(small)
     high, low = halves(lanes.T)
-    gather = np.concatenate([high, low], axis=0)
+    gather = np.tile(np.concatenate([high, low], axis=1), (2, 1))
     high, low = halves(lanes)
     lowest = (lanes - high.astype(np.float64) - low.astype(np.float64)).astype(bf16)
     spread = np.concatenate([high, low, lowest, high, low, high], axis=0)
@@ -263,22 +263,34 @@
 
 
 def main_kernel(
-    both, columns, norms, rows, gather, fleft, fright, ileft, iright, tcos, tsin,
-    high_in, low_in, slope_in, filt_in, window_in,
-    small, first, cotan,
-    high, low, slope, filt, window, dmix, product, sems,
+    both, columns, gains, norms, rows, gather, fleft, fright, ileft, iright, tcos, tsin,
+    high_in, low_in, slope_in, filt_in, window_in, spectra_in,
+    small, first, grad,
+    high, low, slope, filt, window, spectra, dmix, product, early, late,
 ):
     order = slope.shape[0]
     factor = 1.0 / math.sqrt(LENGTH)
-    copies = [
-        pltpu.make_async_copy(source, target, sems.at[n])
-        for n, (source, target) in enumerate((
-            (filt_in, filt), (window_in, window),
-            (high_in, high), (low_in, low), (slope_in, slope),
-        ))
+    batch = TAIL_BATCH
+    wide = batch * COLS
+    starts = [
+        pltpu.make_async_copy(source, target, early.at[n])
+        for n, (source, target) in enumerate(
+            ((filt_in, filt), (window_in, window), (spectra_in, spectra))
+        )
     ]
-    for one in copies:
-        one.start()
+
+    def fetch(n):
+        here = pl.ds(pl.multiple_of(n * wide, wide), wide)
+        return [
+            pltpu.make_async_copy(source.at[:, here], target.at[:, here], late.at[m, n])
+            for m, (source, target) in enumerate(((high_in, high), (low_in, low), (slope_in, slope)))
+        ]
+
+    for copy in starts:
+        copy.start()
+    for n in range(ROWS // batch):
+        for copy in fetch(n):
+            copy.start()
     lane = lax.broadcasted_iota(jnp.int32, (1, COLS), 1)
     scalars = jnp.zeros((1, COLS), f32)
     fraction = fraction_rows(ROWS, 0)
@@ -289,35 +301,32 @@
         skip = factor * jnp.sum(x * y, keepdims=True)
         scalars = jnp.where(lane == NARROW + c, skip, scalars)
         val, cot = forward_pair(x, y, fleft[...], fright[...], tcos[...], tsin[...])
-        cotan[c] = cot
+        if c == 0:
+            for copy in starts:
+                copy.wait()
         product[c] = times_conj(val, cot)
-    copies[0].wait()
-    copies[1].wait()
-    for c in range(0, NARROW, 2):
-        pair = inverse_pair(
-            product[c], product[c + 1], ileft[...], iright[...], tcos[...], tsin[...]
-        )
-        for n in range(2):
-            i = c + n
-            dfilt = pair[n] * (factor / LENGTH)
-            project = jnp.sum(filt[i] * dfilt, keepdims=True)
-            norm = norms[pl.ds(i, 1), :][:, :1]
-            draw = (dfilt - filt[i] * project) / norm
-            decay = -jnp.sum(draw * filt[i] * fraction, keepdims=True) * norm
-            dmix[pl.ds(i, ROWS, stride=8), :] = draw * window[i]
-            scalars = jnp.where(lane == i, decay, scalars)
+        product[NARROW + c] = times_conj(spectra[c], cot)
+    for c in range(NARROW):
+        back, into = inverse_pair(
+            product[c], product[NARROW + c], ileft[...], iright[...], tcos[...], tsin[...]
+        )
+        y = both[pl.ds(NARROW + c, ROWS, stride=2 * NARROW), :]
+        grad[pl.ds(c, ROWS, stride=NARROW), :] = into * (1.0 / LENGTH) + gains[c] * y
+        dfilt = back * (factor / LENGTH)
+        project = jnp.sum(filt[c] * dfilt, keepdims=True)
+        norm = norms[pl.ds(c, 1), :][:, :1]
+        draw = (dfilt - filt[c] * project) / norm
+        decay = -jnp.sum(draw * filt[c] * fraction, keepdims=True) * norm
+        dmix[pl.ds(c, ROWS, stride=8), :] = draw * window[c]
+        scalars = jnp.where(lane == c, decay, scalars)
     lanes = lax.broadcasted_iota(jnp.int32, columns.shape, 1)
     col_high = columns[...].astype(bf16).astype(f32)
     mixer = jnp.where(lanes // 8 == 2, columns[...] - col_high, col_high).astype(bf16)[:, :32]
-    copies[2].wait()
-    copies[3].wait()
-    copies[4].wait()
-    batch = TAIL_BATCH
-    wide = batch * COLS
-    contract = (((1,), (1,)), ((), ()))
 
     def tail(n, carry):
         firsts, seconds = carry
+        for copy in fetch(n):
+            copy.wait()
         stack = []
         for i in range(batch):
             d = dmix[pl.ds(pl.multiple_of((n * batch + i) * 8, 8), 8), :]
@@ -327,20 +336,23 @@
             )
         stack = jnp.concatenate(stack, axis=1)
         here = pl.ds(pl.multiple_of(n * wide, wide), wide)
-        for part in (high, low):
-            seconds = seconds + lax.dot_general(
-                stack[:16], part[:, here], contract, preferred_element_type=f32
-            )
+        both_halves = jnp.concatenate([high[:, here], low[:, here]], axis=0)
+        seconds = seconds + lax.dot_general(
+            both_halves, stack[:16], (((1,), (1,)), ((), ())), preferred_element_type=f32
+        )
         q = mm(mixer, stack) * slope[:, here]
         q = jnp.concatenate([q[:, i * COLS : (i + 1) * COLS] for i in range(batch)], axis=0)
-        r = dot_cols(q, gather[...])
+        r = mm(jnp.concatenate(split(q), axis=1), gather[...])
+        r = r[:, :COLS] + r[:, COLS:]
         for i in range(batch):
             firsts = firsts + r[i * order : (i + 1) * order] * rows[pl.ds(n * batch + i, 1), :]
         return firsts, seconds
 
     firsts, seconds = lax.fori_loop(
-        0, ROWS // batch, tail, (jnp.zeros((order, COLS), f32), jnp.zeros((16, order), f32))
-    )
+        0, ROWS // batch, tail,
+        (jnp.zeros((order, COLS), f32), jnp.zeros((2 * order, 16), f32)),
+    )
+    seconds = jnp.transpose(seconds[:order] + seconds[order:], (1, 0))
     seconds = seconds[:8] + seconds[8:]
     small[:1] = jnp.concatenate([seconds[0:1], seconds[1:2]], axis=1)
     small[1:2] = jnp.concatenate([seconds[2:3], seconds[3:4]], axis=1)
@@ -349,18 +361,6 @@
     half = COLS // 2
     folded = turned[:half] + turned[half:]
     first[...] = jnp.concatenate([folded[:20], folded[20:40]], axis=1)
-
-
-def input_kernel(both, gains, spectra, cotan, ileft, iright, tcos, tsin, grad):
-    for c in range(0, NARROW, 2):
-        pair = inverse_pair(
-            times_conj(spectra[c], cotan[c]), times_conj(spectra[c + 1], cotan[c + 1]),
-            ileft[...], iright[...], tcos[...], tsin[...],
-        )
-        for n in range(2):
-            i = c + n
-            y = both[pl.ds(NARROW + i, ROWS, stride=2 * NARROW), :]
-            grad[pl.ds(i, ROWS, stride=NARROW), :] = pair[n] * (1.0 / LENGTH) + gains[i] * y
 
 
 def join_kernel(grad, small, own, one, two, three, out, tile):
@@ -470,18 +470,20 @@
         ],
         out_specs=(hbm,) * 5 + (vmem, hbm),
     )
-    small, first, cotan = call(
+    small, first, grad = call(
         main_kernel, "correlate",
-        (shape((3, COLS), f32), shape((20, COLS), f32), shape(wide, f32)),
-        [vmem] * 11 + [hbm] * 5,
+        (shape((3, COLS), f32), shape((20, COLS), f32), shape((groups * rows, COLS), f32)),
+        [vmem] * 2 + [smem] + [vmem] * 9 + [hbm] * 6,
         (
-            spread, tiled, norms, t["rows"], t["gather"],
+            spread, tiled, gains, norms, t["rows"], t["gather"],
             t["forward_left"], t["forward_right"], t["inverse_left"], t["inverse_right"],
-            t["twist_cos"], t["twist_sin"], *map(keep, state),
+            t["twist_cos"], t["twist_sin"], *map(keep, state), keep(spectra),
         ),
         40, flops=10_000_000_000,
         scratch=[pltpu.VMEM(*k) for k in kept] + [
-            pltpu.VMEM(tall, f32), pltpu.VMEM(wide, f32), pltpu.SemaphoreType.DMA((5,)),
+            pltpu.VMEM(wide, f32), pltpu.VMEM(tall, f32),
+            pltpu.VMEM((2 * NARROW, ROWS, 2 * COLS), f32),
+            pltpu.SemaphoreType.DMA((3,)), pltpu.SemaphoreType.DMA((3, ROWS // TAIL_BATCH)),
         ],
     )
 
@@ -491,15 +493,6 @@
         ring = [(i, (i + step) % sides) for i in range(sides)]
         piece = lax.dynamic_slice_in_dim(first, (side + step) % sides * quarter, quarter, 0)
         pieces.append(lax.ppermute(piece, "chan", ring))
-    (grad,) = call(
-        input_kernel, "input_grad", (shape((groups * rows, COLS), f32),),
-        [vmem, smem] + [vmem] * 6,
-        (
-            spread, gains, spectra, cotan, t["inverse_left"], t["inverse_right"],
-            t["twist_cos"], t["twist_sin"],
-        ),
-        16, flops=4_000_000_000,
-    )
     (back,) = call(
         join_kernel, "join", (shape((groups, rows + 8, COLS), f32),), [vmem] * 6,
         (grad, small, *pieces), 8, scratch=[pltpu.VMEM((8, COLS), f32)],

time: 107 us -> 110 us (1.028)
  waiting for transfers between devices: 28 us -> 31.8 us
  starting transfers between devices: 30.6 us -> 28.9 us
    ppermute x3, waiting for transfers between devices: 0.94 us -> 3.03 us  [local(): pieces.append(lax.ppermute(piece, 'chan', ring))]
    all_to_all x1, waiting for transfers between devices: 22.7 us -> 24.4 us  [local(): lax.all_to_all(back, 'batch', split_axis=0, concat_axis=0, tiled=True)]
    ppermute x3, starting transfers between devices: 4.56 us -> 2.86 us  [local(): gathered.append(lax.ppermute(mine, 'chan', ring))]
    pallas_call x6 -> x5, Pallas kernels: 44.9 us -> 45.8 us  [call(): pl.pallas_call(body, out_shape=outs, in_specs=specs, out_specs=out_specs...]
  transfers between devices with their start and end apart: 8 -> 8, of which waited for: 3 -> 4; matrix products, arithmetic and copies ran while one was open for 1% -> 1% of each run, Pallas kernels for 24% -> 21%
where the time goes in v5:
time: 110 us; the launch traced here: 109 us
  Pallas kernels  45.8 us (42%)
  waiting for transfers between devices  31.8 us (29%)
  starting transfers between devices  28.9 us (26%)
  local copies, waits for them, and re-layouts  1.16 us (1%)
    pallas_call x5, Pallas kernels, call(): pl.pallas_call(body, out_shape=outs, in_specs=specs, out_specs=out_specs...  45.8 us
    all_to_all x1, waiting for transfers between devices, local(): lax.all_to_all(back, 'batch', split_axis=0, concat_axis=0, tiled=True)  24.4 us
    all_to_all x1, starting transfers between devices, local(): lax.all_to_all(sent.reshape(groups, 2 * rows, COLS), 'batch', split_axis=...  15.1 us
    all_to_all x1, starting transfers between devices, local(): lax.all_to_all(back, 'batch', split_axis=0, concat_axis=0, tiled=True)  5.6 us
    ppermute x3, starting transfers between devices, local(): pieces.append(lax.ppermute(piece, 'chan', ring))  5.3 us
    all_to_all x1, waiting for transfers between devices, local(): lax.all_to_all(sent.reshape(groups, 2 * rows, COLS), 'batch', split_axis=...  4.35 us
    ppermute x3, waiting for transfers between devices, local(): pieces.append(lax.ppermute(piece, 'chan', ring))  3.03 us
    ppermute x3, starting transfers between devices, local(): gathered.append(lax.ppermute(mine, 'chan', ring))  2.86 us
  transfers between devices with their start and end apart: 8, of which 4 were waited for; matrix products, arithmetic and copies ran while one was open for 1% of the time, Pallas kernels for 21%

profile of v5, /device:TPU:1, one launch (start us, length us, event | category | flops | bytes accessed | tf_op | source)
XLA Modules:
  0.0 109.4 jit_solution(3537801064564066993)
XLA Ops:
  0.6 0.0 copy-start
  0.6 0.0 copy-start.6
  0.7 0.0 copy-start.5
  0.7 0.0 copy-start.1
  0.7 0.0 copy-start.3
  0.7 0.0 copy-start.7
  0.7 0.0 copy-start.8
  0.7 0.0 copy-start.10
  0.7 0.0 copy-start.11
  0.7 0.0 copy-start.12
  0.8 2.4 %pack.1 = f32[32,2,32,128]{3,2,1,0:T(8,128)} custom-call(f32[256,512]{1,0:T(8,128)} %signal.1, f32[256,512]{1,0:T(8,128)} %cotangent.1), custom_call_target="tpu_custom_call" | custom-call | tf_op jit(solution)/shard_map/pack/pallas_call | solution.py:418
  3.1 15.1 %all-to-all-start = ((f32[64,32,128]{2,1,0:T(8,128)}), f32[64,32,128]{2,1,0:T(8,128)S(1)}, u32[]{:S(2)}, u32[]{:S(2)}) async-start(f32[64,32,128]{2,1,0:T(8,128)} %bitcast.13), calls=%async_computation | async-start | bytes 2097152 | tf_op jit(solution)/shard_map/all_to_all | solution.py:440
  18.3 0.0 copy-done
  18.3 0.1 constant_dynamic-slice_fusion.5
  18.4 0.1 copy.29
  18.5 0.0 copy-done.10
  18.5 0.1 copy.27
  18.6 0.1 copy.26
  18.7 0.0 copy-done.11
  18.7 0.1 dynamic_slice.25.gains
  18.8 0.0 copy-done.12
  18.8 0.1 dynamic_slice.26
  18.9 0.1 pad_maximum_fusion.weights
  19.0 0.1 broadcast_in_dim.2.rates
  19.0 0.0 copy-done.6
  19.0 0.0 copy-done.5
  19.0 0.0 copy-done.1
  19.0 0.0 copy-done.3
  19.0 0.0 copy-done.7
  19.1 0.0 copy-done.8
  19.1 0.0 copy-start.2
  19.1 0.0 copy-start.4
  19.1 0.0 copy-start.9
  19.1 22.3 %make_filter.1 = (bf16[64,32768]{1,0:T(8,128)(2,1)}, bf16[64,32768]{1,0:T(8,128)(2,1)}, f32[64,32768]{1,0:T(8,128)}, f32[4,256,128]{2,1,0:T(8,128)}, f32[4,256,1...) custom-call(f32[64,128]{1,0:T(8,128)S(1)} %pad_maximum_fusion.weights, ...), custom_call_target="tpu_custom_call" | custom-call | flops 20000000000 | tf_op jit(solution)/shard_map/make_filter/pallas_call | solution.py:418
  41.4 4.3 %all-to-all-done = f32[64,32,128]{2,1,0:T(8,128)S(1)} async-done(((f32[64,32,128]{2,1,0:T(8,128)}), f32[64,32,128]{2,1,0:T(8,128)S(1)}, u32[]{:S(2)}, u32[]{:S(2)}) %all-to-all-start) | async-done | bytes 1048608 | tf_op jit(solution)/shard_map/all_to_all | solution.py:440
  45.7 0.0 copy-done.2
  45.7 0.0 copy-done.4
  45.7 0.0 copy-done.9
  45.7 19.1 %correlate.1 = (f32[3,128]{1,0:T(4,128)S(1)}, f32[20,128]{1,0:T(8,128)S(1)}, f32[1024,128]{1,0:T(8,128)S(1)}) custom-call(f32[2048,128]{1,0:T(8,128)S(1)} %bitcast.12, f32[64,128]{1,0:T(8,128)S(1)} %pad.17.columns, f32[4]{0:T(128)S(1)} %dynamic_slice.25.gains, f32[8,128]{1,0:T(8,128)S(1)} %get-tuple-element.19.norms, f32[256,128]{1,0:T(8,128)S(1)} %copy-done.6, ...), custom_call_target="tpu_custom_call" | custom-call | flops 10000000000 | tf_op jit(solution)/shard_map/correlate/pallas_call | solution.py:418
  64.8 4.2 %collective-permute-start = (f32[5,128]{1,0:T(8,128)S(1)}, f32[5,128]{1,0:T(8,128)S(1)}, u32[]{:S(2)}, u32[]{:S(2)}) collective-permute-start(f32[5,128]{1,0:T(8,128)S(1)} %get-tuple-element.37), channel_id=1, source_target_pairs={{0,1},{1,2},{2,3},{3,0},{4,5},{5,6},{6,7},{7,4},{8,9},{9,10},{10,1... | collective-permute-start | bytes 7688 | tf_op jit(solution)/shard_map/ppermute | solution.py:495
  69.1 1.1 collective-permute-start.1
  70.1 0.0 collective-permute-start.2
  70.1 0.0 collective-permute-done.one
  70.1 1.4 %collective-permute-done.1.two = f32[5,128]{1,0:T(8,128)S(1)} collective-permute-done((f32[5,128]{1,0:T(8,128)S(1)}, f32[5,128]{1,0:T(8,128)S(1)}, u32[]{:S(2)}, u32[]{:S(2)}) %collective-permute-start.1) | collective-permute-done | bytes 2592 | tf_op jit(solution)/shard_map/ppermute | solution.py:495
  71.5 1.6 %collective-permute-done.2.three = f32[5,128]{1,0:T(8,128)S(1)} collective-permute-done((f32[5,128]{1,0:T(8,128)S(1)}, f32[5,128]{1,0:T(8,128)S(1)}, u32[]{:S(2)}, u32[]{:S(2)}) %collective-permute-start.2) | collective-permute-done | bytes 2592 | tf_op jit(solution)/shard_map/ppermute | solution.py:495
  73.2 0.9 join.1
  74.1 5.6 %all-to-all-start.1 = ((f32[64,24,128]{2,1,0:T(8,128)}), f32[64,24,128]{2,1,0:T(8,128)S(1)}, u32[]{:S(2)}, u32[]{:S(2)}) async-start(f32[64,24,128]{2,1,0:T(8,128)} %join.1), calls=%async_computation.1 | async-start | bytes 1572864 | tf_op jit(solution)/shard_map/all_to_all | solution.py:500
  79.7 24.4 %all-to-all-done.1 = f32[64,24,128]{2,1,0:T(8,128)S(1)} async-done(((f32[64,24,128]{2,1,0:T(8,128)}), f32[64,24,128]{2,1,0:T(8,128)S(1)}, u32[]{:S(2)}, u32[]{:S(2)}) %all-to-all-start.1) | async-done | bytes 786464 | tf_op jit(solution)/shard_map/all_to_all | solution.py:500
  104.1 0.1 slice_reduce_fusion
  104.2 1.1 %collective-permute-start.3 = (f32[5,128]{1,0:T(8,128)S(1)}, f32[5,128]{1,0:T(8,128)S(1)}, u32[]{:S(2)}, u32[]{:S(2)}) collective-permute-start(f32[5,128]{1,0:T(8,128)S(1)} %slice_reduce_fusion), channel_id=1, source_target_pairs={{1,0},{2,1},{3,2},{0,3},{5,4},{6,5},{7,6},{4,7},{9,8},{10,9},{11,1... | collective-permute-start | bytes 7688 | tf_op jit(solution)/shard_map/ppermute | solution.py:506
  105.3 0.4 collective-permute-start.4
  105.7 1.4 %collective-permute-start.5 = (f32[5,128]{1,0:T(8,128)S(1)}, f32[5,128]{1,0:T(8,128)S(1)}, u32[]{:S(2)}, u32[]{:S(2)}) collective-permute-start(f32[5,128]{1,0:T(8,128)S(1)} %slice_reduce_fusion), channel_id=1, source_target_pairs={{3,0},{0,1},{1,2},{2,3},{7,4},{4,5},{5,6},{6,7},{11,8},{8,9},{9,10... | collective-permute-start | bytes 7688 | tf_op jit(solution)/shard_map/ppermute | solution.py:506
  107.1 1.2 %unpack.1 = (f32[256,512]{1,0:T(8,128)}, f32[64,256]{1,0:T(8,128)}, f32[1,256]{1,0:T(1,128)}, f32[1,256]{1,0:T(1,128)}) custom-call(f32[32,2,24,128]{3,2,1,0:T(8,128)S(1)} %bitcast.10, f32[1536,128]{1,0:T(8,128)S(1)} %bitcast.11), custom_call_target="tpu_custom_call" | custom-call | flops 1000000000 | tf_op jit(solution)/shard_map/unpack/pallas_call | solution.py:418
  108.2 0.0 collective-permute-done.3
  108.2 0.0 collective-permute-done.4
  108.3 0.0 collective-permute-done.5
  108.3 0.4 concatenate.14
  108.7 0.1 constant_dynamic-slice_fusion
  108.7 0.6 pad_maximum_fusion.1
  (7 shorter events, 0.1 us)
Async XLA Ops:
  0.6 17.7 %copy-start = (f32[64,256]{1,0:T(8,128)S(1)}, f32[64,256]{1,0:T(8,128)}, u32[]{:S(2)}) copy-start(f32[64,256]{1,0:T(8,128)} %param.18) | copy-start | bytes 196612
  0.6 18.4 %copy-start.6 = (f32[256,128]{1,0:T(8,128)S(1)}, f32[256,128]{1,0:T(8,128)}, u32[]{:S(2)}) copy-start(f32[256,128]{1,0:T(8,128)} %constant.71.clone.rows) | copy-start | bytes 393220
  0.7 18.4 %copy-start.5 = (bf16[768,128]{1,0:T(8,128)(2,1)S(1)}, bf16[768,128]{1,0:T(8,128)(2,1)}, u32[]{:S(2)}) copy-start(bf16[768,128]{1,0:T(8,128)(2,1)} %constant.72.clone.spread) | copy-start | bytes 589828
  0.7 18.4 %copy-start.1 = (bf16[512,512]{1,0:T(8,128)(2,1)S(1)}, bf16[512,512]{1,0:T(8,128)(2,1)}, u32[]{:S(2)}) copy-start(bf16[512,512]{1,0:T(8,128)(2,1)} %constant.73.clone.left.fleft) | copy-start | bytes 1572868
  0.7 18.4 %copy-start.3 = (bf16[512,256]{1,0:T(8,128)(2,1)S(1)}, bf16[512,256]{1,0:T(8,128)(2,1)}, u32[]{:S(2)}) copy-start(bf16[512,256]{1,0:T(8,128)(2,1)} %constant.74.clone.right.fright) | copy-start | bytes 786436
  0.7 18.4 %copy-start.7 = (f32[256,128]{1,0:T(8,128)S(1)}, f32[256,128]{1,0:T(8,128)}, u32[]{:S(2)}) copy-start(f32[256,128]{1,0:T(8,128)} %constant.75.clone.tcos) | copy-start | bytes 393220
  0.7 18.3 %copy-start.8 = (f32[256,128]{1,0:T(8,128)S(1)}, f32[256,128]{1,0:T(8,128)}, u32[]{:S(2)}) copy-start(f32[256,128]{1,0:T(8,128)} %constant.76.clone.tsin) | copy-start | bytes 393220
  0.7 17.8 %copy-start.10 = (f32[33,64]{1,0:T(8,128)S(1)}, f32[33,64]{1,0:T(8,128)}, u32[]{:S(2)}) copy-start(f32[33,64]{1,0:T(8,128)} %param.17) | copy-start | bytes 25348
  0.7 18.0 %copy-start.11 = (f32[256]{0:T(256)S(1)}, f32[256]{0:T(256)}, u32[]{:S(2)}) copy-start(f32[256]{0:T(256)} %param.20) | copy-start | bytes 3076
  0.7 18.0 %copy-start.12 = (f32[256]{0:T(256)S(1)}, f32[256]{0:T(256)}, u32[]{:S(2)}) copy-start(f32[256]{0:T(256)} %param.19) | copy-start | bytes 3076
  3.1 42.6 %all-to-all-start = ((f32[64,32,128]{2,1,0:T(8,128)}), f32[64,32,128]{2,1,0:T(8,128)S(1)}, u32[]{:S(2)}, u32[]{:S(2)}) async-start(f32[64,32,128]{2,1,0:T(8,128)} %bitcast.13), calls=%async_computation | async-start | bytes 2097152 | tf_op jit(solution)/shard_map/all_to_all | solution.py:440
  19.1 26.7 %copy-start.2 = (bf16[256,1024]{1,0:T(8,128)(2,1)S(1)}, bf16[256,1024]{1,0:T(8,128)(2,1)}, u32[]{:S(2)}) copy-start(bf16[256,1024]{1,0:T(8,128)(2,1)} %constant.78.clone.ileft) | copy-start | bytes 1572868
  19.1 26.6 %copy-start.4 = (bf16[512,256]{1,0:T(8,128)(2,1)S(1)}, bf16[512,256]{1,0:T(8,128)(2,1)}, u32[]{:S(2)}) copy-start(bf16[512,256]{1,0:T(8,128)(2,1)} %constant.79.clone.iright) | copy-start | bytes 786436
  19.1 26.6 %copy-start.9 = (bf16[256,256]{1,0:T(8,128)(2,1)S(1)}, bf16[256,256]{1,0:T(8,128)(2,1)}, u32[]{:S(2)}) copy-start(bf16[256,256]{1,0:T(8,128)(2,1)} %constant.77.clone.gather) | copy-start | bytes 393220
  64.8 5.3 %collective-permute-start = (f32[5,128]{1,0:T(8,128)S(1)}, f32[5,128]{1,0:T(8,128)S(1)}, u32[]{:S(2)}, u32[]{:S(2)}) collective-permute-start(f32[5,128]{1,0:T(8,128)S(1)} %get-tuple-element.37), channel_id=1, source_target_pairs={{0,1},{1,2},{2,3},{3,0},{4,5},{5,6},{6,7},{7,4},{8,9},{9,10},{10,1... | collective-permute-start | bytes 7688 | tf_op jit(solution)/shard_map/ppermute | solution.py:495
  69.1 2.5 %collective-permute-start.1 = (f32[5,128]{1,0:T(8,128)S(1)}, f32[5,128]{1,0:T(8,128)S(1)}, u32[]{:S(2)}, u32[]{:S(2)}) collective-permute-start(f32[5,128]{1,0:T(8,128)S(1)} %get-tuple-element.36), channel_id=1, source_target_pairs={{0,2},{1,3},{2,0},{3,1},{4,6},{5,7},{6,4},{7,5},{8,10},{9,11},{10,... | collective-permute-start | bytes 7688 | tf_op jit(solution)/shard_map/ppermute | solution.py:495
  70.1 3.0 %collective-permute-start.2 = (f32[5,128]{1,0:T(8,128)S(1)}, f32[5,128]{1,0:T(8,128)S(1)}, u32[]{:S(2)}, u32[]{:S(2)}) collective-permute-start(f32[5,128]{1,0:T(8,128)S(1)} %get-tuple-element.35), channel_id=1, source_target_pairs={{0,3},{1,0},{2,1},{3,2},{4,7},{5,4},{6,5},{7,6},{8,11},{9,8},{10,9... | collective-permute-start | bytes 7688 | tf_op jit(solution)/shard_map/ppermute | solution.py:495
  74.1 30.0 %all-to-all-start.1 = ((f32[64,24,128]{2,1,0:T(8,128)}), f32[64,24,128]{2,1,0:T(8,128)S(1)}, u32[]{:S(2)}, u32[]{:S(2)}) async-start(f32[64,24,128]{2,1,0:T(8,128)} %join.1), calls=%async_computation.1 | async-start | bytes 1572864 | tf_op jit(solution)/shard_map/all_to_all | solution.py:500
  104.2 4.0 %collective-permute-start.3 = (f32[5,128]{1,0:T(8,128)S(1)}, f32[5,128]{1,0:T(8,128)S(1)}, u32[]{:S(2)}, u32[]{:S(2)}) collective-permute-start(f32[5,128]{1,0:T(8,128)S(1)} %slice_reduce_fusion), channel_id=1, source_target_pairs={{1,0},{2,1},{3,2},{0,3},{5,4},{6,5},{7,6},{4,7},{9,8},{10,9},{11,1... | collective-permute-start | bytes 7688 | tf_op jit(solution)/shard_map/ppermute | solution.py:506
  105.3 2.9 %collective-permute-start.4 = (f32[5,128]{1,0:T(8,128)S(1)}, f32[5,128]{1,0:T(8,128)S(1)}, u32[]{:S(2)}, u32[]{:S(2)}) collective-permute-start(f32[5,128]{1,0:T(8,128)S(1)} %slice_reduce_fusion), channel_id=1, source_target_pairs={{2,0},{3,1},{0,2},{1,3},{6,4},{7,5},{4,6},{5,7},{10,8},{11,9},{8,1... | collective-permute-start | bytes 7688 | tf_op jit(solution)/shard_map/ppermute | solution.py:506
  105.7 2.6 %collective-permute-start.5 = (f32[5,128]{1,0:T(8,128)S(1)}, f32[5,128]{1,0:T(8,128)S(1)}, u32[]{:S(2)}, u32[]{:S(2)}) collective-permute-start(f32[5,128]{1,0:T(8,128)S(1)} %slice_reduce_fusion), channel_id=1, source_target_pairs={{3,0},{0,1},{1,2},{2,3},{7,4},{4,5},{5,6},{6,7},{11,8},{8,9},{9,10... | collective-permute-start | bytes 7688 | tf_op jit(solution)/shard_map/ppermute | solution.py:506

commit v6 on v4

--- a/solution.py
+++ b/solution.py
@@ -68,7 +68,7 @@
         lanes[bands + b] = np.cos(small)
         lanes[half + bands + b] = np.sin(small)
     high, low = halves(lanes.T)
-    gather = np.concatenate([high, low], axis=0)
+    gather = np.tile(np.concatenate([high, low], axis=1), (2, 1))
     high, low = halves(lanes)
     lowest = (lanes - high.astype(np.float64) - low.astype(np.float64)).astype(bf16)
     spread = np.concatenate([high, low, lowest, high, low, high], axis=0)
@@ -266,19 +266,26 @@
     both, columns, norms, rows, gather, fleft, fright, ileft, iright, tcos, tsin,
     high_in, low_in, slope_in, filt_in, window_in,
     small, first, cotan,
-    high, low, slope, filt, window, dmix, product, sems,
+    high, low, slope, filt, window, dmix, product, early, late,
 ):
     order = slope.shape[0]
     factor = 1.0 / math.sqrt(LENGTH)
-    copies = [
-        pltpu.make_async_copy(source, target, sems.at[n])
-        for n, (source, target) in enumerate((
-            (filt_in, filt), (window_in, window),
-            (high_in, high), (low_in, low), (slope_in, slope),
-        ))
+    batch = TAIL_BATCH
+    wide = batch * COLS
+    starts = [
+        pltpu.make_async_copy(source, target, early.at[n])
+        for n, (source, target) in enumerate(((filt_in, filt), (window_in, window)))
     ]
-    for one in copies:
-        one.start()
+
+    def fetch(n):
+        here = pl.ds(pl.multiple_of(n * wide, wide), wide)
+        return [
+            pltpu.make_async_copy(source.at[:, here], target.at[:, here], late.at[m, n])
+            for m, (source, target) in enumerate(((high_in, high), (low_in, low), (slope_in, slope)))
+        ]
+
+    for copy in starts:
+        copy.start()
     lane = lax.broadcasted_iota(jnp.int32, (1, COLS), 1)
     scalars = jnp.zeros((1, COLS), f32)
     fraction = fraction_rows(ROWS, 0)
@@ -289,10 +296,14 @@
         skip = factor * jnp.sum(x * y, keepdims=True)
         scalars = jnp.where(lane == NARROW + c, skip, scalars)
         val, cot = forward_pair(x, y, fleft[...], fright[...], tcos[...], tsin[...])
+        if c == 0:
+            for copy in starts:
+                copy.wait()
+            for n in range(ROWS // batch):
+                for copy in fetch(n):
+                    copy.start()
         cotan[c] = cot
         product[c] = times_conj(val, cot)
-    copies[0].wait()
-    copies[1].wait()
     for c in range(0, NARROW, 2):
         pair = inverse_pair(
             product[c], product[c + 1], ileft[...], iright[...], tcos[...], tsin[...]
@@ -309,15 +320,11 @@
     lanes = lax.broadcasted_iota(jnp.int32, columns.shape, 1)
     col_high = columns[...].astype(bf16).astype(f32)
     mixer = jnp.where(lanes // 8 == 2, columns[...] - col_high, col_high).astype(bf16)[:, :32]
-    copies[2].wait()
-    copies[3].wait()
-    copies[4].wait()
-    batch = TAIL_BATCH
-    wide = batch * COLS
-    contract = (((1,), (1,)), ((), ()))
 
     def tail(n, carry):
         firsts, seconds = carry
+        for copy in fetch(n):
+            copy.wait()
         stack = []
         for i in range(batch):
             d = dmix[pl.ds(pl.multiple_of((n * batch + i) * 8, 8), 8), :]
@@ -327,20 +334,23 @@
             )
         stack = jnp.concatenate(stack, axis=1)
         here = pl.ds(pl.multiple_of(n * wide, wide), wide)
-        for part in (high, low):
-            seconds = seconds + lax.dot_general(
-                stack[:16], part[:, here], contract, preferred_element_type=f32
-            )
+        both_halves = jnp.concatenate([high[:, here], low[:, here]], axis=0)
+        seconds = seconds + lax.dot_general(
+            both_halves, stack[:16], (((1,), (1,)), ((), ())), preferred_element_type=f32
+        )
         q = mm(mixer, stack) * slope[:, here]
         q = jnp.concatenate([q[:, i * COLS : (i + 1) * COLS] for i in range(batch)], axis=0)
-        r = dot_cols(q, gather[...])
+        r = mm(jnp.concatenate(split(q), axis=1), gather[...])
+        r = r[:, :COLS] + r[:, COLS:]
         for i in range(batch):
             firsts = firsts + r[i * order : (i + 1) * order] * rows[pl.ds(n * batch + i, 1), :]
         return firsts, seconds
 
     firsts, seconds = lax.fori_loop(
-        0, ROWS // batch, tail, (jnp.zeros((order, COLS), f32), jnp.zeros((16, order), f32))
-    )
+        0, ROWS // batch, tail,
+        (jnp.zeros((order, COLS), f32), jnp.zeros((2 * order, 16), f32)),
+    )
+    seconds = jnp.transpose(seconds[:order] + seconds[order:], (1, 0))
     seconds = seconds[:8] + seconds[8:]
     small[:1] = jnp.concatenate([seconds[0:1], seconds[1:2]], axis=1)
     small[1:2] = jnp.concatenate([seconds[2:3], seconds[3:4]], axis=1)
@@ -398,6 +408,20 @@
     skip[...] = jnp.sum(scalars[NARROW:], axis=0, keepdims=True)
 
 
+def finish_kernel(side, own, one, two, three, out, table):
+    pieces = (own[...], one[...], two[...], three[...])
+    count = own.shape[0]
+    order = out.shape[1]
+    for n in range(len(pieces)):
+        chosen = jnp.zeros(own.shape, f32)
+        for i, piece in enumerate(pieces):
+            chosen = jnp.where((side[0] + i) % len(pieces) == n, piece, chosen)
+        table[n * count : (n + 1) * count] = chosen
+    total = table.shape[0]
+    out[:total] = table[:, :order]
+    out[total:] = table[: out.shape[0] - total, order:]
+
+
 def local(signal, cotangent, first_layer, second_layer, decay_rate, skip_gain):
     groups = lax.axis_size("batch")
     place = lax.axis_index("batch")
@@ -481,7 +505,8 @@
         ),
         40, flops=10_000_000_000,
         scratch=[pltpu.VMEM(*k) for k in kept] + [
-            pltpu.VMEM(tall, f32), pltpu.VMEM(wide, f32), pltpu.SemaphoreType.DMA((5,)),
+            pltpu.VMEM(tall, f32), pltpu.VMEM(wide, f32),
+            pltpu.SemaphoreType.DMA((2,)), pltpu.SemaphoreType.DMA((3, ROWS // TAIL_BATCH)),
         ],
     )
 
@@ -520,11 +545,11 @@
         [vmem] * 2, (home.reshape(groups // 2, 2, -1, COLS), home.reshape(-1, COLS)), 8,
         flops=1_000_000_000,
     )
-    twice = jnp.concatenate(gathered + gathered, axis=0)
-    ordered = lax.dynamic_slice_in_dim(
-        twice, (sides - side) % sides * quarter, sides * quarter, 0
-    )
-    first_grad = jnp.concatenate([ordered[:, :order], ordered[:, order:]], axis=0)[:embed]
+    (first_grad,) = call(
+        finish_kernel, "finish", (shape((embed, order), f32),), [smem] + [vmem] * 4,
+        (side.reshape(1), *gathered), 4,
+        scratch=[pltpu.VMEM((sides * quarter, 2 * order), f32)],
+    )
     return (input_grad, first_grad, second_grad, decay_grad[0], skip_grad[0])
 
 

time: 107 us -> 103 us (0.963)
  blocking collectives: 0 us -> 28.1 us
  waiting for transfers between devices: 28 us -> 5.27 us
  starting transfers between devices: 30.6 us -> 24.9 us
  Pallas kernels: 44.9 us -> 42.1 us
    all_to_all x0 -> x1, blocking collectives: none -> 28.1 us  [local(): lax.all_to_all(back, 'batch', split_axis=0, concat_axis=0, tiled=True)]
    all_to_all x1 -> x0, waiting for transfers between devices: 22.7 us -> none  [local(): lax.all_to_all(back, 'batch', split_axis=0, concat_axis=0, tiled=True)]
    all_to_all x1 -> x0, starting transfers between devices: 5.6 us -> none  [local(): lax.all_to_all(back, 'batch', split_axis=0, concat_axis=0, tiled=True)]
    pallas_call x6 -> x7, Pallas kernels: 44.9 us -> 42.1 us  [call(): pl.pallas_call(body, out_shape=outs, in_specs=specs, out_specs=out_specs...]
  transfers between devices with their start and end apart: 8 -> 7, of which waited for: 3 -> 2; matrix products, arithmetic and copies ran while one was open for 1% -> 1% of each run, Pallas kernels for 24% -> 25%
where the time goes in v6:
time: 103 us; the launch traced here: 102 us
  Pallas kernels  42.1 us (41%)
  blocking collectives  28.1 us (27%)
  starting transfers between devices  24.9 us (24%)
  waiting for transfers between devices  5.27 us (5%)
    pallas_call x7, Pallas kernels, call(): pl.pallas_call(body, out_shape=outs, in_specs=specs, out_specs=out_specs...  42.1 us
    all_to_all x1, blocking collectives, local(): lax.all_to_all(back, 'batch', split_axis=0, concat_axis=0, tiled=True)  28.1 us
    all_to_all x1, starting transfers between devices, local(): lax.all_to_all(sent.reshape(groups, 2 * rows, COLS), 'batch', split_axis=...  15.1 us
    ppermute x3, starting transfers between devices, local(): pieces.append(lax.ppermute(piece, 'chan', ring))  5.29 us
    ppermute x3, starting transfers between devices, local(): gathered.append(lax.ppermute(mine, 'chan', ring))  4.54 us
    all_to_all x1, waiting for transfers between devices, local(): lax.all_to_all(sent.reshape(groups, 2 * rows, COLS), 'batch', split_axis=...  4.33 us
  transfers between devices with their start and end apart: 7, of which 2 were waited for; matrix products, arithmetic and copies ran while one was open for 1% of the time, Pallas kernels for 25%

profile of v6, /device:TPU:1, one launch (start us, length us, event | category | flops | bytes accessed | tf_op | source)
XLA Modules:
  0.0 102.3 jit_solution(7151376702997138828)
XLA Ops:
  0.6 0.0 copy-start
  0.6 0.0 copy-start.8
  0.7 0.0 copy-start.5
  0.7 0.0 copy-start.2
  0.7 0.0 copy-start.4
  0.7 0.0 copy-start.6
  0.7 0.0 copy-start.7
  0.7 0.0 copy-start.11
  0.7 0.0 copy-start.12
  0.7 0.0 copy-start.13
  0.8 2.4 %pack.1 = f32[32,2,32,128]{3,2,1,0:T(8,128)} custom-call(f32[256,512]{1,0:T(8,128)} %signal.1, f32[256,512]{1,0:T(8,128)} %cotangent.1), custom_call_target="tpu_custom_call" | custom-call | tf_op jit(solution)/shard_map/pack/pallas_call | solution.py:442
  3.1 15.1 %all-to-all-start = ((f32[64,32,128]{2,1,0:T(8,128)}), f32[64,32,128]{2,1,0:T(8,128)S(1)}, u32[]{:S(2)}, u32[]{:S(2)}) async-start(f32[64,32,128]{2,1,0:T(8,128)} %bitcast.15), calls=%async_computation | async-start | bytes 2097152 | tf_op jit(solution)/shard_map/all_to_all | solution.py:464
  18.3 0.0 copy-done.11
  18.3 0.1 copy.25
  18.4 0.0 copy-done.12
  18.4 0.1 dynamic_slice.21.gains
  18.5 0.0 copy-done
  18.5 0.1 constant_dynamic-slice_fusion.4
  18.6 0.1 copy.29
  18.7 0.0 copy-done.13
  18.7 0.1 dynamic_slice.23
  18.8 0.1 copy.28
  18.9 0.1 pad_maximum_fusion.weights
  19.0 0.1 broadcast_in_dim.2.rates
  19.0 0.0 copy-done.8
  19.0 0.0 copy-done.5
  19.0 0.0 copy-done.2
  19.0 0.0 copy-done.4
  19.1 0.0 copy-done.6
  19.1 0.0 copy-done.7
  19.1 0.0 copy-start.1
  19.1 0.0 copy-start.3
  19.1 0.0 copy-start.9
  19.1 22.3 %make_filter.1 = (bf16[64,32768]{1,0:T(8,128)(2,1)}, bf16[64,32768]{1,0:T(8,128)(2,1)}, f32[64,32768]{1,0:T(8,128)}, f32[4,256,128]{2,1,0:T(8,128)}, f32[4,256,1...) custom-call(f32[64,128]{1,0:T(8,128)S(1)} %pad_maximum_fusion.weights, ...), custom_call_target="tpu_custom_call" | custom-call | flops 20000000000 | tf_op jit(solution)/shard_map/make_filter/pallas_call | solution.py:442
  41.4 4.3 %all-to-all-done = f32[64,32,128]{2,1,0:T(8,128)S(1)} async-done(((f32[64,32,128]{2,1,0:T(8,128)}), f32[64,32,128]{2,1,0:T(8,128)S(1)}, u32[]{:S(2)}, u32[]{:S(2)}) %all-to-all-start) | async-done | bytes 1048608 | tf_op jit(solution)/shard_map/all_to_all | solution.py:464
  45.7 0.0 copy-done.1
  45.7 0.0 copy-done.3
  45.7 0.0 copy-done.9
  45.7 0.0 copy-start.10
  45.7 13.5 %correlate.1 = (f32[3,128]{1,0:T(4,128)S(1)}, f32[20,128]{1,0:T(8,128)S(1)}, f32[4,256,256]{2,1,0:T(8,128)S(1)}) custom-call(f32[2048,128]{1,0:T(8,128)S(1)} %bitcast.13, f32[64,128]{1,0:T(8,128)S(1)} %pad.19.columns, f32[8,128]{1,0:T(8,128)S(1)} %get-tuple-element.20.norms, f32[256,128]{1,0:T(8,128)S(1)} %copy-done.8, bf16[256,256]{1,0:T(8,128)(2,1)S(1)} %copy-done.9, ...), custom_call_target="tpu_custom_call" | custom-call | flops 10000000000 | tf_op jit(solution)/shard_map/correlate/pallas_call | solution.py:442
  59.3 4.2 %collective-permute-start = (f32[5,128]{1,0:T(8,128)S(1)}, f32[5,128]{1,0:T(8,128)S(1)}, u32[]{:S(2)}, u32[]{:S(2)}) collective-permute-start(f32[5,128]{1,0:T(8,128)S(1)} %get-tuple-element.35), channel_id=1, source_target_pairs={{0,1},{1,2},{2,3},{3,0},{4,5},{5,6},{6,7},{7,4},{8,9},{9,10},{10,1... | collective-permute-start | bytes 7688 | tf_op jit(solution)/shard_map/ppermute | solution.py:518
  63.5 1.1 %collective-permute-start.1 = (f32[5,128]{1,0:T(8,128)S(1)}, f32[5,128]{1,0:T(8,128)S(1)}, u32[]{:S(2)}, u32[]{:S(2)}) collective-permute-start(f32[5,128]{1,0:T(8,128)S(1)} %get-tuple-element.34), channel_id=1, source_target_pairs={{0,2},{1,3},{2,0},{3,1},{4,6},{5,7},{6,4},{7,5},{8,10},{9,11},{10,... | collective-permute-start | bytes 7688 | tf_op jit(solution)/shard_map/ppermute | solution.py:518
  64.6 0.0 collective-permute-start.2
  64.6 0.0 copy-done.10
  64.6 2.1 %input_grad.1.grad = f32[1024,128]{1,0:T(8,128)S(1)} custom-call(f32[2048,128]{1,0:T(8,128)S(1)} %bitcast.14, f32[4]{0:T(128)S(1)} %dynamic_slice.21.gains, f32[4,256,256]{2,1,0:T(8,128)S(1)} %copy-done.10, f32[4,256,256]{2,1,0:T(8,128)S(1)} %get-tuple-element.26.cotan, bf16[256,1024]{1,0:T(8,128)(2,1)S(1)} %copy-done.1, bf16[512,256]{1,0:T(8,128)(2,1)S(1)} %copy-done.3, ...), custom_call_target="tpu_custom_call" | custom-call | flops 4000000000 | tf_op jit(solution)/shard_map/input_grad/pallas_call | solution.py:442
  66.6 0.0 collective-permute-done.one
  66.7 0.0 collective-permute-done.1.two
  66.7 0.9 collective-permute-done.2.three
  67.6 0.1 join.1
  67.7 28.1 %all_to_all.10 = f32[64,24,128]{2,1,0:T(8,128)S(1)} all-to-all(f32[64,24,128]{2,1,0:T(8,128)S(1)} %join.1), channel_id=1, replica_groups=mesh['batch'=64,'chan'=4] {'batch'}, dimensions={0} | all-to-all | bytes 1572864 | tf_op jit(solution)/shard_map/all_to_all | solution.py:532
  95.8 0.1 slice_reduce_fusion.own
  95.9 2.8 %collective-permute-start.3 = (f32[5,128]{1,0:T(8,128)S(1)}, f32[5,128]{1,0:T(8,128)S(1)}, u32[]{:S(2)}, u32[]{:S(2)}) collective-permute-start(f32[5,128]{1,0:T(8,128)S(1)} %slice_reduce_fusion.own), channel_id=1, source_target_pairs={{1,0},{2,1},{3,2},{0,3},{5,4},{6,5},{7,6},{4,7},{9,8},{10,9},{11,1... | collective-permute-start | bytes 7688 | tf_op jit(solution)/shard_map/ppermute | solution.py:538
  98.7 0.3 collective-permute-start.4
  99.0 1.4 %collective-permute-start.5 = (f32[5,128]{1,0:T(8,128)S(1)}, f32[5,128]{1,0:T(8,128)S(1)}, u32[]{:S(2)}, u32[]{:S(2)}) collective-permute-start(f32[5,128]{1,0:T(8,128)S(1)} %slice_reduce_fusion.own), channel_id=1, source_target_pairs={{3,0},{0,1},{1,2},{2,3},{7,4},{4,5},{5,6},{6,7},{11,8},{8,9},{9,10... | collective-permute-start | bytes 7688 | tf_op jit(solution)/shard_map/ppermute | solution.py:538
  100.4 1.2 %unpack.1 = (f32[256,512]{1,0:T(8,128)}, f32[64,256]{1,0:T(8,128)}, f32[1,256]{1,0:T(1,128)}, f32[1,256]{1,0:T(1,128)}) custom-call(f32[32,2,24,128]{3,2,1,0:T(8,128)S(1)} %bitcast.11, f32[1536,128]{1,0:T(8,128)S(1)} %bitcast.12), custom_call_target="tpu_custom_call" | custom-call | flops 1000000000 | tf_op jit(solution)/shard_map/unpack/pallas_call | solution.py:442
  101.6 0.0 collective-permute-done.3.one
  101.6 0.0 collective-permute-done.4.two
  101.6 0.0 collective-permute-done.5.three
  101.6 0.7 finish.1
  (7 shorter events, 0.1 us)
Async XLA Ops:
  0.6 17.9 %copy-start = (f32[64,256]{1,0:T(8,128)S(1)}, f32[64,256]{1,0:T(8,128)}, u32[]{:S(2)}) copy-start(f32[64,256]{1,0:T(8,128)} %param.18) | copy-start | bytes 196612
  0.6 18.4 %copy-start.8 = (f32[256,128]{1,0:T(8,128)S(1)}, f32[256,128]{1,0:T(8,128)}, u32[]{:S(2)}) copy-start(f32[256,128]{1,0:T(8,128)} %constant.65.clone.rows) | copy-start | bytes 393220
  0.7 18.4 %copy-start.5 = (bf16[768,128]{1,0:T(8,128)(2,1)S(1)}, bf16[768,128]{1,0:T(8,128)(2,1)}, u32[]{:S(2)}) copy-start(bf16[768,128]{1,0:T(8,128)(2,1)} %constant.66.clone.spread) | copy-start | bytes 589828
  0.7 18.4 %copy-start.2 = (bf16[512,512]{1,0:T(8,128)(2,1)S(1)}, bf16[512,512]{1,0:T(8,128)(2,1)}, u32[]{:S(2)}) copy-start(bf16[512,512]{1,0:T(8,128)(2,1)} %constant.67.clone.left.fleft) | copy-start | bytes 1572868
  0.7 18.4 %copy-start.4 = (bf16[512,256]{1,0:T(8,128)(2,1)S(1)}, bf16[512,256]{1,0:T(8,128)(2,1)}, u32[]{:S(2)}) copy-start(bf16[512,256]{1,0:T(8,128)(2,1)} %constant.68.clone.right.fright) | copy-start | bytes 786436
  0.7 18.4 %copy-start.6 = (f32[256,128]{1,0:T(8,128)S(1)}, f32[256,128]{1,0:T(8,128)}, u32[]{:S(2)}) copy-start(f32[256,128]{1,0:T(8,128)} %constant.69.clone.tcos) | copy-start | bytes 393220
  0.7 18.4 %copy-start.7 = (f32[256,128]{1,0:T(8,128)S(1)}, f32[256,128]{1,0:T(8,128)}, u32[]{:S(2)}) copy-start(f32[256,128]{1,0:T(8,128)} %constant.70.clone.tsin) | copy-start | bytes 393220
  0.7 17.6 %copy-start.11 = (f32[33,64]{1,0:T(8,128)S(1)}, f32[33,64]{1,0:T(8,128)}, u32[]{:S(2)}) copy-start(f32[33,64]{1,0:T(8,128)} %param.17) | copy-start | bytes 25348
  0.7 17.7 %copy-start.12 = (f32[256]{0:T(256)S(1)}, f32[256]{0:T(256)}, u32[]{:S(2)}) copy-start(f32[256]{0:T(256)} %param.20) | copy-start | bytes 3076
  0.7 17.9 %copy-start.13 = (f32[256]{0:T(256)S(1)}, f32[256]{0:T(256)}, u32[]{:S(2)}) copy-start(f32[256]{0:T(256)} %param.19) | copy-start | bytes 3076
  3.1 42.6 %all-to-all-start = ((f32[64,32,128]{2,1,0:T(8,128)}), f32[64,32,128]{2,1,0:T(8,128)S(1)}, u32[]{:S(2)}, u32[]{:S(2)}) async-start(f32[64,32,128]{2,1,0:T(8,128)} %bitcast.15), calls=%async_computation | async-start | bytes 2097152 | tf_op jit(solution)/shard_map/all_to_all | solution.py:464
  19.1 26.6 %copy-start.1 = (bf16[256,1024]{1,0:T(8,128)(2,1)S(1)}, bf16[256,1024]{1,0:T(8,128)(2,1)}, u32[]{:S(2)}) copy-start(bf16[256,1024]{1,0:T(8,128)(2,1)} %constant.72.clone.ileft) | copy-start | bytes 1572868
  19.1 26.6 %copy-start.3 = (bf16[512,256]{1,0:T(8,128)(2,1)S(1)}, bf16[512,256]{1,0:T(8,128)(2,1)}, u32[]{:S(2)}) copy-start(bf16[512,256]{1,0:T(8,128)(2,1)} %constant.73.clone.iright) | copy-start | bytes 786436
  19.1 26.6 %copy-start.9 = (bf16[256,256]{1,0:T(8,128)(2,1)S(1)}, bf16[256,256]{1,0:T(8,128)(2,1)}, u32[]{:S(2)}) copy-start(bf16[256,256]{1,0:T(8,128)(2,1)} %constant.71.clone.gather) | copy-start | bytes 393220
  45.7 18.8 %copy-start.10 = (f32[4,256,256]{2,1,0:T(8,128)S(1)}, f32[4,256,256]{2,1,0:T(8,128)}, u32[]{:S(2)}) copy-start(f32[4,256,256]{2,1,0:T(8,128)} %get-tuple-element.19.spectra) | copy-start | bytes 3145732
  59.3 7.4 %collective-permute-start = (f32[5,128]{1,0:T(8,128)S(1)}, f32[5,128]{1,0:T(8,128)S(1)}, u32[]{:S(2)}, u32[]{:S(2)}) collective-permute-start(f32[5,128]{1,0:T(8,128)S(1)} %get-tuple-element.35), channel_id=1, source_target_pairs={{0,1},{1,2},{2,3},{3,0},{4,5},{5,6},{6,7},{7,4},{8,9},{9,10},{10,1... | collective-permute-start | bytes 7688 | tf_op jit(solution)/shard_map/ppermute | solution.py:518
  63.5 3.1 %collective-permute-start.1 = (f32[5,128]{1,0:T(8,128)S(1)}, f32[5,128]{1,0:T(8,128)S(1)}, u32[]{:S(2)}, u32[]{:S(2)}) collective-permute-start(f32[5,128]{1,0:T(8,128)S(1)} %get-tuple-element.34), channel_id=1, source_target_pairs={{0,2},{1,3},{2,0},{3,1},{4,6},{5,7},{6,4},{7,5},{8,10},{9,11},{10,... | collective-permute-start | bytes 7688 | tf_op jit(solution)/shard_map/ppermute | solution.py:518
  64.6 3.0 %collective-permute-start.2 = (f32[5,128]{1,0:T(8,128)S(1)}, f32[5,128]{1,0:T(8,128)S(1)}, u32[]{:S(2)}, u32[]{:S(2)}) collective-permute-start(f32[5,128]{1,0:T(8,128)S(1)} %get-tuple-element.33), channel_id=1, source_target_pairs={{0,3},{1,0},{2,1},{3,2},{4,7},{5,4},{6,5},{7,6},{8,11},{9,8},{10,9... | collective-permute-start | bytes 7688 | tf_op jit(solution)/shard_map/ppermute | solution.py:518
  95.9 5.7 %collective-permute-start.3 = (f32[5,128]{1,0:T(8,128)S(1)}, f32[5,128]{1,0:T(8,128)S(1)}, u32[]{:S(2)}, u32[]{:S(2)}) collective-permute-start(f32[5,128]{1,0:T(8,128)S(1)} %slice_reduce_fusion.own), channel_id=1, source_target_pairs={{1,0},{2,1},{3,2},{0,3},{5,4},{6,5},{7,6},{4,7},{9,8},{10,9},{11,1... | collective-permute-start | bytes 7688 | tf_op jit(solution)/shard_map/ppermute | solution.py:538
  98.7 2.9 %collective-permute-start.4 = (f32[5,128]{1,0:T(8,128)S(1)}, f32[5,128]{1,0:T(8,128)S(1)}, u32[]{:S(2)}, u32[]{:S(2)}) collective-permute-start(f32[5,128]{1,0:T(8,128)S(1)} %slice_reduce_fusion.own), channel_id=1, source_target_pairs={{2,0},{3,1},{0,2},{1,3},{6,4},{7,5},{4,6},{5,7},{10,8},{11,9},{8,1... | collective-permute-start | bytes 7688 | tf_op jit(solution)/shard_map/ppermute | solution.py:538
  99.0 2.6 %collective-permute-start.5 = (f32[5,128]{1,0:T(8,128)S(1)}, f32[5,128]{1,0:T(8,128)S(1)}, u32[]{:S(2)}, u32[]{:S(2)}) collective-permute-start(f32[5,128]{1,0:T(8,128)S(1)} %slice_reduce_fusion.own), channel_id=1, source_target_pairs={{3,0},{0,1},{1,2},{2,3},{7,4},{4,5},{5,6},{6,7},{11,8},{8,9},{9,10... | collective-permute-start | bytes 7688 | tf_op jit(solution)/shard_map/ppermute | solution.py:538
